TPU v7x, 32 devices: a whole 2x2x4 slice. The times are simulated.
32 devices in a mesh: fsdp: 8 (over y, x, core), tp: 4 (over z).
Axes of the slice: x: 2, y: 2, z: 4, core: 2. Of those that a mesh axis runs over, the one named last changes fastest.
Arguments:
- inputs: float32 [8192, 768], P(('fsdp', 'tp')), may hold values from -6 to 6
- out_cotangent: float32 [8192, 768], P('fsdp'), may hold values from -6 to 6
- clip_lengths: int32 [6], replicated, may hold values from 384 to 1536, as said below
- norm1_gain: float32 [768], replicated, may hold values from 0.5 to 1.5
- norm1_shift: float32 [768], replicated, may hold values from -3 to 3
- query_weight: bfloat16 [768, 768], P('fsdp', 'tp'), may hold values from -0.21875 to 0.21875
- query_bias: float32 [768], replicated, may hold values from -3 to 3
- key_weight: bfloat16 [768, 768], P('fsdp', 'tp'), may hold values from -0.21875 to 0.21875
- value_weight: bfloat16 [768, 768], P('fsdp', 'tp'), may hold values from -0.21875 to 0.21875
- value_bias: float32 [768], replicated, may hold values from -3 to 3
- out_weight: bfloat16 [768, 768], P('fsdp', 'tp'), may hold values from -0.75 to 0.75
- out_bias: float32 [768], replicated, may hold values from -3 to 3
- norm2_gain: float32 [768], replicated, may hold values from 0.5 to 1.5
- norm2_shift: float32 [768], replicated, may hold values from -3 to 3
- fc1_weight: bfloat16 [3072, 768], P(('fsdp', 'tp')), may hold values from -0.21875 to 0.21875
- fc1_bias: float32 [3072], replicated, may hold values from -3 to 3
- fc2_weight: bfloat16 [3072, 768], P(('fsdp', 'tp')), may hold values from -0.3125 to 0.3125
- fc2_bias: float32 [768], replicated, may hold values from -3 to 3
Outputs:
- outputs: float32 [8192, 768], P(('fsdp', 'tp'))
- inputs_grad: float32 [8192, 768], P(('fsdp', 'tp'))
- norm1_gain_grad: float32 [768], replicated
- norm1_shift_grad: float32 [768], replicated
- query_weight_grad: float32 [768, 768], P('fsdp', 'tp')
- query_bias_grad: float32 [768], replicated
- key_weight_grad: float32 [768, 768], P('fsdp', 'tp')
- value_weight_grad: float32 [768, 768], P('fsdp', 'tp')
- value_bias_grad: float32 [768], replicated
- out_weight_grad: float32 [768, 768], P('fsdp', 'tp')
- out_bias_grad: float32 [768], replicated
- norm2_gain_grad: float32 [768], replicated
- norm2_shift_grad: float32 [768], replicated
- fc1_weight_grad: float32 [3072, 768], P(('fsdp', 'tp'))
- fc1_bias_grad: float32 [3072], replicated
- fc2_weight_grad: float32 [3072, 768], P(('fsdp', 'tp'))
- fc2_bias_grad: float32 [768], replicated
Inputs may be any that keep to these rules, and one draw needn't show every extreme that they name: `clip_lengths`: clip c has at most min(1536, 8192 - c * 1536) valid frames; some clip has all 1536 frames valid.
All inputs are finite; a program needn't handle non-finite values.
Results may differ from a plain program's by a relative error of at most 0.03.
Values may be sent and summed in bfloat16 or wider, within the bound.
A program may use at most 128 MiB of HBM per device.

v0:
```python
import math

import jax
import jax.numpy as jnp
from jax import lax
from jax.sharding import PartitionSpec as P

HD = 64
CLIP = 1536
QB = 512


eps_norm = 1e-05
root_half = 0.7071067811865476
inv_root_tau = 0.3989422804014327
far_negative = -1e30


def extended(value, sides, width):
    for axis, dim in sides:
        size, length = (lax.axis_size(axis), value.shape[dim])
        up = [(i, (i + 1) % size) for i in range(size - 1)]
        down = [(j, i) for i, j in up]
        last = lax.slice_in_dim(value, length - width, length, axis=dim)
        initial = lax.slice_in_dim(value, 0, width, axis=dim)
        before = lax.ppermute(last, axis, up)
        after = lax.ppermute(initial, axis, down)
        value = jnp.concatenate([before, value, after], axis=dim)
    return value


def normalize(rows, gain, shift):
    centre = jnp.mean(rows, axis=-1, keepdims=True)
    centred = rows - centre
    inv_spread = lax.rsqrt(jnp.mean(centred * centred, axis=-1, keepdims=True) + eps_norm)
    unit_rows = centred * inv_spread
    return (unit_rows, inv_spread, unit_rows * gain + shift)


def norm_back(upstream, unit_rows, inv_spread, gain):
    scaled = upstream * gain
    return inv_spread * (
        scaled
        - jnp.mean(scaled, axis=-1, keepdims=True)
        - unit_rows * jnp.mean(scaled * unit_rows, axis=-1, keepdims=True)
    )


def gelu_exact(values):
    return 0.5 * values * (1.0 + lax.erf(values * root_half))


def gelu_slope(values):
    return (
        0.5 * (1.0 + lax.erf(values * root_half))
        + values * jnp.exp(-0.5 * values * values) * inv_root_tau
    )


def contract_rows(left_rows, right_rows):
    return lax.dot_general(
        left_rows, right_rows, (((0,), (0,)), ((), ())), preferred_element_type=jnp.float32
    )


def contract_cols(left_rows, right_rows):
    return lax.dot_general(
        left_rows, right_rows, (((1,), (1,)), ((), ())), preferred_element_type=jnp.float32
    )


def fetch_attention(query_weight, key_weight, value_weight, out_weight):
    return (
        lax.all_gather(query_weight, "fsdp", axis=0, tiled=True),
        lax.all_gather(key_weight, "fsdp", axis=0, tiled=True),
        lax.all_gather(value_weight, "fsdp", axis=0, tiled=True),
        lax.all_gather(out_weight, "fsdp", axis=0, tiled=True),
    )


def on_device(
    inputs,
    out_cotangent,
    clip_lengths,
    norm1_gain,
    norm1_shift,
    query_weight,
    query_bias,
    key_weight,
    value_weight,
    value_bias,
    out_weight,
    out_bias,
    norm2_gain,
    norm2_shift,
    fc1_weight,
    fc1_bias,
    fc2_weight,
    fc2_bias,
):
    bf16 = jnp.bfloat16
    f32 = jnp.float32
    tp_count = lax.axis_size("tp")
    fsdp_count = lax.axis_size("fsdp")
    tp_index = lax.axis_index("tp")
    fsdp_index = lax.axis_index("fsdp")
    own_rows = inputs.shape[0]
    group_rows = out_cotangent.shape[0]
    score_scale = 1.0 / math.sqrt(HD)
    margin = CLIP - QB
    tp_slot = (jnp.arange(tp_count) == tp_index).astype(f32)
    own_cotangent = lax.dynamic_slice_in_dim(out_cotangent, tp_index * own_rows, own_rows, 0)
    unit1, spread1, normed_own = normalize(inputs, norm1_gain, norm1_shift)
    normed = lax.all_gather(normed_own.astype(bf16), "tp", axis=0, tiled=True)
    query_w, key_w, value_w, out_w = fetch_attention(
        query_weight, key_weight, value_weight, out_weight
    )
    local_width = query_w.shape[1]
    heads_here = local_width // HD
    column_start = tp_index * local_width
    query = (
        jnp.dot(normed, query_w, preferred_element_type=f32)
        + lax.dynamic_slice_in_dim(query_bias, column_start, local_width, 0)
    ).astype(bf16)
    key = jnp.dot(normed, key_w, preferred_element_type=f32).astype(bf16)
    value = (
        jnp.dot(normed, value_w, preferred_element_type=f32)
        + lax.dynamic_slice_in_dim(value_bias, column_start, local_width, 0)
    ).astype(bf16)
    padded = extended(jnp.stack([key, value]), (("fsdp", 1),), margin)
    group_base = fsdp_index * group_rows
    clip_ids = jnp.arange(clip_lengths.shape[0])
    block_count = group_rows // QB

    def block_scores(block_index):
        first_row = block_index * QB
        clip_index = (group_base + first_row) // CLIP
        key_start = clip_index * CLIP - group_base + margin
        length = jnp.sum(jnp.where(clip_ids == clip_index, clip_lengths, 0))
        query_block = lax.dynamic_slice_in_dim(query, first_row, QB, 0).reshape(QB, heads_here, HD)
        pair = lax.dynamic_slice_in_dim(padded, key_start, CLIP, 1).reshape(2, CLIP, heads_here, HD)
        scores = (
            jnp.einsum("qhe,khe->hqk", query_block, pair[0], preferred_element_type=f32)
            * score_scale
        )
        scores = jnp.where((jnp.arange(CLIP) < length)[None, None, :], scores, far_negative)
        return (first_row, key_start, query_block, pair[0], pair[1], scores)

    def attend(block_index, carry):
        context_rows, total_rows = carry
        first_row, key_start, query_block, key_block, value_block, scores = block_scores(
            block_index
        )
        highest = jnp.max(scores, axis=-1, keepdims=True)
        log_total = highest[..., 0] + jnp.log(jnp.sum(jnp.exp(scores - highest), axis=-1))
        weights = jnp.exp(scores - log_total[..., None]).astype(bf16)
        block_out = jnp.einsum("hqk,khe->qhe", weights, value_block, preferred_element_type=f32)
        block_out = block_out.astype(bf16).reshape(QB, local_width)
        context_rows = lax.dynamic_update_slice_in_dim(context_rows, block_out, first_row, 0)
        total_rows = lax.dynamic_update_slice_in_dim(total_rows, log_total, first_row, 1)
        return (context_rows, total_rows)

    context, totals = lax.fori_loop(
        0,
        block_count,
        attend,
        (jnp.zeros((group_rows, local_width), bf16), jnp.zeros((heads_here, group_rows), f32)),
    )
    attended = lax.psum_scatter(
        contract_cols(context, out_w), "tp", scatter_dimension=0, tiled=True
    )
    hidden = inputs + attended + out_bias
    unit2, spread2, normed2_full = normalize(hidden, norm2_gain, norm2_shift)
    normed2_own = normed2_full.astype(bf16)
    normed2 = lax.all_gather(normed2_own, "tp", axis=0, tiled=True)
    w_up, w_down = (
        lax.all_gather(fc1_weight, "fsdp", axis=0, tiled=True),
        lax.all_gather(fc2_weight, "fsdp", axis=0, tiled=True),
    )
    unit_count = fc1_weight.shape[0]
    bias_up = lax.dynamic_index_in_dim(
        fc1_bias.reshape(fsdp_count, tp_count, unit_count), tp_index, 1, False
    ).reshape(-1)
    preact = contract_cols(normed2, w_up) + bias_up
    activated = gelu_exact(preact).astype(bf16)
    mixed = lax.psum_scatter(
        jnp.dot(activated, w_down, preferred_element_type=f32),
        "tp",
        scatter_dimension=0,
        tiled=True,
    )
    outputs = hidden + mixed + fc2_bias
    up_rounded = out_cotangent.astype(bf16)
    dactivated = contract_cols(up_rounded, w_down)
    dpreact = (dactivated * gelu_slope(preact)).astype(bf16)
    grad_up_part = contract_rows(dpreact, normed2)
    grad_down_part = contract_rows(activated, up_rounded)
    upbias_part = jnp.sum(dpreact.astype(f32), axis=0)
    grad_b1 = (upbias_part.reshape(fsdp_count, 1, unit_count) * tp_slot[None, :, None]).reshape(-1)
    dnorm2 = lax.psum_scatter(
        jnp.dot(dpreact, w_up, preferred_element_type=f32), "tp", scatter_dimension=0, tiled=True
    )
    grad_fc1, grad_fc2 = (
        lax.psum_scatter(grad_up_part, "fsdp", scatter_dimension=0, tiled=True),
        lax.psum_scatter(grad_down_part, "fsdp", scatter_dimension=0, tiled=True),
    )
    grad_b2 = jnp.sum(own_cotangent, axis=0)
    grad_gain2 = jnp.sum(dnorm2 * unit2, axis=0)
    grad_shift2 = jnp.sum(dnorm2, axis=0)
    dhidden = own_cotangent + norm_back(dnorm2, unit2, spread2, norm2_gain)
    grad_obias = jnp.sum(dhidden, axis=0)
    query_w, key_w, value_w, out_w = fetch_attention(
        query_weight, key_weight, value_weight, out_weight
    )
    dh_all = lax.all_gather(dhidden.astype(bf16), "tp", axis=0, tiled=True)
    dcontext = jnp.dot(dh_all, out_w, preferred_element_type=f32).astype(bf16)
    grad_out = contract_rows(dh_all, context)
    delta = jnp.sum(
        (dcontext.astype(f32) * context.astype(f32)).reshape(group_rows, heads_here, HD), axis=-1
    ).T

    def attend_back(block_index, carry):
        dquery_rows, dpair = carry
        first_row, key_start, query_block, key_block, value_block, scores = block_scores(
            block_index
        )
        grad_block = lax.dynamic_slice_in_dim(dcontext, first_row, QB, 0).reshape(
            QB, heads_here, HD
        )
        probs = jnp.exp(scores - lax.dynamic_slice_in_dim(totals, first_row, QB, 1)[..., None])
        delta_block = lax.dynamic_slice_in_dim(delta, first_row, QB, 1)
        dprobs = jnp.einsum("qhe,khe->hqk", grad_block, value_block, preferred_element_type=f32)
        dscores = (probs * (dprobs - delta_block[..., None]) * score_scale).astype(bf16)
        dquery_block = jnp.einsum("hqk,khe->qhe", dscores, key_block, preferred_element_type=f32)
        dquery_block = dquery_block.astype(bf16).reshape(QB, local_width)
        dkey_block = jnp.einsum(
            "hqk,qhe->khe", dscores, query_block, preferred_element_type=f32
        ).reshape(CLIP, local_width)
        dvalue_block = jnp.einsum(
            "hqk,qhe->khe", probs.astype(bf16), grad_block, preferred_element_type=f32
        ).reshape(CLIP, local_width)
        current = lax.dynamic_slice_in_dim(dpair, key_start, CLIP, 1)
        dpair = lax.dynamic_update_slice_in_dim(
            dpair, current + jnp.stack([dkey_block, dvalue_block]), key_start, 1
        )
        dquery_rows = lax.dynamic_update_slice_in_dim(dquery_rows, dquery_block, first_row, 0)
        return (dquery_rows, dpair)

    dquery, dpair = lax.fori_loop(
        0,
        block_count,
        attend_back,
        (jnp.zeros((group_rows, local_width), bf16), jnp.zeros(padded.shape, f32)),
    )
    rims = jnp.concatenate([dpair[:, :margin], dpair[:, margin + group_rows :]], axis=1)
    received = extended(rims, (("fsdp", 1),), margin)
    inner_part = dpair[:, margin : margin + group_rows]
    inner_part = inner_part.at[:, :margin].add(received[:, :margin])
    inner_part = inner_part.at[:, group_rows - margin :].add(received[:, 3 * margin :])
    dkey = inner_part[0].astype(bf16)
    dvalue = inner_part[1].astype(bf16)
    grad_query = contract_rows(normed, dquery)
    grad_key = contract_rows(normed, dkey)
    grad_value = contract_rows(normed, dvalue)
    grad_qbias = (tp_slot[:, None] * jnp.sum(dquery.astype(f32), axis=0)[None, :]).reshape(-1)
    grad_vbias = (tp_slot[:, None] * jnp.sum(dvalue.astype(f32), axis=0)[None, :]).reshape(-1)
    dnorm1 = lax.psum_scatter(
        contract_cols(dquery, query_w)
        + contract_cols(dkey, key_w)
        + contract_cols(dvalue, value_w),
        "tp",
        scatter_dimension=0,
        tiled=True,
    )
    grad_gain1 = jnp.sum(dnorm1 * unit1, axis=0)
    grad_shift1 = jnp.sum(dnorm1, axis=0)
    inputs_grad = dhidden + norm_back(dnorm1, unit1, spread1, norm1_gain)
    grad_query, grad_key, grad_value, grad_out = (
        lax.psum_scatter(grad_query, "fsdp", scatter_dimension=0, tiled=True),
        lax.psum_scatter(grad_key, "fsdp", scatter_dimension=0, tiled=True),
        lax.psum_scatter(grad_value, "fsdp", scatter_dimension=0, tiled=True),
        lax.psum_scatter(grad_out, "fsdp", scatter_dimension=0, tiled=True),
    )
    (
        grad_gain1,
        grad_shift1,
        grad_qbias,
        grad_vbias,
        grad_obias,
        grad_gain2,
        grad_shift2,
        grad_b1,
        grad_b2,
    ) = lax.psum(
        (
            grad_gain1,
            grad_shift1,
            grad_qbias,
            grad_vbias,
            grad_obias,
            grad_gain2,
            grad_shift2,
            grad_b1,
            grad_b2,
        ),
        ("fsdp", "tp"),
    )
    return (
        outputs,
        inputs_grad,
        grad_gain1,
        grad_shift1,
        grad_query,
        grad_qbias,
        grad_key,
        grad_value,
        grad_vbias,
        grad_out,
        grad_obias,
        grad_gain2,
        grad_shift2,
        grad_fc1,
        grad_b1,
        grad_fc2,
        grad_b2,
    )


def solution(mesh):
    in_specs = (
        P(("fsdp", "tp"), None),
        P("fsdp", None),
        P(),
        P(),
        P(),
        P("fsdp", "tp"),
        P(),
        P("fsdp", "tp"),
        P("fsdp", "tp"),
        P(),
        P("fsdp", "tp"),
        P(),
        P(),
        P(),
        P(("fsdp", "tp"), None),
        P(),
        P(("fsdp", "tp"), None),
        P(),
    )
    out_specs = (
        P(("fsdp", "tp"), None),
        P(("fsdp", "tp"), None),
        P(),
        P(),
        P("fsdp", "tp"),
        P(),
        P("fsdp", "tp"),
        P("fsdp", "tp"),
        P(),
        P("fsdp", "tp"),
        P(),
        P(),
        P(),
        P(("fsdp", "tp"), None),
        P(),
        P(("fsdp", "tp"), None),
        P(),
    )
    return jax.shard_map(
        on_device, mesh=mesh, in_specs=in_specs, out_specs=out_specs, check_vma=False
    )
```

profile of v0, /device:TPU:0, one launch (start us, length us, event | category | flops | bytes accessed | tf_op | source)
XLA Modules:
  0.0 818.0 jit_solution(7291975622718793777)
XLA Ops:
  10.7 2.1 add_convert_fusion.2
  13.7 11.0 %all_gather.32 = bf16[768,192]{1,0:T(8,128)(2,1)S(1)} all-gather(bf16[96,192]{1,0:T(8,128)(2,1)S(1)} %copy-done.22), channel_id=1, replica_groups=mesh['fsdp'=8,'tp'=4] {'fsdp'}, dimensions={0}, use_global_device_ids=true | all-gather | bytes 331776 | tf_op jit(solution)/shard_map/all_gather | solution.py:75
  24.7 9.5 %all_gather.33 = bf16[768,192]{1,0:T(8,128)(2,1)S(1)} all-gather(bf16[96,192]{1,0:T(8,128)(2,1)S(1)} %copy-done.23), channel_id=1, replica_groups=mesh['fsdp'=8,'tp'=4] {'fsdp'}, dimensions={0}, use_global_device_ids=true | all-gather | bytes 331776 | tf_op jit(solution)/shard_map/all_gather | solution.py:76
  34.3 18.5 %all-gather.6.cloned.1.call-done = bf16[1024,768]{1,0:T(8,128)(2,1)} async-done(((bf16[256,768]{1,0:T(8,128)(2,1)}), bf16[1024,768]{1,0:T(8,128)(2,1)}) %all-gather.6.cloned.1.call-update) | async-done | bytes 1572880 | tf_op jit(solution)/shard_map/all_gather | solution.py:114
  52.8 2.2 fusion.27
  55.0 2.1 fusion.28
  59.3 4.0 collective-permute-start
  64.0 18.6 %all_gather.34 = bf16[768,192]{1,0:T(8,128)(2,1)S(1)} all-gather(bf16[96,192]{1,0:T(8,128)(2,1)S(1)} %copy-done.24), channel_id=1, replica_groups=mesh['fsdp'=8,'tp'=4] {'fsdp'}, dimensions={0}, use_global_device_ids=true | all-gather | bytes 331776 | tf_op jit(solution)/shard_map/all_gather | solution.py:74
  82.6 11.4 %all_gather.35 = bf16[768,192]{1,0:T(8,128)(2,1)} all-gather(bf16[96,192]{1,0:T(8,128)(2,1)S(1)} %copy-done.25), channel_id=1, replica_groups=mesh['fsdp'=8,'tp'=4] {'fsdp'}, dimensions={0}, use_global_device_ids=true | all-gather | bytes 331776 | tf_op jit(solution)/shard_map/all_gather | solution.py:77
  94.7 1.5 pad_maximum_fusion
  97.1 17.5 %while.40 = (s32[]{:T(128)}, bf16[1024,192]{0,1:T(8,128)(2,1)}, f32[3,1024]{1,0:T(4,128)S(1)}, s32[]{:T(128)}, bf16[2,3072,192]{1,2,0:T(8,128)(2,1)S(1)}, /*inde...) while((s32[]{:T(128)}, bf16[1024,192]{0,1:T(8,128)(2,1)}, ...), condition=%wide.region_6.7_spmd.clone, body=%wide.region_2.6_spmd.clone.sunk | while | flops 630030336 | bytes 36239832 | solution.py:163
  99.1 1.6 fusion.114
  100.7 2.1 exponential_reduce_fusion.2
  102.8 2.2 fusion.115
  107.9 1.6 fusion.114
  109.5 2.1 exponential_reduce_fusion.2
  111.6 2.2 fusion.115
  114.6 3.5 fusion.40
  118.7 58.8 %reduce-scatter.11.cloned.1.call-done = f32[256,768]{1,0:T(8,128)} async-done(((f32[1024,768]{1,0:T(8,128)}), f32[256,768]{1,0:T(8,128)}) %reduce-scatter.11.cloned.1.call-update) | async-done | bytes 786448 | tf_op jit(solution)/shard_map/reduce_scatter | solution.py:169
  181.5 1.4 reshape.289
  184.3 33.2 %all-gather.8.cloned.1.call-done = bf16[1024,768]{1,0:T(8,128)(2,1)} async-done(((bf16[256,768]{1,0:T(8,128)(2,1)}), bf16[1024,768]{1,0:T(8,128)(2,1)}) %all-gather.8.cloned.1.call-update) | async-done | bytes 1572880 | tf_op jit(solution)/shard_map/all_gather | solution.py:175
  217.6 5.4 multiply_convert_fusion.1
  223.0 19.1 %all-gather.12.cloned.1.call-done = bf16[768,768]{1,0:T(8,128)(2,1)} async-done(((bf16[96,768]{1,0:T(8,128)(2,1)}), bf16[768,768]{1,0:T(8,128)(2,1)}) %all-gather.12.cloned.1.call-update) | async-done | bytes 1179664 | tf_op jit(solution)/shard_map/all_gather | solution.py:178
  242.1 6.1 convert_reduce_fusion
  249.4 3.0 fusion.42
  252.5 4.8 fusion.41
  257.4 55.6 %reduce-scatter.15.cloned.1.call-done = f32[256,768]{1,0:T(8,128)} async-done(((f32[1024,768]{1,0:T(8,128)}), f32[256,768]{1,0:T(8,128)}) %reduce-scatter.15.cloned.1.call-update) | async-done | bytes 786448 | tf_op jit(solution)/shard_map/reduce_scatter | solution.py:200
  312.9 2.4 multiply_reduce_fusion
  315.9 59.7 %reduce-scatter.13.cloned.1.call-done = f32[256,768]{1,0:T(8,128)} async-done(((f32[1024,768]{1,0:T(8,128)}), f32[256,768]{1,0:T(8,128)}) %reduce-scatter.13.cloned.1.call-update) | async-done | bytes 786448 | tf_op jit(solution)/shard_map/reduce_scatter | solution.py:186
  375.5 3.7 fusion.35
  381.2 36.8 %all-gather.14.cloned.1.call-done = bf16[1024,768]{1,0:T(8,128)(2,1)} async-done(((bf16[256,768]{1,0:T(8,128)(2,1)}), bf16[1024,768]{1,0:T(8,128)(2,1)}) %all-gather.14.cloned.1.call-update) | async-done | bytes 1572880 | tf_op jit(solution)/shard_map/all_gather | solution.py:215
  418.0 3.3 convert_multiply_fusion
  423.2 2.7 broadcast_in_dim.131
  425.9 32.3 %while.41 = (s32[]{:T(128)}, bf16[1024,192]{0,1:T(8,128)(2,1)}, f32[2,3072,192]{1,2,0:T(8,128)}, s32[]{:T(128)}, bf16[2,3072,192]{1,2,0:T(8,128)(2,1)S(1)}, /*in...) while((s32[]{:T(128)}, bf16[1024,192]{0,1:T(8,128)(2,1)}, ...), condition=%wide.region_17.18_spmd.clone, body=%wide.region_15.17_spmd.clone.sunk | while | flops 1537181184 | bytes 94420032 | solution.py:249
  429.7 1.4 fusion.126
  431.1 2.1 fusion.128
  433.2 3.4 multiply_convert_fusion.3
  436.6 1.5 convolution_convert_fusion.4
  440.0 2.1 copy-done
  445.8 1.4 fusion.126
  447.2 2.1 fusion.128
  449.3 3.4 multiply_convert_fusion.3
  452.8 1.5 convolution_convert_fusion.4
  456.1 2.1 copy-done
  458.2 2.2 fusion.37
  460.4 1.4 collective-permute-start.2
  464.7 4.0 collective-permute-done.3
  468.7 1.8 add_convert_fusion
  471.8 2.3 add_add_fusion
  475.5 4.3 fusion.46
  480.2 5.2 fusion.29
  485.5 3.0 fusion.45
  488.6 1.6 fusion.44
  491.4 1.6 fusion.32
  496.9 2.5 fusion.34
  499.4 63.9 %reduce-scatter.17.cloned.1.call-done = f32[256,768]{1,0:T(8,128)} async-done(((f32[1024,768]{1,0:T(8,128)}), f32[256,768]{1,0:T(8,128)}) %reduce-scatter.17.cloned.1.call-update) | async-done | bytes 786448 | tf_op jit(solution)/shard_map/reduce_scatter | solution.py:267
  563.3 1.5 multiply_reduce_fusion.1
  564.9 41.5 %all-reduce = (f32[768]{0:T(1024)}, f32[768]{0:T(1024)}, f32[768]{0:T(1024)}, f32[768]{0:T(1024)}, f32[768]{0:T(1024)}, /*index=5*/f32[768]{0:T(1024)}, f32[768]{0:T(1024)}, f32[3072]{0:T(1024)}, f32[768]{0:T(1024)}) all-reduce(f32[768]{0:T(1024)S(1)} %get-tuple-element.569, ...), channel_id=1, replica_groups=mesh['fsdp'=8,'tp'=4] {'fsdp','tp'}, use_global_device_ids=true, to_apply=%region_22.23 | all-reduce | flops 9216 | bytes 73728 | tf_op jit(solution)/shard_map/psum | solution.py:294
  606.4 2.3 multiply_add_fusion
  609.5 46.3 %reduce-scatter.29.cloned.1.call-done = f32[96,768]{1,0:T(8,128)} async-done(((f32[768,768]{1,0:T(8,128)}), f32[96,768]{1,0:T(8,128)}) %reduce-scatter.29.cloned.1.call-update) | async-done | bytes 294928 | tf_op jit(solution)/shard_map/reduce_scatter | solution.py:205
  655.8 38.7 %reduce-scatter.25.cloned.1.call-done = f32[96,192]{1,0:T(8,128)} async-done(((f32[768,192]{1,0:T(8,128)}), f32[96,192]{1,0:T(8,128)}) %reduce-scatter.25.cloned.1.call-update) | async-done | bytes 73744 | tf_op jit(solution)/shard_map/reduce_scatter | solution.py:282
  694.5 38.7 %reduce-scatter.19.cloned.1.call-done = f32[96,192]{1,0:T(8,128)} async-done(((f32[768,192]{1,0:T(8,128)}), f32[96,192]{1,0:T(8,128)}) %reduce-scatter.19.cloned.1.call-update) | async-done | bytes 73744 | tf_op jit(solution)/shard_map/reduce_scatter | solution.py:279
  733.2 38.7 %reduce-scatter.21.cloned.1.call-done = f32[96,192]{1,0:T(8,128)} async-done(((f32[768,192]{1,0:T(8,128)}), f32[96,192]{1,0:T(8,128)}) %reduce-scatter.21.cloned.1.call-update) | async-done | bytes 73744 | tf_op jit(solution)/shard_map/reduce_scatter | solution.py:280
  771.9 38.6 %reduce-scatter.23.cloned.1.call-done = f32[96,192]{1,0:T(8,128)} async-done(((f32[768,192]{1,0:T(8,128)}), f32[96,192]{1,0:T(8,128)}) %reduce-scatter.23.cloned.1.call-update) | async-done | bytes 73744 | tf_op jit(solution)/shard_map/reduce_scatter | solution.py:281
  (203 shorter events, 48.2 us)
Async XLA Ops:
  8.0 5.7 copy-start.22
  8.0 16.7 %copy-start.23 = (bf16[96,192]{1,0:T(8,128)(2,1)S(1)}, bf16[96,192]{1,0:T(8,128)(2,1)}, u32[]{:S(2)}) copy-start(bf16[96,192]{1,0:T(8,128)(2,1)} %param.38) | copy-start | bytes 110596
  8.0 44.7 %all-gather.6.cloned.1.call-start = ((), (), s32[]{:S(2)}) async-start(), calls=%async_computation.10 | async-start | bytes 1966080 | tf_op jit(solution)/shard_map/all_gather | solution.py:114
  9.3 24.9 %copy-start.29 = (f32[256]{0:T(256)}, f32[256]{0:T(256)S(1)}, u32[]{:S(2)}) copy-start(f32[256]{0:T(256)S(1)} %broadcast_multiply_fusion.8) | copy-start | bytes 3076
  10.7 23.5 %copy-start.31 = (f32[256]{0:T(256)}, f32[256]{0:T(256)S(1)}, u32[]{:S(2)}) copy-start(f32[256]{0:T(256)S(1)} %add_rsqrt_fusion.1) | copy-start | bytes 3076
  12.9 164.7 %reduce-scatter.11.cloned.1.call-start = ((), (), s32[]{:S(2)}) async-start(), calls=%async_computation.11 | async-start | bytes 3932160 | tf_op jit(solution)/shard_map/reduce_scatter | solution.py:169
  24.7 33.3 %copy-start.17 = (bf16[768,192]{1,0:T(8,128)(2,1)}, bf16[768,192]{1,0:T(8,128)(2,1)S(1)}, u32[]{:S(2)}) copy-start(bf16[768,192]{1,0:T(8,128)(2,1)S(1)} %all_gather.32) | copy-start | bytes 884740
  34.3 23.7 %copy-start.15 = (bf16[768,192]{1,0:T(8,128)(2,1)}, bf16[768,192]{1,0:T(8,128)(2,1)S(1)}, u32[]{:S(2)}) copy-start(bf16[768,192]{1,0:T(8,128)(2,1)S(1)} %all_gather.33) | copy-start | bytes 884740
  34.3 29.8 %copy-start.24 = (bf16[96,192]{1,0:T(8,128)(2,1)S(1)}, bf16[96,192]{1,0:T(8,128)(2,1)}, u32[]{:S(2)}) copy-start(bf16[96,192]{1,0:T(8,128)(2,1)} %param.35) | copy-start | bytes 110596
  34.3 48.3 %copy-start.25 = (bf16[96,192]{1,0:T(8,128)(2,1)S(1)}, bf16[96,192]{1,0:T(8,128)(2,1)}, u32[]{:S(2)}) copy-start(bf16[96,192]{1,0:T(8,128)(2,1)} %param.40) | copy-start | bytes 110596
  52.8 41.2 %copy-start.2 = (bf16[1024,768]{1,0:T(8,128)(2,1)S(1)}, bf16[1024,768]{1,0:T(8,128)(2,1)}, u32[]{:S(2)}) copy-start(bf16[1024,768]{1,0:T(8,128)(2,1)} %all-gather.6.cloned.1.call-done) | copy-start | bytes 4718596
  58.0 36.7 %collective-permute-start.1 = (bf16[2,1024,192]{1,2,0:T(8,128)(2,1)}, bf16[2,1024,192]{1,2,0:T(8,128)(2,1)}, u32[]{:S(2)}, u32[]{:S(2)}) collective-permute-start(bf16[2,1024,192]{1,2,0:T(8,128)(2,1)} %pad_maximum_fusion.1), channel_id=1, source_target_pairs={{4,0},{8,4},{12,8},{16,12},{20,16},{24,20},{28,24},{5,1},{9,5},{13... | collective-permute-start | bytes 2359304 | tf_op jit(solution)/shard_map/ppermute | solution.py:27
  59.3 35.4 %collective-permute-start = (bf16[2,1024,192]{1,2,0:T(8,128)(2,1)}, bf16[2,1024,192]{1,2,0:T(8,128)(2,1)}, u32[]{:S(2)}, u32[]{:S(2)}) collective-permute-start(bf16[2,1024,192]{1,2,0:T(8,128)(2,1)} %pad_maximum_fusion.1), channel_id=1, source_target_pairs={{0,4},{4,8},{8,12},{12,16},{16,20},{20,24},{24,28},{1,5},{5,9},{9,... | collective-permute-start | bytes 2359304 | tf_op jit(solution)/shard_map/ppermute | solution.py:26
  82.6 12.1 %copy-start.19 = (bf16[768,192]{1,0:T(8,128)(2,1)}, bf16[768,192]{1,0:T(8,128)(2,1)S(1)}, u32[]{:S(2)}) copy-start(bf16[768,192]{1,0:T(8,128)(2,1)S(1)} %all_gather.34) | copy-start | bytes 884740
  102.8 2.2 copy-start.7
  111.6 2.2 copy-start.7
  114.6 3.5 copy-start.21
  114.6 63.0 %copy-start.1 = (f32[256,768]{1,0:T(8,128)S(1)}, f32[256,768]{1,0:T(8,128)}, u32[]{:S(2)}) copy-start(f32[256,768]{1,0:T(8,128)} %param.30) | copy-start | bytes 2359300
  118.1 66.3 %all-gather.10.cloned.1.call-start = ((), (), s32[]{:S(2)}) async-start(), calls=%async_computation.13 | async-start | bytes 1327104 | tf_op jit(solution)/shard_map/all_gather | solution.py:177
  118.1 61.6 %copy-start.28 = (f32[768]{0:T(1024)S(1)}, f32[768]{0:T(1024)}, u32[]{:S(2)}) copy-start(f32[768]{0:T(1024)} %param.42) | copy-start | bytes 9220
  118.1 61.6 %copy-start.37 = (f32[768]{0:T(1024)S(1)}, f32[768]{0:T(1024)}, u32[]{:S(2)}) copy-start(f32[768]{0:T(1024)} %param.43) | copy-start | bytes 9220
  118.7 98.9 %all-gather.8.cloned.1.call-start = ((), (), s32[]{:S(2)}) async-start(), calls=%async_computation.12 | async-start | bytes 1966080 | tf_op jit(solution)/shard_map/all_gather | solution.py:175
  180.7 61.4 %all-gather.12.cloned.1.call-start = ((), (), s32[]{:S(2)}) async-start(), calls=%async_computation.14 | async-start | bytes 1327104 | tf_op jit(solution)/shard_map/all_gather | solution.py:178
  181.3 131.6 %reduce-scatter.15.cloned.1.call-start = ((), (), s32[]{:S(2)}) async-start(), calls=%async_computation.16 | async-start | bytes 3932160 | tf_op jit(solution)/shard_map/reduce_scatter | solution.py:200
  184.3 57.8 %copy-start.39 = (f32[768]{0:T(1024)S(1)}, f32[768]{0:T(1024)}, u32[]{:S(2)}) copy-start(f32[768]{0:T(1024)} %add.362) | copy-start | bytes 9220
  242.1 7.3 copy-start.41
  248.2 1.2 copy-start.42
  252.4 123.1 %reduce-scatter.13.cloned.1.call-start = ((), (), s32[]{:S(2)}) async-start(), calls=%async_computation.15 | async-start | bytes 3932160 | tf_op jit(solution)/shard_map/reduce_scatter | solution.py:186
  257.3 160.7 %all-gather.14.cloned.1.call-start = ((), (), s32[]{:S(2)}) async-start(), calls=%async_computation.17 | async-start | bytes 1966080 | tf_op jit(solution)/shard_map/all_gather | solution.py:215
  380.9 182.4 %reduce-scatter.17.cloned.1.call-start = ((), (), s32[]{:S(2)}) async-start(), calls=%async_computation.18 | async-start | bytes 3932160 | tf_op jit(solution)/shard_map/reduce_scatter | solution.py:267
  431.1 8.1 slice-start
  433.2 6.0 slice-start.1
  438.1 1.0 copy-start.10
  440.0 2.1 copy-start
  447.2 8.1 slice-start
  449.3 6.0 slice-start.1
  456.1 2.1 copy-start
  458.2 4.9 copy-start.12
  458.2 4.9 copy-start.20
  460.4 4.3 collective-permute-start.2
  461.8 6.9 collective-permute-start.3
  463.8 6.7 copy-start.18
  470.5 3.6 copy-start.13
  470.5 1.3 copy-start.16
  474.1 1.4 copy-start.40
  474.1 135.3 %reduce-scatter.27.cloned.1.call-start = ((), (), s32[]{:S(2)}) async-start(), calls=%async_computation.23 | async-start | bytes 2654208 | tf_op jit(solution)/shard_map/reduce_scatter | solution.py:204
  479.9 5.6 copy-start.9
  479.9 175.9 %reduce-scatter.29.cloned.1.call-start = ((), (), s32[]{:S(2)}) async-start(), calls=%async_computation.24 | async-start | bytes 2654208 | tf_op jit(solution)/shard_map/reduce_scatter | solution.py:205
  485.4 3.2 copy-start.3
  485.4 5.4 copy-start.38
  485.4 209.1 %reduce-scatter.25.cloned.1.call-start = ((), (), s32[]{:S(2)}) async-start(), calls=%async_computation.22 | async-start | bytes 884736 | tf_op jit(solution)/shard_map/reduce_scatter | solution.py:282
  488.5 2.9 copy-start.14
  488.5 244.7 %reduce-scatter.19.cloned.1.call-start = ((), (), s32[]{:S(2)}) async-start(), calls=%async_computation.19 | async-start | bytes 884736 | tf_op jit(solution)/shard_map/reduce_scatter | solution.py:279
  490.2 281.7 %reduce-scatter.21.cloned.1.call-start = ((), (), s32[]{:S(2)}) async-start(), calls=%async_computation.20 | async-start | bytes 884736 | tf_op jit(solution)/shard_map/reduce_scatter | solution.py:280
  493.0 113.4 %copy-start.6 = (f32[256,768]{1,0:T(8,128)S(1)}, f32[256,768]{1,0:T(8,128)}, u32[]{:S(2)}) copy-start(f32[256,768]{1,0:T(8,128)} %copy-done.5) | copy-start | bytes 2359300
  493.1 317.4 %reduce-scatter.23.cloned.1.call-start = ((), (), s32[]{:S(2)}) async-start(), calls=%async_computation.21 | async-start | bytes 884736 | tf_op jit(solution)/shard_map/reduce_scatter | solution.py:281
  494.6 68.7 %copy-start.27 = (f32[768]{0:T(1024)S(1)}, f32[768]{0:T(1024)}, u32[]{:S(2)}) copy-start(f32[768]{0:T(1024)} %param.33) | copy-start | bytes 9220
  494.6 70.2 %copy-start.26 = (f32[3072]{0:T(1024)S(1)}, f32[3072]{0:T(1024)}, u32[]{:S(2)}) copy-start(f32[3072]{0:T(1024)} %mul.315) | copy-start | bytes 36868
  494.8 68.5 %copy-start.30 = (f32[256]{0:T(256)S(1)}, f32[256]{0:T(256)}, u32[]{:S(2)}) copy-start(f32[256]{0:T(256)} %copy-done.29) | copy-start | bytes 3076
  494.8 68.5 %copy-start.32 = (f32[256]{0:T(256)S(1)}, f32[256]{0:T(256)}, u32[]{:S(2)}) copy-start(f32[256]{0:T(256)} %copy-done.31) | copy-start | bytes 3076
  494.8 70.1 %copy-start.33 = (f32[768]{0:T(1024)S(1)}, f32[768]{0:T(1024)}, u32[]{:S(2)}) copy-start(f32[768]{0:T(1024)} %get-tuple-element.567) | copy-start | bytes 9220
  494.8 70.1 %copy-start.34 = (f32[768]{0:T(1024)S(1)}, f32[768]{0:T(1024)}, u32[]{:S(2)}) copy-start(f32[768]{0:T(1024)} %get-tuple-element.573) | copy-start | bytes 9220
  494.8 70.1 %copy-start.35 = (f32[768]{0:T(1024)S(1)}, f32[768]{0:T(1024)}, u32[]{:S(2)}) copy-start(f32[768]{0:T(1024)} %get-tuple-element.620) | copy-start | bytes 9220
  494.8 70.1 %copy-start.36 = (f32[768]{0:T(1024)S(1)}, f32[768]{0:T(1024)}, u32[]{:S(2)}) copy-start(f32[768]{0:T(1024)} %get-tuple-element.636) | copy-start | bytes 9220
  (7 other events, 5.8 us)
Sparse Core Ops, SparseCore 0:
  13.0 39.7 all-gather.5
  118.2 59.3 reduce-scatter.10
  381.1 36.8 all-gather.13
  474.3 89.0 reduce-scatter.16
  567.1 42.3 reduce-scatter.26
  613.3 42.4 reduce-scatter.28
  659.5 34.9 reduce-scatter.24
  698.2 34.9 reduce-scatter.18
  736.9 34.9 reduce-scatter.20
  775.5 34.9 reduce-scatter.22
Sparse Core Ops, SparseCore 1:
  120.4 22.7 all-gather.9
  180.8 36.7 all-gather.7
  219.3 22.7 all-gather.11
  252.5 60.4 reduce-scatter.14
  315.3 60.2 reduce-scatter.12
where the time goes:
time: 820 us; the launch traced here: 818 us
  waiting for transfers between devices  553 us (67%)
  blocking collectives  92.1 us (11%)
  matrix products  79.1 us (10%)
  other arithmetic  40.3 us (5%)
  local copies, waits for them, and re-layouts  27.3 us (3%)
  between operations  16.3 us (2%)
  starting transfers between devices  9.21 us (1%)
    reduce_scatter x1, waiting for transfers between devices, on_device(): lax.psum_scatter(contract_cols(dquery, query_w) + contract_cols(dkey, key...  63.9 us
    reduce_scatter x1, waiting for transfers between devices, on_device(): lax.psum_scatter(jnp.dot(activated, w_down, preferred_element_type=f32),...  59.7 us
    reduce_scatter x1, waiting for transfers between devices, on_device(): lax.psum_scatter(contract_cols(context, out_w), 'tp', scatter_dimension=0...  58.8 us
    reduce_scatter x1, waiting for transfers between devices, on_device(): lax.psum_scatter(jnp.dot(dpreact, w_up, preferred_element_type=f32), 'tp'...  55.6 us
    reduce_scatter x1, waiting for transfers between devices, on_device(): lax.psum_scatter(grad_down_part, 'fsdp', scatter_dimension=0, tiled=True)  46.3 us
    psum x1, blocking collectives, on_device(): lax.psum((grad_gain1, grad_shift1, grad_qbias, grad_vbias, grad_obias, gr...  41.5 us
    reduce_scatter x1, waiting for transfers between devices, on_device(): lax.psum_scatter(grad_key, 'fsdp', scatter_dimension=0, tiled=True)  38.7 us
    reduce_scatter x1, waiting for transfers between devices, on_device(): lax.psum_scatter(grad_query, 'fsdp', scatter_dimension=0, tiled=True)  38.7 us
  transfers between devices with their start and end apart: 19, of which 16 were waited for; matrix products, arithmetic and copies ran while one was open for 6% of the time, Pallas kernels for 0%

commit v1 on v0

--- a/solution.py
+++ b/solution.py
@@ -70,12 +70,14 @@
 
 
 def fetch_attention(query_weight, key_weight, value_weight, out_weight):
-    return (
-        lax.all_gather(query_weight, "fsdp", axis=0, tiled=True),
-        lax.all_gather(key_weight, "fsdp", axis=0, tiled=True),
-        lax.all_gather(value_weight, "fsdp", axis=0, tiled=True),
-        lax.all_gather(out_weight, "fsdp", axis=0, tiled=True),
-    )
+    joined = jnp.concatenate([query_weight, key_weight, value_weight, out_weight], axis=1)
+    return jnp.split(lax.all_gather(joined, "fsdp", axis=0, tiled=True), 4, axis=1)
+
+
+def scatter_rows(partial_rows, axis):
+    return lax.psum_scatter(
+        partial_rows.astype(jnp.bfloat16), axis, scatter_dimension=0, tiled=True
+    ).astype(jnp.float32)
 
 
 def on_device(
@@ -166,16 +168,17 @@
         attend,
         (jnp.zeros((group_rows, local_width), bf16), jnp.zeros((heads_here, group_rows), f32)),
     )
-    attended = lax.psum_scatter(
-        contract_cols(context, out_w), "tp", scatter_dimension=0, tiled=True
-    )
+    attended = scatter_rows(contract_cols(context, out_w), "tp")
     hidden = inputs + attended + out_bias
     unit2, spread2, normed2_full = normalize(hidden, norm2_gain, norm2_shift)
     normed2_own = normed2_full.astype(bf16)
     normed2 = lax.all_gather(normed2_own, "tp", axis=0, tiled=True)
-    w_up, w_down = (
-        lax.all_gather(fc1_weight, "fsdp", axis=0, tiled=True),
-        lax.all_gather(fc2_weight, "fsdp", axis=0, tiled=True),
+    w_up, w_down = jnp.split(
+        lax.all_gather(
+            jnp.concatenate([fc1_weight, fc2_weight], axis=1), "fsdp", axis=0, tiled=True
+        ),
+        2,
+        axis=1,
     )
     unit_count = fc1_weight.shape[0]
     bias_up = lax.dynamic_index_in_dim(
@@ -183,12 +186,7 @@
     ).reshape(-1)
     preact = contract_cols(normed2, w_up) + bias_up
     activated = gelu_exact(preact).astype(bf16)
-    mixed = lax.psum_scatter(
-        jnp.dot(activated, w_down, preferred_element_type=f32),
-        "tp",
-        scatter_dimension=0,
-        tiled=True,
-    )
+    mixed = scatter_rows(jnp.dot(activated, w_down, preferred_element_type=f32), "tp")
     outputs = hidden + mixed + fc2_bias
     up_rounded = out_cotangent.astype(bf16)
     dactivated = contract_cols(up_rounded, w_down)
@@ -197,21 +195,15 @@
     grad_down_part = contract_rows(activated, up_rounded)
     upbias_part = jnp.sum(dpreact.astype(f32), axis=0)
     grad_b1 = (upbias_part.reshape(fsdp_count, 1, unit_count) * tp_slot[None, :, None]).reshape(-1)
-    dnorm2 = lax.psum_scatter(
-        jnp.dot(dpreact, w_up, preferred_element_type=f32), "tp", scatter_dimension=0, tiled=True
-    )
-    grad_fc1, grad_fc2 = (
-        lax.psum_scatter(grad_up_part, "fsdp", scatter_dimension=0, tiled=True),
-        lax.psum_scatter(grad_down_part, "fsdp", scatter_dimension=0, tiled=True),
+    dnorm2 = scatter_rows(jnp.dot(dpreact, w_up, preferred_element_type=f32), "tp")
+    grad_fc1, grad_fc2 = jnp.split(
+        scatter_rows(jnp.concatenate([grad_up_part, grad_down_part], axis=1), "fsdp"), 2, axis=1
     )
     grad_b2 = jnp.sum(own_cotangent, axis=0)
     grad_gain2 = jnp.sum(dnorm2 * unit2, axis=0)
     grad_shift2 = jnp.sum(dnorm2, axis=0)
     dhidden = own_cotangent + norm_back(dnorm2, unit2, spread2, norm2_gain)
     grad_obias = jnp.sum(dhidden, axis=0)
-    query_w, key_w, value_w, out_w = fetch_attention(
-        query_weight, key_weight, value_weight, out_weight
-    )
     dh_all = lax.all_gather(dhidden.astype(bf16), "tp", axis=0, tiled=True)
     dcontext = jnp.dot(dh_all, out_w, preferred_element_type=f32).astype(bf16)
     grad_out = contract_rows(dh_all, context)
@@ -264,22 +256,21 @@
     grad_value = contract_rows(normed, dvalue)
     grad_qbias = (tp_slot[:, None] * jnp.sum(dquery.astype(f32), axis=0)[None, :]).reshape(-1)
     grad_vbias = (tp_slot[:, None] * jnp.sum(dvalue.astype(f32), axis=0)[None, :]).reshape(-1)
-    dnorm1 = lax.psum_scatter(
+    dnorm1 = scatter_rows(
         contract_cols(dquery, query_w)
         + contract_cols(dkey, key_w)
         + contract_cols(dvalue, value_w),
         "tp",
-        scatter_dimension=0,
-        tiled=True,
     )
     grad_gain1 = jnp.sum(dnorm1 * unit1, axis=0)
     grad_shift1 = jnp.sum(dnorm1, axis=0)
     inputs_grad = dhidden + norm_back(dnorm1, unit1, spread1, norm1_gain)
-    grad_query, grad_key, grad_value, grad_out = (
-        lax.psum_scatter(grad_query, "fsdp", scatter_dimension=0, tiled=True),
-        lax.psum_scatter(grad_key, "fsdp", scatter_dimension=0, tiled=True),
-        lax.psum_scatter(grad_value, "fsdp", scatter_dimension=0, tiled=True),
-        lax.psum_scatter(grad_out, "fsdp", scatter_dimension=0, tiled=True),
+    grad_query, grad_key, grad_value, grad_out = jnp.split(
+        scatter_rows(
+            jnp.concatenate([grad_query, grad_key, grad_value, grad_out], axis=1), "fsdp"
+        ),
+        4,
+        axis=1,
     )
     (
         grad_gain1,

time: 820 us -> 567 us (0.69)
  waiting for transfers between devices: 553 us -> 357 us
  blocking collectives: 92.1 us -> 40.4 us
  matrix products: 79.1 us -> 63.6 us
  local copies, waits for them, and re-layouts: 27.3 us -> 38 us
    reduce_scatter x10 -> x4, waiting for transfers between devices: 440 us -> 144 us  [scatter_rows(): lax.psum_scatter(partial_rows.astype(jnp.bfloat16), axis, scatter_dimensi...]
    unnamed x15 -> x13, waiting for transfers between devices: 1.23 us -> 58.2 us
    all_gather x4 -> x0, blocking collectives: 50.6 us -> none  [the longest x1 18.6 us: fetch_attention(): lax.all_gather(query_weight, 'fsdp', axis=0, tiled=True)]
    all_gather x2, waiting for transfers between devices: 19.1 us -> 47.2 us  [the longest x1 24.2 us: on_device(): lax.all_gather(jnp.concatenate([fc1_weight, fc2_weight], axis=1), 'fsdp',...]
    all_gather x1, waiting for transfers between devices: 18.5 us -> 39.2 us  [on_device(): normed = lax.all_gather(normed_own.astype(bf16), 'tp', axis=0, tiled=True)]
    all_gather x1, waiting for transfers between devices: 36.8 us -> 24.9 us  [on_device(): dh_all = lax.all_gather(dhidden.astype(bf16), 'tp', axis=0, tiled=True)]
    unnamed x76 -> x78, local copies, waits for them, and re-layouts: 4.8 us -> 16.6 us
    dot_general x6, matrix products: 18.2 us -> 6.93 us  [contract_rows(): lax.dot_general(left_rows, right_rows, (((0,), (0,)), ((), ())), preferre...]
  transfers between devices with their start and end apart: 19 -> 15, of which waited for: 16 -> 12; matrix products, arithmetic and copies ran while one was open for 6% -> 16% of each run, Pallas kernels for 0% -> 0%
where the time goes in v1:
time: 567 us; the launch traced here: 566 us
  waiting for transfers between devices  357 us (63%)
  matrix products  63.6 us (11%)
  other arithmetic  42.5 us (7%)
  blocking collectives  40.4 us (7%)
  local copies, waits for them, and re-layouts  38 us (7%)
  between operations  14.4 us (3%)
  starting transfers between devices  8.88 us (2%)
    reduce_scatter x4, waiting for transfers between devices, scatter_rows(): lax.psum_scatter(partial_rows.astype(jnp.bfloat16), axis, scatter_dimensi...  144 us
    unnamed x13, waiting for transfers between devices  58.2 us
    psum x1, blocking collectives, on_device(): lax.psum((grad_gain1, grad_shift1, grad_qbias, grad_vbias, grad_obias, gr...  40.4 us
    all_gather x1, waiting for transfers between devices, on_device(): normed = lax.all_gather(normed_own.astype(bf16), 'tp', axis=0, tiled=True)  39.2 us
    all_gather x1, waiting for transfers between devices, on_device(): normed2 = lax.all_gather(normed2_own, 'tp', axis=0, tiled=True)  39 us
    all_gather x1, waiting for transfers between devices, on_device(): dh_all = lax.all_gather(dhidden.astype(bf16), 'tp', axis=0, tiled=True)  24.9 us
    all_gather x1, waiting for transfers between devices, on_device(): lax.all_gather(jnp.concatenate([fc1_weight, fc2_weight], axis=1), 'fsdp',...  24.2 us
    all_gather x1, waiting for transfers between devices, fetch_attention(): lax.all_gather(joined, 'fsdp', axis=0, tiled=True)  23 us
  transfers between devices with their start and end apart: 15, of which 12 were waited for; matrix products, arithmetic and copies ran while one was open for 16% of the time, Pallas kernels for 0%

profile of v1, /device:TPU:0, one launch (start us, length us, event | category | flops | bytes accessed | tf_op | source)
XLA Modules:
  0.0 565.7 jit_solution(6796248868020964043)
XLA Ops:
  7.2 1.7 pad_maximum_fusion.5
  10.3 1.4 multiply_reduce_fusion.1
  11.7 1.6 add_convert_fusion.3
  14.2 23.0 %all-gather.8.cloned.1.call-done = bf16[768,768]{1,0:T(8,128)(2,1)} async-done(((bf16[96,768]{1,0:T(8,128)(2,1)}), bf16[768,768]{1,0:T(8,128)(2,1)}) %all-gather.8.cloned.1.call-update) | async-done | bytes 1179664 | tf_op jit(solution)/shard_map/all_gather | solution.py:74
  37.2 39.2 %all-gather.6.cloned.1.call-done = bf16[1024,768]{1,0:T(8,128)(2,1)} async-done(((bf16[256,768]{1,0:T(8,128)(2,1)}), bf16[1024,768]{1,0:T(8,128)(2,1)}) %all-gather.6.cloned.1.call-update) | async-done | bytes 1572880 | tf_op jit(solution)/shard_map/all_gather | solution.py:116
  76.3 2.4 fusion.27
  78.8 1.8 fusion.28
  82.9 3.9 collective-permute-start
  87.6 1.7 fusion.26
  89.4 1.7 pad_maximum_fusion
  91.8 17.5 %while.40 = (s32[]{:T(128)}, bf16[1024,192]{0,1:T(8,128)(2,1)}, f32[3,1024]{1,0:T(4,128)S(1)}, s32[]{:T(128)}, bf16[2,3072,192]{1,2,0:T(8,128)(2,1)S(1)}, /*inde...) while((s32[]{:T(128)}, bf16[1024,192]{0,1:T(8,128)(2,1)}, ...), condition=%wide.region_6.7_spmd.clone, body=%wide.region_2.6_spmd.clone.sunk | while | flops 630030336 | bytes 36239832 | solution.py:165
  91.8 1.3 fusion.124
  93.9 1.6 fusion.125
  95.5 2.1 exponential_reduce_fusion.2
  97.6 2.2 fusion.126
  100.6 1.3 fusion.124
  102.7 1.6 fusion.125
  104.2 2.1 exponential_reduce_fusion.2
  106.3 2.2 fusion.126
  109.3 3.0 convolution_convert_fusion.3
  112.5 1.7 pad_maximum_fusion.4
  114.3 47.0 %reduce-scatter.11.cloned.1.call-done = bf16[256,768]{1,0:T(8,128)(2,1)} async-done(((bf16[1024,768]{1,0:T(8,128)(2,1)}), bf16[256,768]{1,0:T(8,128)(2,1)}) %reduce-scatter.11.cloned.1.call-update) | async-done | bytes 393232 | tf_op jit(solution)/shard_map/reduce_scatter | solution.py:78
  164.4 1.4 reshape.289
  167.2 24.2 %all-gather.12.cloned.1.call-done = bf16[768,1536]{1,0:T(8,128)(2,1)} async-done(((bf16[96,1536]{1,0:T(8,128)(2,1)}), bf16[768,1536]{1,0:T(8,128)(2,1)}) %all-gather.12.cloned.1.call-update) | async-done | bytes 2359312 | tf_op jit(solution)/shard_map/all_gather | solution.py:177
  191.4 39.0 %all-gather.10.cloned.1.call-done = bf16[1024,768]{1,0:T(8,128)(2,1)} async-done(((bf16[256,768]{1,0:T(8,128)(2,1)}), bf16[1024,768]{1,0:T(8,128)(2,1)}) %all-gather.10.cloned.1.call-update) | async-done | bytes 1572880 | tf_op jit(solution)/shard_map/all_gather | solution.py:175
  230.4 4.6 multiply_convert_fusion.1
  235.1 3.2 convert_reduce_fusion
  239.4 2.6 convolution_convert_fusion.1
  242.3 4.3 convolution_convert_fusion.2
  246.6 29.9 %reduce-scatter.15.cloned.1.call-done = bf16[256,768]{1,0:T(8,128)(2,1)} async-done(((bf16[1024,768]{1,0:T(8,128)(2,1)}), bf16[256,768]{1,0:T(8,128)(2,1)}) %reduce-scatter.15.cloned.1.call-update) | async-done | bytes 393232 | tf_op jit(solution)/shard_map/reduce_scatter | solution.py:78
  276.5 2.3 fusion.48
  279.3 33.8 %reduce-scatter.13.cloned.1.call-done = bf16[256,768]{1,0:T(8,128)(2,1)} async-done(((bf16[1024,768]{1,0:T(8,128)(2,1)}), bf16[256,768]{1,0:T(8,128)(2,1)}) %reduce-scatter.13.cloned.1.call-update) | async-done | bytes 393232 | tf_op jit(solution)/shard_map/reduce_scatter | solution.py:78
  313.1 3.5 fusion.62
  318.4 3.5 convolution_convert_fusion.5
  321.9 1.5 convolution_convert_fusion.4
  323.4 1.6 pad_maximum_fusion.1
  324.9 4.4 copy.52
  329.4 24.9 %all-gather.14.cloned.1.call-done = bf16[1024,768]{1,0:T(8,128)(2,1)} async-done(((bf16[256,768]{1,0:T(8,128)(2,1)}), bf16[1024,768]{1,0:T(8,128)(2,1)}) %all-gather.14.cloned.1.call-update) | async-done | bytes 1572880 | tf_op jit(solution)/shard_map/all_gather | solution.py:207
  354.3 3.4 convert_multiply_fusion.4
  359.7 2.7 broadcast_in_dim.131
  362.4 32.3 %while.41 = (s32[]{:T(128)}, bf16[1024,192]{0,1:T(8,128)(2,1)}, f32[2,3072,192]{1,2,0:T(8,128)}, s32[]{:T(128)}, bf16[2,3072,192]{1,2,0:T(8,128)(2,1)S(1)}, /*in...) while((s32[]{:T(128)}, bf16[1024,192]{0,1:T(8,128)(2,1)}, ...), condition=%wide.region_17.18_spmd.clone, body=%wide.region_15.17_spmd.clone.sunk | while | flops 1537181184 | bytes 94420032 | solution.py:241
  362.4 1.3 fusion.138
  366.1 1.4 fusion.137
  367.6 2.1 fusion.139
  369.7 3.4 multiply_convert_fusion.3
  373.1 1.5 convolution_convert_fusion.13
  376.4 2.1 copy-done
  378.6 1.3 fusion.138
  382.3 1.4 fusion.137
  383.7 2.1 fusion.139
  385.8 3.4 multiply_convert_fusion.3
  389.3 1.5 convolution_convert_fusion.13
  392.6 2.1 copy-done
  394.7 2.2 fusion.65
  397.0 1.5 collective-permute-start.2
  401.5 4.0 collective-permute-done.3
  405.5 1.8 add_convert_fusion.1
  409.3 2.5 copy.50
  413.6 1.8 add_convert_fusion
  419.2 58.0 %reduce-scatter.19.cloned.1.call-done = bf16[96,768]{1,0:T(8,128)(2,1)} async-done(((bf16[768,768]{1,0:T(8,128)(2,1)}), bf16[96,768]{1,0:T(8,128)(2,1)}) %reduce-scatter.19.cloned.1.call-update) | async-done | bytes 147472
  481.3 33.7 %reduce-scatter.17.cloned.1.call-done = bf16[256,768]{1,0:T(8,128)(2,1)} async-done(((bf16[1024,768]{1,0:T(8,128)(2,1)}), bf16[256,768]{1,0:T(8,128)(2,1)}) %reduce-scatter.17.cloned.1.call-update) | async-done | bytes 393232 | tf_op jit(solution)/shard_map/reduce_scatter | solution.py:78
  515.1 1.4 fusion.49
  516.5 40.4 %all-reduce = (f32[768]{0:T(1024)}, f32[768]{0:T(1024)}, f32[768]{0:T(1024)}, f32[768]{0:T(1024)}, f32[768]{0:T(1024)}, /*index=5*/f32[768]{0:T(1024)}, f32[768]{0:T(1024)}, f32[3072]{0:T(1024)}, f32[768]{0:T(1024)}) all-reduce(f32[768]{0:T(1024)S(1)} %get-tuple-element.603, ...), channel_id=1, replica_groups=mesh['fsdp'=8,'tp'=4] {'fsdp','tp'}, use_global_device_ids=true, to_apply=%region_22.23 | all-reduce | flops 9216 | bytes 73728 | tf_op jit(solution)/shard_map/psum | solution.py:285
  557.0 2.2 fusion.42
  (195 shorter events, 42.4 us)
Async XLA Ops:
  7.2 4.5 copy-start.3
  7.2 29.9 %all-gather.8.cloned.1.call-start = ((), (), s32[]{:S(2)}) async-start(), calls=%async_computation.7 | async-start | bytes 1327104 | tf_op jit(solution)/shard_map/all_gather | solution.py:74
  9.0 67.4 %all-gather.6.cloned.1.call-start = ((), (), s32[]{:S(2)}) async-start(), calls=%async_computation.6 | async-start | bytes 1966080 | tf_op jit(solution)/shard_map/all_gather | solution.py:116
  10.3 26.9 %copy-start.24 = (f32[256]{0:T(256)}, f32[256]{0:T(256)S(1)}, u32[]{:S(2)}) copy-start(f32[256]{0:T(256)S(1)} %broadcast_multiply_fusion.8) | copy-start | bytes 3076
  11.7 25.5 %copy-start.26 = (f32[256]{0:T(256)}, f32[256]{0:T(256)S(1)}, u32[]{:S(2)}) copy-start(f32[256]{0:T(256)S(1)} %add_rsqrt_fusion.1) | copy-start | bytes 3076
  13.4 147.9 %reduce-scatter.11.cloned.1.call-start = ((), (), s32[]{:S(2)}) async-start(), calls=%async_computation.8 | async-start | bytes 1966080 | tf_op jit(solution)/shard_map/reduce_scatter | solution.py:78
  76.3 2.4 copy-start.1
  78.8 8.8 %copy-start.16 = (bf16[1,1024,192]{1,2,0:T(8,128)(2,1)}, bf16[1,1024,192]{1,2,0:T(8,128)(2,1)S(1)}, u32[]{:S(2)}) copy-start(bf16[1,1024,192]{1,2,0:T(8,128)(2,1)S(1)} %fusion.27) | copy-start | bytes 1179652
  80.6 8.7 %copy-start.18 = (bf16[1,1024,192]{1,2,0:T(8,128)(2,1)}, bf16[1,1024,192]{1,2,0:T(8,128)(2,1)S(1)}, u32[]{:S(2)}) copy-start(bf16[1,1024,192]{1,2,0:T(8,128)(2,1)S(1)} %fusion.28) | copy-start | bytes 1179652
  81.6 7.7 %collective-permute-start.1 = (bf16[2,1024,192]{1,2,0:T(8,128)(2,1)}, bf16[2,1024,192]{1,2,0:T(8,128)(2,1)}, u32[]{:S(2)}, u32[]{:S(2)}) collective-permute-start(bf16[2,1024,192]{1,2,0:T(8,128)(2,1)} %pad_maximum_fusion.3), channel_id=1, source_target_pairs={{4,0},{8,4},{12,8},{16,12},{20,16},{24,20},{28,24},{5,1},{9,5},{13... | collective-permute-start | bytes 2359304 | tf_op jit(solution)/shard_map/ppermute | solution.py:27
  82.9 6.4 %collective-permute-start = (bf16[2,1024,192]{1,2,0:T(8,128)(2,1)}, bf16[2,1024,192]{1,2,0:T(8,128)(2,1)}, u32[]{:S(2)}, u32[]{:S(2)}) collective-permute-start(bf16[2,1024,192]{1,2,0:T(8,128)(2,1)} %pad_maximum_fusion.3), channel_id=1, source_target_pairs={{0,4},{4,8},{8,12},{12,16},{16,20},{20,24},{24,28},{1,5},{5,9},{9,... | collective-permute-start | bytes 2359304 | tf_op jit(solution)/shard_map/ppermute | solution.py:26
  87.6 1.8 copy-start.17
  97.6 2.2 copy-start.9
  99.8 0.7 copy-start.10
  106.3 2.2 copy-start.9
  108.6 0.7 copy-start.10
  109.3 4.9 copy-start.19
  112.4 78.9 %all-gather.12.cloned.1.call-start = ((), (), s32[]{:S(2)}) async-start(), calls=%async_computation.10 | async-start | bytes 2654208 | tf_op jit(solution)/shard_map/all_gather | solution.py:177
  114.2 116.2 %all-gather.10.cloned.1.call-start = ((), (), s32[]{:S(2)}) async-start(), calls=%async_computation.9 | async-start | bytes 1966080 | tf_op jit(solution)/shard_map/all_gather | solution.py:175
  114.3 49.1 %copy-start.22 = (f32[768]{0:T(1024)S(1)}, f32[768]{0:T(1024)}, u32[]{:S(2)}) copy-start(f32[768]{0:T(1024)} %param.42) | copy-start | bytes 9220
  114.3 49.1 %copy-start.32 = (f32[768]{0:T(1024)S(1)}, f32[768]{0:T(1024)}, u32[]{:S(2)}) copy-start(f32[768]{0:T(1024)} %param.43) | copy-start | bytes 9220
  162.5 0.9 copy-start.4
  164.3 112.2 %reduce-scatter.15.cloned.1.call-start = ((), (), s32[]{:S(2)}) async-start(), calls=%async_computation.12 | async-start | bytes 1966080 | tf_op jit(solution)/shard_map/reduce_scatter | solution.py:78
  167.2 67.9 %copy-start.35 = (f32[768]{0:T(1024)S(1)}, f32[768]{0:T(1024)}, u32[]{:S(2)}) copy-start(f32[768]{0:T(1024)} %add.354) | copy-start | bytes 9220
  230.4 4.6 copy-start.20
  230.4 4.6 copy-start.36
  238.2 1.2 copy-start.38
  242.0 71.1 %reduce-scatter.13.cloned.1.call-start = ((), (), s32[]{:S(2)}) async-start(), calls=%async_computation.11 | async-start | bytes 1966080 | tf_op jit(solution)/shard_map/reduce_scatter | solution.py:78
  246.5 66.6 %copy-start.33 = (f32[768]{0:T(1024)S(1)}, f32[768]{0:T(1024)}, u32[]{:S(2)}) copy-start(f32[768]{0:T(1024)} %param.47) | copy-start | bytes 9220
  246.6 107.7 %all-gather.14.cloned.1.call-start = ((), (), s32[]{:S(2)}) async-start(), calls=%async_computation.13 | async-start | bytes 1966080 | tf_op jit(solution)/shard_map/all_gather | solution.py:207
  316.6 0.9 copy-start.6
  318.3 97.4 %reduce-scatter.21.cloned.1.call-start = ((), (), s32[]{:S(2)}) async-start(), calls=%async_computation.16 | async-start | bytes 2654208
  318.3 3.5 copy-start.21
  318.4 3.5 copy-start.37
  329.3 147.9 %reduce-scatter.19.cloned.1.call-start = ((), (), s32[]{:S(2)}) async-start(), calls=%async_computation.15 | async-start | bytes 1327104
  367.6 8.1 %slice-start = ((s8[4718592]{0:T(1024)(128)(4,1)}), s8[4194304]{0:T(1024)(128)(4,1)S(1)}, s32[]{:S(2)}) async-start(s8[4718592]{0:T(1024)(128)(4,1)} %bitcast.118), calls=%async_computation.17 | async-start | bytes 8388608 | tf_op jit(solution)/shard_map/while
  369.6 6.0 %slice-start.1 = ((s8[4718592]{0:T(1024)(128)(4,1)}), s8[524288]{0:T(1024)(128)(4,1)S(1)}, s32[]{:S(2)}) async-start(s8[4718592]{0:T(1024)(128)(4,1)} %bitcast.118), calls=%async_computation.18 | async-start | bytes 1048576 | tf_op jit(solution)/shard_map/while
  374.6 1.0 copy-start.12
  375.7 0.8 copy-start.13
  376.4 2.1 copy-start
  383.7 8.1 %slice-start = ((s8[4718592]{0:T(1024)(128)(4,1)}), s8[4194304]{0:T(1024)(128)(4,1)S(1)}, s32[]{:S(2)}) async-start(s8[4718592]{0:T(1024)(128)(4,1)} %bitcast.118), calls=%async_computation.17 | async-start | bytes 8388608 | tf_op jit(solution)/shard_map/while
  385.8 6.0 %slice-start.1 = ((s8[4718592]{0:T(1024)(128)(4,1)}), s8[524288]{0:T(1024)(128)(4,1)S(1)}, s32[]{:S(2)}) async-start(s8[4718592]{0:T(1024)(128)(4,1)} %bitcast.118), calls=%async_computation.18 | async-start | bytes 1048576 | tf_op jit(solution)/shard_map/while
  390.8 1.0 copy-start.12
  391.8 0.8 copy-start.13
  392.6 2.1 copy-start
  394.7 5.1 copy-start.8
  394.7 5.1 copy-start.11
  397.0 3.4 copy-start.2
  397.0 3.4 copy-start.14
  397.0 4.4 collective-permute-start.2
  398.5 6.9 %collective-permute-start.3 = (f32[2,1024,192]{1,2,0:T(8,128)S(1)}, f32[2,1024,192]{1,2,0:T(8,128)S(1)}, u32[]{:S(2)}, u32[]{:S(2)}) collective-permute-start(f32[2,1024,192]{1,2,0:T(8,128)S(1)} %get-tuple-element.669), channel_id=1, source_target_pairs={{4,0},{8,4},{12,8},{16,12},{20,16},{24,20},{28,24},{5,1},{9,5},{13... | collective-permute-start | bytes 4718600 | tf_op jit(solution)/shard_map/ppermute | solution.py:27
  409.3 2.8 copy-start.5
  409.3 2.8 copy-start.15
  411.9 103.2 %reduce-scatter.17.cloned.1.call-start = ((), (), s32[]{:S(2)}) async-start(), calls=%async_computation.14 | async-start | bytes 1966080 | tf_op jit(solution)/shard_map/reduce_scatter | solution.py:78
  413.6 1.8 copy-start.34
  416.9 98.1 %copy-start.23 = (f32[768]{0:T(1024)S(1)}, f32[768]{0:T(1024)}, u32[]{:S(2)}) copy-start(f32[768]{0:T(1024)} %param.33) | copy-start | bytes 9220
  416.9 98.1 %copy-start.25 = (f32[256]{0:T(256)S(1)}, f32[256]{0:T(256)}, u32[]{:S(2)}) copy-start(f32[256]{0:T(256)} %copy-done.24) | copy-start | bytes 3076
  417.0 98.1 %copy-start.27 = (f32[256]{0:T(256)S(1)}, f32[256]{0:T(256)}, u32[]{:S(2)}) copy-start(f32[256]{0:T(256)} %copy-done.26) | copy-start | bytes 3076
  417.8 98.6 %copy-start.28 = (f32[768]{0:T(1024)S(1)}, f32[768]{0:T(1024)}, u32[]{:S(2)}) copy-start(f32[768]{0:T(1024)} %get-tuple-element.601) | copy-start | bytes 9220
  417.8 98.7 %copy-start.29 = (f32[768]{0:T(1024)S(1)}, f32[768]{0:T(1024)}, u32[]{:S(2)}) copy-start(f32[768]{0:T(1024)} %get-tuple-element.607) | copy-start | bytes 9220
  417.8 98.7 %copy-start.30 = (f32[768]{0:T(1024)S(1)}, f32[768]{0:T(1024)}, u32[]{:S(2)}) copy-start(f32[768]{0:T(1024)} %get-tuple-element.654) | copy-start | bytes 9220
  417.9 98.7 %copy-start.31 = (f32[768]{0:T(1024)S(1)}, f32[768]{0:T(1024)}, u32[]{:S(2)}) copy-start(f32[768]{0:T(1024)} %get-tuple-element.670) | copy-start | bytes 9220
  417.9 139.1 %copy-start.7 = (f32[256,768]{1,0:T(8,128)S(1)}, f32[256,768]{1,0:T(8,128)}, u32[]{:S(2)}) copy-start(f32[256,768]{1,0:T(8,128)} %copy-done.6) | copy-start | bytes 2359300
Sparse Core Ops, SparseCore 0:
  10.5 26.6 all-gather.7
  39.3 37.0 all-gather.5
  112.5 48.6 reduce-scatter.10
  163.6 27.7 all-gather.11
  193.3 37.0 all-gather.9
  242.2 34.2 reduce-scatter.14
  278.8 34.2 reduce-scatter.12
  318.4 35.8 all-gather.13
  357.7 41.2 reduce-scatter.20
  412.0 65.2 reduce-scatter.18
  479.6 35.4 reduce-scatter.16

commit v2 on v1

--- a/solution.py
+++ b/solution.py
@@ -1,8 +1,11 @@
+import functools
 import math
 
 import jax
 import jax.numpy as jnp
 from jax import lax
+from jax.experimental import pallas as pl
+from jax.experimental.pallas import tpu as pltpu
 from jax.sharding import PartitionSpec as P
 
 HD = 64
@@ -69,15 +72,273 @@
     )
 
 
-def fetch_attention(query_weight, key_weight, value_weight, out_weight):
-    joined = jnp.concatenate([query_weight, key_weight, value_weight, out_weight], axis=1)
-    return jnp.split(lax.all_gather(joined, "fsdp", axis=0, tiled=True), 4, axis=1)
-
-
 def scatter_rows(partial_rows, axis):
     return lax.psum_scatter(
         partial_rows.astype(jnp.bfloat16), axis, scatter_dimension=0, tiled=True
     ).astype(jnp.float32)
+
+
+MESH = pl.DeviceIdType.MESH
+VMEM_LIMIT = 60 * 1024 * 1024
+
+
+def remote(source, target, send_sem, recv_sem, fsdp_to, tp_to):
+    return pltpu.make_async_remote_copy(
+        src_ref=source,
+        dst_ref=target,
+        send_sem=send_sem,
+        recv_sem=recv_sem,
+        device_id=(fsdp_to, tp_to),
+        device_id_type=MESH,
+    )
+
+
+def greet(fsdp_count, tp_count, f, t):
+    barrier = pltpu.get_barrier_semaphore()
+
+    def greet_fsdp(i, carry):
+        pl.semaphore_signal(
+            barrier, inc=1, device_id=(lax.rem(f + i, fsdp_count), t), device_id_type=MESH
+        )
+        return carry
+
+    def greet_tp(j, carry):
+        pl.semaphore_signal(
+            barrier, inc=1, device_id=(f, lax.rem(t + j, tp_count)), device_id_type=MESH
+        )
+        return carry
+
+    lax.fori_loop(1, fsdp_count, greet_fsdp, 0)
+    lax.fori_loop(1, tp_count, greet_tp, 0)
+    pl.semaphore_wait(barrier, fsdp_count + tp_count - 2)
+
+
+def halo_plan(f, fsdp_count):
+    phase = lax.rem(f, 3)
+    above = f + 1 < fsdp_count
+    below = f > 0
+    sends = (
+        (f + 1, 0, above & (phase == 0)),
+        (f + 1, 1, above & (phase < 2)),
+        (f - 1, 0, below & (phase > 0)),
+        (f - 1, 1, below & (phase == 2)),
+    )
+    receives = (
+        below & (phase == 1),
+        below & (phase > 0),
+        above & (phase < 2),
+        above & (phase == 1),
+    )
+    return (sends, receives)
+
+
+def project_kernel(
+    fsdp_count,
+    tp_count,
+    x_ref,
+    gain_ref,
+    shift_ref,
+    weight_ref,
+    bias_ref,
+    query_ref,
+    pair_ref,
+    normed_ref,
+    full_ref,
+    weight_send,
+    weight_recv,
+    row_send,
+    row_recv,
+    halo_send,
+    halo_recv,
+):
+    f = lax.axis_index("fsdp")
+    t = lax.axis_index("tp")
+    rows = x_ref.shape[0]
+    depth = weight_ref.shape[0]
+    group = rows * tp_count
+    width = query_ref.shape[1]
+    margin = (pair_ref.shape[0] - group) // 2
+    blank = jnp.zeros((256, 2 * width), jnp.bfloat16)
+
+    def clear(i, carry):
+        pair_ref[pl.ds(i * 256, 256), :] = blank
+        pair_ref[pl.ds(margin + group + i * 256, 256), :] = blank
+        return carry
+
+    lax.fori_loop(0, margin // 256, clear, 0)
+    greet(fsdp_count, tp_count, f, t)
+
+    def weight_copy(i):
+        return remote(
+            weight_ref,
+            full_ref.at[pl.ds(f * depth, depth)],
+            weight_send.at[i],
+            weight_recv.at[i],
+            lax.rem(f + i, fsdp_count),
+            t,
+        )
+
+    def weight_start(i, carry):
+        weight_copy(i).start()
+        return carry
+
+    def weight_done(i, carry):
+        weight_copy(i).wait_send()
+        source = lax.rem(f + fsdp_count - i, fsdp_count)
+        remote(
+            weight_ref,
+            full_ref.at[pl.ds(source * depth, depth)],
+            weight_send.at[i],
+            weight_recv.at[i],
+            source,
+            t,
+        ).wait_recv()
+        return carry
+
+    _, _, normed = normalize(x_ref[...], gain_ref[...], shift_ref[...])
+    normed_ref[t] = normed.astype(jnp.bfloat16)
+
+    def row_copy(source, lane, toward):
+        return remote(
+            normed_ref.at[source],
+            normed_ref.at[source],
+            row_send.at[lane],
+            row_recv.at[source],
+            f,
+            toward,
+        )
+
+    @pl.when(t > 0)
+    def _():
+        row_copy(t, tp_count, t - 1).start()
+
+    @pl.when(t < tp_count - 1)
+    def _():
+        row_copy(t, tp_count + 1, t + 1).start()
+
+    lax.fori_loop(1, fsdp_count, weight_start, 0)
+    full_ref[pl.ds(f * depth, depth), :] = weight_ref[...]
+    lax.fori_loop(1, fsdp_count, weight_done, 0)
+
+    def compute(source):
+        out = jnp.dot(normed_ref[source], full_ref[...], preferred_element_type=jnp.float32)
+        out = (out + bias_ref[t]).astype(jnp.bfloat16)
+        pair_ref[pl.ds(margin + source * rows, rows), :] = out[:, : 2 * width]
+        query_ref[pl.ds(source * rows, rows), :] = out[:, 2 * width :]
+
+    compute(t)
+
+    def arrival(k):
+        step = k // 2 + 1
+        side = 2 * lax.rem(k, 2) - 1
+        source = t + side * step
+        onward = t - side
+        valid = (source >= 0) & (source < tp_count)
+        return (source, onward, valid, valid & (onward >= 0) & (onward < tp_count))
+
+    def receive(k, carry):
+        source, onward, valid, forward = arrival(k)
+
+        @pl.when(valid)
+        def _():
+            row_copy(source, 0, t).wait_recv()
+
+            @pl.when(forward)
+            def _():
+                row_copy(source, source, onward).start()
+
+            compute(source)
+
+        return carry
+
+    lax.fori_loop(0, 2 * (tp_count - 1), receive, 0)
+
+    sends, receives = halo_plan(f, fsdp_count)
+    half = group // 2
+    for lane, (toward, part, needed) in enumerate(sends):
+        target = (margin + group if lane >= 2 else 0) + part * half
+
+        @pl.when(needed)
+        def _(lane=lane, toward=toward, part=part, target=target):
+            remote(
+                pair_ref.at[pl.ds(margin + part * half, half)],
+                pair_ref.at[pl.ds(target, half)],
+                halo_send.at[lane],
+                halo_recv.at[lane],
+                toward,
+                t,
+            ).start()
+
+    def sent(k, carry):
+        source, onward, valid, forward = arrival(k)
+
+        @pl.when(forward)
+        def _():
+            row_copy(source, source, onward).wait_send()
+
+        return carry
+
+    lax.fori_loop(0, 2 * (tp_count - 1), sent, 0)
+
+    @pl.when(t > 0)
+    def _():
+        row_copy(t, tp_count, t - 1).wait_send()
+
+    @pl.when(t < tp_count - 1)
+    def _():
+        row_copy(t, tp_count + 1, t + 1).wait_send()
+
+    for lane, (toward, part, needed) in enumerate(sends):
+        target = (margin + group if lane >= 2 else 0) + part * half
+        handle = remote(
+            pair_ref.at[pl.ds(margin + part * half, half)],
+            pair_ref.at[pl.ds(target, half)],
+            halo_send.at[lane],
+            halo_recv.at[lane],
+            toward,
+            t,
+        )
+
+        @pl.when(needed)
+        def _(handle=handle):
+            handle.wait_send()
+
+        @pl.when(receives[lane])
+        def _(handle=handle):
+            handle.wait_recv()
+
+
+def project(fsdp_count, tp_count, x, gain, shift, weights, bias, margin):
+    bf16 = jnp.bfloat16
+    rows, features = x.shape
+    width = weights.shape[1] // 3
+    group = rows * tp_count
+    depth = weights.shape[0]
+    whole = pl.BlockSpec(memory_space=pltpu.VMEM)
+    dma = pltpu.SemaphoreType.DMA
+    return pl.pallas_call(
+        functools.partial(project_kernel, fsdp_count, tp_count),
+        out_shape=(
+            jax.ShapeDtypeStruct((group, width), bf16),
+            jax.ShapeDtypeStruct((group + 2 * margin, 2 * width), bf16),
+            jax.ShapeDtypeStruct((tp_count, rows, features), bf16),
+            jax.ShapeDtypeStruct((depth * fsdp_count, 3 * width), bf16),
+        ),
+        in_specs=[whole] * 5,
+        out_specs=(whole,) * 4,
+        scratch_shapes=[
+            dma((fsdp_count,)),
+            dma((fsdp_count,)),
+            dma((tp_count + 2,)),
+            dma((tp_count,)),
+            dma((4,)),
+            dma((4,)),
+        ],
+        compiler_params=pltpu.CompilerParams(
+            collective_id=1, has_side_effects=True, vmem_limit_bytes=VMEM_LIMIT
+        ),
+        name="project",
+    )(x, gain, shift, weights, bias)
 
 
 def on_device(
@@ -112,24 +373,27 @@
     margin = CLIP - QB
     tp_slot = (jnp.arange(tp_count) == tp_index).astype(f32)
     own_cotangent = lax.dynamic_slice_in_dim(out_cotangent, tp_index * own_rows, own_rows, 0)
-    unit1, spread1, normed_own = normalize(inputs, norm1_gain, norm1_shift)
-    normed = lax.all_gather(normed_own.astype(bf16), "tp", axis=0, tiled=True)
-    query_w, key_w, value_w, out_w = fetch_attention(
-        query_weight, key_weight, value_weight, out_weight
-    )
-    local_width = query_w.shape[1]
+    unit1, spread1, _ = normalize(inputs, norm1_gain, norm1_shift)
+    local_width = query_weight.shape[1]
     heads_here = local_width // HD
-    column_start = tp_index * local_width
-    query = (
-        jnp.dot(normed, query_w, preferred_element_type=f32)
-        + lax.dynamic_slice_in_dim(query_bias, column_start, local_width, 0)
-    ).astype(bf16)
-    key = jnp.dot(normed, key_w, preferred_element_type=f32).astype(bf16)
-    value = (
-        jnp.dot(normed, value_w, preferred_element_type=f32)
-        + lax.dynamic_slice_in_dim(value_bias, column_start, local_width, 0)
-    ).astype(bf16)
-    padded = extended(jnp.stack([key, value]), (("fsdp", 1),), margin)
+    by_tp = lambda bias: bias.reshape(tp_count, 1, local_width)
+    attention_bias = jnp.concatenate(
+        [jnp.zeros((tp_count, 1, local_width), f32), by_tp(value_bias), by_tp(query_bias)], axis=2
+    )
+    query, pairs, normed, attention_w = project(
+        fsdp_count,
+        tp_count,
+        inputs,
+        norm1_gain.reshape(1, -1),
+        norm1_shift.reshape(1, -1),
+        jnp.concatenate([key_weight, value_weight, query_weight], axis=1),
+        attention_bias,
+        margin,
+    )
+    normed = normed.reshape(group_rows, -1)
+    key_w, value_w, query_w = jnp.split(attention_w, 3, axis=1)
+    padded = jnp.stack(jnp.split(pairs, 2, axis=1))
+    out_w = lax.all_gather(out_weight, "fsdp", axis=0, tiled=True)
     group_base = fsdp_index * group_rows
     clip_ids = jnp.arange(clip_lengths.shape[0])
     block_count = group_rows // QB

time: 567 us -> 521 us (0.919)
  waiting for transfers between devices: 357 us -> 262 us
  Pallas kernels: 0 us -> 42.9 us
  blocking collectives: 40.4 us -> 53.3 us
  local copies, waits for them, and re-layouts: 38 us -> 44 us
    all_gather x2 -> x0, waiting for transfers between devices: 62.2 us -> none  [the longest x1 39.2 us: on_device(): normed = lax.all_gather(normed_own.astype(bf16), 'tp', axis=0, tiled=True)]
    pallas_call x0 -> x1, Pallas kernels: none -> 42.9 us  [project(): pl.pallas_call(functools.partial(project_kernel, fsdp_count, tp_count), o...]
    all_gather x1, waiting for transfers between devices: 24.2 us -> 0.01 us  [on_device(): lax.all_gather(jnp.concatenate([fc1_weight, fc2_weight], axis=1), 'fsdp',...]
    all_gather x0 -> x1, blocking collectives: none -> 12.9 us  [on_device(): out_w = lax.all_gather(out_weight, 'fsdp', axis=0, tiled=True)]
    all_gather x1, waiting for transfers between devices: 39 us -> 32.8 us  [on_device(): normed2 = lax.all_gather(normed2_own, 'tp', axis=0, tiled=True)]
    dot_general x3 -> x0, matrix products: 5.96 us -> none  [the longest x1 2.43 us: on_device(): key = jnp.dot(normed, key_w, preferred_element_type=f32).astype(bf16)]
    unnamed x78 -> x76, local copies, waits for them, and re-layouts: 16.6 us -> 21.1 us
    unnamed x13 -> x11, waiting for transfers between devices: 58.2 us -> 56.2 us
  transfers between devices with their start and end apart: 15 -> 11, of which waited for: 12 -> 9; matrix products, arithmetic and copies ran while one was open for 16% -> 16% of each run, Pallas kernels for 0% -> 0%
where the time goes in v2:
time: 521 us; the launch traced here: 519 us
  waiting for transfers between devices  262 us (50%)
  matrix products  58.3 us (11%)
  blocking collectives  53.3 us (10%)
  local copies, waits for them, and re-layouts  44 us (8%)
  Pallas kernels  42.9 us (8%)
  other arithmetic  38.5 us (7%)
  between operations  15.8 us (3%)
    reduce_scatter x4, waiting for transfers between devices, scatter_rows(): lax.psum_scatter(partial_rows.astype(jnp.bfloat16), axis, scatter_dimensi...  144 us
    unnamed x11, waiting for transfers between devices  56.2 us
    pallas_call x1, Pallas kernels, project(): pl.pallas_call(functools.partial(project_kernel, fsdp_count, tp_count), o...  42.9 us
    psum x1, blocking collectives, on_device(): lax.psum((grad_gain1, grad_shift1, grad_qbias, grad_vbias, grad_obias, gr...  40.4 us
    all_gather x1, waiting for transfers between devices, on_device(): normed2 = lax.all_gather(normed2_own, 'tp', axis=0, tiled=True)  32.8 us
    all_gather x1, waiting for transfers between devices, on_device(): dh_all = lax.all_gather(dhidden.astype(bf16), 'tp', axis=0, tiled=True)  24.5 us
    unnamed x76, local copies, waits for them, and re-layouts  21.1 us
    dot_general x6, matrix products, contract_cols(): lax.dot_general(left_rows, right_rows, (((1,), (1,)), ((), ())), preferre...  15.1 us
  transfers between devices with their start and end apart: 11, of which 9 were waited for; matrix products, arithmetic and copies ran while one was open for 16% of the time, Pallas kernels for 0%

profile of v2, /device:TPU:0, one launch (start us, length us, event | category | flops | bytes accessed | tf_op | source)
XLA Modules:
  0.0 519.4 jit_solution(11019800345786118881)
XLA Ops:
  8.1 1.3 reshape.304.shift_ref
  9.3 1.3 reshape.303.gain_ref
  12.1 12.9 %all_gather.12 = bf16[768,192]{1,0:T(8,128)(2,1)} all-gather(bf16[96,192]{1,0:T(8,128)(2,1)} %param.40), channel_id=1, replica_groups=mesh['fsdp'=8,'tp'=4] {'fsdp'}, dimensions={0}, use_global_device_ids=true | all-gather | bytes 331776 | tf_op jit(solution)/shard_map/all_gather | solution.py:396
  25.7 1.6 pad_maximum_fusion.4.weight_ref
  27.3 42.9 %project.1 = (bf16[1024,192]{1,0:T(8,128)(2,1)}, bf16[3072,384]{1,0:T(8,128)(2,1)}, bf16[4,256,768]{2,1,0:T(8,128)(2,1)}, bf16[768,576]{1,0:T(8,128)(2,1)}) custom-call(f32[256,768]{1,0:T(8,128)} %x_ref.1, f32[1,768]{1,0:T(1,128)} %reshape.303.gain_ref, f32[1,768]{1,0:T(1,128)} %reshape.304.shift_ref, bf16[96,576]{1,0:T(8,128)(2,1)} %pad_maximum_fusion.4.weight_ref, ...), custom_call_target="tpu_custom_call" | custom-call | tf_op jit(solution)/shard_map/project/pallas_call | solution.py:319
  70.2 1.2 copy.47
  71.4 2.6 slice_bitcast_fusion.1
  74.1 2.3 pad_maximum_fusion
  76.4 3.1 copy.46
  79.6 14.8 %while.40 = (s32[]{:T(128)}, bf16[1024,192]{0,1:T(8,128)(2,1)S(1)}, f32[3,1024]{1,0:T(4,128)S(1)}, s32[]{:T(128)}, bf16[2,3072,192]{1,2,0:T(8,128)(2,1)S(1)}, /*...) while((s32[]{:T(128)}, bf16[1024,192]{0,1:T(8,128)(2,1)S(1)}, ...), condition=%wide.region_4.5_spmd.clone, body=%wide.region_0.4_spmd.clone.sunk | while | flops 630030336 | bytes 33094048 | solution.py:429
  81.0 1.6 fusion.121
  82.6 2.1 exponential_reduce_fusion.2
  84.7 2.2 fusion.122
  88.4 1.6 fusion.121
  90.0 2.1 exponential_reduce_fusion.2
  92.1 2.2 fusion.122
  95.7 3.0 convolution_convert_fusion.3
  98.8 1.7 pad_maximum_fusion.3
  102.0 46.5 %reduce-scatter.11.cloned.1.call-done = bf16[256,768]{1,0:T(8,128)(2,1)} async-done(((bf16[1024,768]{1,0:T(8,128)(2,1)}), bf16[256,768]{1,0:T(8,128)(2,1)}) %reduce-scatter.11.cloned.1.call-update) | async-done | bytes 393232 | tf_op jit(solution)/shard_map/reduce_scatter | solution.py:76
  148.4 2.1 fusion.61
  152.0 1.4 reshape.307
  154.8 32.8 %all-gather.4.cloned.1.call-done = bf16[1024,768]{1,0:T(8,128)(2,1)} async-done(((bf16[256,768]{1,0:T(8,128)(2,1)}), bf16[1024,768]{1,0:T(8,128)(2,1)}) %all-gather.4.cloned.1.call-update) | async-done | bytes 1572880 | tf_op jit(solution)/shard_map/all_gather | solution.py:439
  187.5 4.7 multiply_convert_fusion.1
  192.2 3.2 convert_reduce_fusion
  196.6 2.6 convolution_convert_fusion.1
  199.3 4.3 convolution_convert_fusion.2
  203.6 30.1 %reduce-scatter.15.cloned.1.call-done = bf16[256,768]{1,0:T(8,128)(2,1)} async-done(((bf16[1024,768]{1,0:T(8,128)(2,1)}), bf16[256,768]{1,0:T(8,128)(2,1)}) %reduce-scatter.15.cloned.1.call-update) | async-done | bytes 393232 | tf_op jit(solution)/shard_map/reduce_scatter | solution.py:76
  233.7 2.0 fusion.44
  236.3 34.0 %reduce-scatter.13.cloned.1.call-done = bf16[256,768]{1,0:T(8,128)(2,1)} async-done(((bf16[1024,768]{1,0:T(8,128)(2,1)}), bf16[256,768]{1,0:T(8,128)(2,1)}) %reduce-scatter.13.cloned.1.call-update) | async-done | bytes 393232 | tf_op jit(solution)/shard_map/reduce_scatter | solution.py:76
  270.3 3.2 fusion.59
  275.3 3.5 convolution_convert_fusion.5
  278.8 1.5 convolution_convert_fusion.4
  280.3 1.6 pad_maximum_fusion.1
  281.9 4.4 copy.60
  286.6 24.5 %all-gather.8.cloned.1.call-done = bf16[1024,768]{1,0:T(8,128)(2,1)} async-done(((bf16[256,768]{1,0:T(8,128)(2,1)}), bf16[1024,768]{1,0:T(8,128)(2,1)}) %all-gather.8.cloned.1.call-update) | async-done | bytes 1572880 | tf_op jit(solution)/shard_map/all_gather | solution.py:471
  311.1 3.1 convert_multiply_fusion.4
  314.2 1.2 reduce_sum.216
  315.4 2.7 broadcast_in_dim.131
  318.1 31.7 %while.41 = (s32[]{:T(128)}, bf16[1024,192]{0,1:T(8,128)(2,1)S(1)}, f32[2,3072,192]{1,2,0:T(8,128)}, s32[]{:T(128)}, bf16[2,3072,192]{1,2,0:T(8,128)(2,1)S(1)}, ...) while((s32[]{:T(128)}, bf16[1024,192]{0,1:T(8,128)(2,1)S(1)}, ...), condition=%wide.region_17.18_spmd.clone, body=%wide.region_15.17_spmd.clone.sunk | while | flops 1537181184 | bytes 91274240 | solution.py:505
  318.1 1.3 fusion.134
  321.9 1.4 fusion.133
  323.3 2.1 fusion.135
  325.4 3.4 multiply_convert_fusion.3
  328.8 1.5 convolution_convert_fusion.12
  331.9 2.1 copy-done
  334.0 1.3 fusion.134
  337.7 1.4 fusion.133
  339.2 2.1 fusion.135
  341.2 3.4 multiply_convert_fusion.3
  344.7 1.5 convolution_convert_fusion.12
  347.7 2.1 copy-done
  349.9 2.2 fusion.62
  352.1 1.5 collective-permute-start
  353.6 1.3 collective-permute-start.1
  356.6 4.0 collective-permute-done.1
  360.5 1.8 add_add_fusion
  363.4 1.5 copy.58
  365.2 1.6 fusion.53
  367.5 2.0 add_convert_fusion
  374.4 56.1 %reduce-scatter.19.cloned.1.call-done = bf16[96,768]{1,0:T(8,128)(2,1)} async-done(((bf16[768,768]{1,0:T(8,128)(2,1)}), bf16[96,768]{1,0:T(8,128)(2,1)}) %reduce-scatter.19.cloned.1.call-update) | async-done | bytes 147472
  434.5 33.7 %reduce-scatter.17.cloned.1.call-done = bf16[256,768]{1,0:T(8,128)(2,1)} async-done(((bf16[1024,768]{1,0:T(8,128)(2,1)}), bf16[256,768]{1,0:T(8,128)(2,1)}) %reduce-scatter.17.cloned.1.call-update) | async-done | bytes 393232 | tf_op jit(solution)/shard_map/reduce_scatter | solution.py:76
  468.2 1.4 fusion.45
  469.7 40.4 %all-reduce = (f32[768]{0:T(1024)}, f32[768]{0:T(1024)}, f32[768]{0:T(1024)}, f32[768]{0:T(1024)}, f32[768]{0:T(1024)}, /*index=5*/f32[768]{0:T(1024)}, f32[768]{0:T(1024)}, f32[3072]{0:T(1024)}, f32[768]{0:T(1024)}) all-reduce(f32[768]{0:T(1024)S(1)} %get-tuple-element.645, ...), channel_id=1, replica_groups=mesh['fsdp'=8,'tp'=4] {'fsdp','tp'}, use_global_device_ids=true, to_apply=%region_22.23 | all-reduce | flops 9216 | bytes 73728 | tf_op jit(solution)/shard_map/psum | solution.py:549
  510.1 2.2 fusion.38
  (169 shorter events, 35.1 us)
Async XLA Ops:
  8.0 140.4 %reduce-scatter.11.cloned.1.call-start = ((), (), s32[]{:S(2)}) async-start(), calls=%async_computation.6 | async-start | bytes 1966080 | tf_op jit(solution)/shard_map/reduce_scatter | solution.py:76
  76.4 3.2 copy-start.30
  94.3 0.8 copy-start.7
  95.1 0.6 copy-start.11
  95.7 4.9 copy-start.1
  95.7 52.7 %copy-start.22 = (f32[768]{0:T(1024)S(1)}, f32[768]{0:T(1024)}, u32[]{:S(2)}) copy-start(f32[768]{0:T(1024)} %param.41) | copy-start | bytes 9220
  98.7 52.0 %copy-start.14 = (f32[768]{0:T(1024)S(1)}, f32[768]{0:T(1024)}, u32[]{:S(2)}) copy-start(f32[768]{0:T(1024)} %param.42) | copy-start | bytes 9220
  98.8 52.0 %copy-start.23 = (f32[768]{0:T(1024)S(1)}, f32[768]{0:T(1024)}, u32[]{:S(2)}) copy-start(f32[768]{0:T(1024)} %param.43) | copy-start | bytes 9220
  98.8 56.0 %all-gather.6.cloned.1.call-start = ((), (), s32[]{:S(2)}) async-start(), calls=%async_computation.8 | async-start | bytes 2654208 | tf_op jit(solution)/shard_map/all_gather | solution.py:441
  100.6 87.0 %all-gather.4.cloned.1.call-start = ((), (), s32[]{:S(2)}) async-start(), calls=%async_computation.7 | async-start | bytes 1966080 | tf_op jit(solution)/shard_map/all_gather | solution.py:439
  102.0 48.5 %copy-start.16 = (f32[256]{0:T(256)}, f32[256]{0:T(256)S(1)}, u32[]{:S(2)}) copy-start(f32[256]{0:T(256)S(1)} %broadcast_multiply_fusion.5) | copy-start | bytes 3076
  151.7 82.0 %reduce-scatter.15.cloned.1.call-start = ((), (), s32[]{:S(2)}) async-start(), calls=%async_computation.10 | async-start | bytes 1966080 | tf_op jit(solution)/shard_map/reduce_scatter | solution.py:76
  154.8 37.4 %copy-start.27 = (f32[768]{0:T(1024)S(1)}, f32[768]{0:T(1024)}, u32[]{:S(2)}) copy-start(f32[768]{0:T(1024)} %add.318) | copy-start | bytes 9220
  187.5 4.7 copy-start.12
  187.5 4.7 copy-start.29
  195.4 1.2 copy-start.32
  199.2 71.1 %reduce-scatter.13.cloned.1.call-start = ((), (), s32[]{:S(2)}) async-start(), calls=%async_computation.9 | async-start | bytes 1966080 | tf_op jit(solution)/shard_map/reduce_scatter | solution.py:76
  203.5 66.8 %copy-start.24 = (f32[768]{0:T(1024)S(1)}, f32[768]{0:T(1024)}, u32[]{:S(2)}) copy-start(f32[768]{0:T(1024)} %param.47) | copy-start | bytes 9220
  203.6 107.5 %all-gather.8.cloned.1.call-start = ((), (), s32[]{:S(2)}) async-start(), calls=%async_computation.11 | async-start | bytes 1966080 | tf_op jit(solution)/shard_map/all_gather | solution.py:471
  273.6 0.9 copy-start.4
  275.2 94.9 %reduce-scatter.21.cloned.1.call-start = ((), (), s32[]{:S(2)}) async-start(), calls=%async_computation.14 | async-start | bytes 2654208
  275.3 3.5 copy-start.13
  275.3 3.5 copy-start.31
  286.3 24.8 %copy-start.8 = (bf16[1024,192]{0,1:T(8,128)(2,1)S(1)}, bf16[1024,192]{0,1:T(8,128)(2,1)}, u32[]{:S(2)}) copy-start(bf16[1024,192]{0,1:T(8,128)(2,1)} %copy-done.7) | copy-start | bytes 1179652
  286.3 24.8 %copy-start.9 = (bf16[768,192]{1,0:T(8,128)(2,1)S(1)}, bf16[768,192]{1,0:T(8,128)(2,1)}, u32[]{:S(2)}) copy-start(bf16[768,192]{1,0:T(8,128)(2,1)} %all_gather.12) | copy-start | bytes 884740
  286.3 144.2 %reduce-scatter.19.cloned.1.call-start = ((), (), s32[]{:S(2)}) async-start(), calls=%async_computation.13 | async-start | bytes 1327104
  323.3 8.0 %slice-start = ((s8[4718592]{0:T(1024)(128)(4,1)}), s8[4194304]{0:T(1024)(128)(4,1)S(1)}, s32[]{:S(2)}) async-start(s8[4718592]{0:T(1024)(128)(4,1)} %bitcast.118), calls=%async_computation.15 | async-start | bytes 8388608 | tf_op jit(solution)/shard_map/while
  325.4 6.0 %slice-start.1 = ((s8[4718592]{0:T(1024)(128)(4,1)}), s8[524288]{0:T(1024)(128)(4,1)S(1)}, s32[]{:S(2)}) async-start(s8[4718592]{0:T(1024)(128)(4,1)} %bitcast.118), calls=%async_computation.16 | async-start | bytes 1048576 | tf_op jit(solution)/shard_map/while
  331.9 2.1 copy-start
  339.1 8.0 %slice-start = ((s8[4718592]{0:T(1024)(128)(4,1)}), s8[4194304]{0:T(1024)(128)(4,1)S(1)}, s32[]{:S(2)}) async-start(s8[4718592]{0:T(1024)(128)(4,1)} %bitcast.118), calls=%async_computation.15 | async-start | bytes 8388608 | tf_op jit(solution)/shard_map/while
  341.2 6.0 %slice-start.1 = ((s8[4718592]{0:T(1024)(128)(4,1)}), s8[524288]{0:T(1024)(128)(4,1)S(1)}, s32[]{:S(2)}) async-start(s8[4718592]{0:T(1024)(128)(4,1)} %bitcast.118), calls=%async_computation.16 | async-start | bytes 1048576 | tf_op jit(solution)/shard_map/while
  347.7 2.1 copy-start
  349.9 5.1 copy-start.3
  352.1 3.3 copy-start.6
  352.1 4.4 collective-permute-start
  353.6 6.9 %collective-permute-start.1 = (f32[2,1024,192]{1,2,0:T(8,128)S(1)}, f32[2,1024,192]{1,2,0:T(8,128)S(1)}, u32[]{:S(2)}, u32[]{:S(2)}) collective-permute-start(f32[2,1024,192]{1,2,0:T(8,128)S(1)} %get-tuple-element.711), channel_id=1, source_target_pairs={{4,0},{8,4},{12,8},{16,12},{20,16},{24,20},{28,24},{5,1},{9,5},{13... | collective-permute-start | bytes 4718600 | tf_op jit(solution)/shard_map/ppermute | solution.py:30
  364.8 2.0 copy-start.10
  364.9 103.4 %reduce-scatter.17.cloned.1.call-start = ((), (), s32[]{:S(2)}) async-start(), calls=%async_computation.12 | async-start | bytes 1966080 | tf_op jit(solution)/shard_map/reduce_scatter | solution.py:76
  367.4 2.1 copy-start.25
  367.5 2.1 copy-start.26
  369.5 0.5 copy-start.28
  371.4 96.8 %copy-start.2 = (f32[256,768]{1,0:T(8,128)S(1)}, f32[256,768]{1,0:T(8,128)}, u32[]{:S(2)}) copy-start(f32[256,768]{1,0:T(8,128)} %x_ref.1) | copy-start | bytes 2359300
  371.4 96.8 %copy-start.15 = (f32[768]{0:T(1024)S(1)}, f32[768]{0:T(1024)}, u32[]{:S(2)}) copy-start(f32[768]{0:T(1024)} %param.33) | copy-start | bytes 9220
  371.4 96.8 %copy-start.17 = (f32[256]{0:T(256)S(1)}, f32[256]{0:T(256)}, u32[]{:S(2)}) copy-start(f32[256]{0:T(256)} %copy-done.16) | copy-start | bytes 3076
  372.3 97.3 %copy-start.18 = (f32[768]{0:T(1024)S(1)}, f32[768]{0:T(1024)}, u32[]{:S(2)}) copy-start(f32[768]{0:T(1024)} %get-tuple-element.643) | copy-start | bytes 9220
  372.3 97.4 %copy-start.19 = (f32[768]{0:T(1024)S(1)}, f32[768]{0:T(1024)}, u32[]{:S(2)}) copy-start(f32[768]{0:T(1024)} %get-tuple-element.649) | copy-start | bytes 9220
  372.3 97.4 %copy-start.20 = (f32[768]{0:T(1024)S(1)}, f32[768]{0:T(1024)}, u32[]{:S(2)}) copy-start(f32[768]{0:T(1024)} %get-tuple-element.696) | copy-start | bytes 9220
  372.3 97.4 %copy-start.21 = (f32[768]{0:T(1024)S(1)}, f32[768]{0:T(1024)}, u32[]{:S(2)}) copy-start(f32[768]{0:T(1024)} %get-tuple-element.712) | copy-start | bytes 9220
  372.3 137.8 %copy-start.5 = (f32[256,768]{1,0:T(8,128)S(1)}, f32[256,768]{1,0:T(8,128)}, u32[]{:S(2)}) copy-start(f32[256,768]{1,0:T(8,128)} %copy-done.4) | copy-start | bytes 2359300
Sparse Core Ops, SparseCore 0:
  98.9 49.5 reduce-scatter.10
  199.3 34.3 reduce-scatter.14
  236.0 34.2 reduce-scatter.12
Sparse Core Ops, SparseCore 1:
  101.7 42.8 all-gather.5
  151.8 35.7 all-gather.3
  275.3 35.7 all-gather.7
  314.4 41.2 reduce-scatter.20
  364.9 65.5 reduce-scatter.18
  432.8 35.4 reduce-scatter.16

commit v3 on v2

--- a/solution.py
+++ b/solution.py
@@ -80,6 +80,7 @@
 
 MESH = pl.DeviceIdType.MESH
 VMEM_LIMIT = 60 * 1024 * 1024
+LANES = 128
 
 
 def remote(source, target, send_sem, recv_sem, fsdp_to, tp_to):
@@ -113,23 +114,74 @@
     pl.semaphore_wait(barrier, fsdp_count + tp_count - 2)
 
 
-def halo_plan(f, fsdp_count):
-    phase = lax.rem(f, 3)
-    above = f + 1 < fsdp_count
-    below = f > 0
-    sends = (
-        (f + 1, 0, above & (phase == 0)),
-        (f + 1, 1, above & (phase < 2)),
-        (f - 1, 0, below & (phase > 0)),
-        (f - 1, 1, below & (phase == 2)),
-    )
-    receives = (
-        below & (phase == 1),
-        below & (phase > 0),
-        above & (phase < 2),
-        above & (phase == 1),
-    )
-    return (sends, receives)
+def gather_copies(f, t, fsdp_count, sources, targets, depth, sends, recvs):
+    partner = f + 1 - 2 * lax.rem(f, 2)
+
+    def piece(target, owner):
+        return target.at[:, pl.ds(owner * depth, depth)]
+
+    def copies(owner, toward, lane, first):
+        return [
+            remote(
+                source if first else piece(target, owner),
+                piece(target, owner),
+                send.at[lane],
+                recv.at[owner],
+                toward,
+                t,
+            )
+            for source, target, send, recv in zip(sources, targets, sends, recvs)
+        ]
+
+    def start():
+        def body(i, carry):
+            for handle in copies(f, lax.rem(f + 2 * i, fsdp_count), i, True):
+                handle.start()
+            return carry
+
+        lax.fori_loop(1, fsdp_count // 2, body, 0)
+        for handle in copies(f, partner, 0, True):
+            handle.start()
+        for source, target in zip(sources, targets):
+            target[:, pl.ds(f * depth, depth), :] = source[...]
+
+    def relay():
+        def body(i, carry):
+            owner = lax.rem(f + fsdp_count - 2 * i, fsdp_count)
+            for handle in copies(owner, partner, fsdp_count // 2 + i, False):
+                handle.wait_recv()
+                handle.start()
+            return carry
+
+        lax.fori_loop(1, fsdp_count // 2, body, 0)
+
+    def finish():
+        def body(i, carry):
+            owner = lax.rem(partner + 2 * i, fsdp_count)
+            for handle in copies(owner, partner, 0, False):
+                handle.wait_recv()
+            return carry
+
+        lax.fori_loop(0, fsdp_count // 2, body, 0)
+
+    def drain():
+        def body(i, carry):
+            for handle in copies(f, lax.rem(f + 2 * i, fsdp_count), i, True):
+                handle.wait_send()
+            for handle in copies(
+                lax.rem(f + fsdp_count - 2 * i, fsdp_count),
+                partner,
+                fsdp_count // 2 + i,
+                False,
+            ):
+                handle.wait_send()
+            return carry
+
+        lax.fori_loop(1, fsdp_count // 2, body, 0)
+        for handle in copies(f, partner, 0, True):
+            handle.wait_send()
+
+    return (start, relay, finish, drain)
 
 
 def project_kernel(
@@ -140,12 +192,20 @@
     shift_ref,
     weight_ref,
     bias_ref,
+    mlp_ref,
+    out_ref,
     query_ref,
     pair_ref,
     normed_ref,
     full_ref,
+    mlp_full,
+    heads_ref,
+    side_send,
+    side_recv,
     weight_send,
     weight_recv,
+    mlp_send,
+    mlp_recv,
     row_send,
     row_recv,
     halo_send,
@@ -154,11 +214,15 @@
     f = lax.axis_index("fsdp")
     t = lax.axis_index("tp")
     rows = x_ref.shape[0]
-    depth = weight_ref.shape[0]
+    depth = weight_ref.shape[1]
     group = rows * tp_count
-    width = query_ref.shape[1]
+    pair_width = pair_ref.shape[1]
     margin = (pair_ref.shape[0] - group) // 2
-    blank = jnp.zeros((256, 2 * width), jnp.bfloat16)
+    per_half = tp_count // 2
+    phase = lax.rem(f, 3)
+    above = f + 1 < fsdp_count
+    below = f > 0
+    blank = jnp.zeros((256, pair_width), jnp.bfloat16)
 
     def clear(i, carry):
         pair_ref[pl.ds(i * 256, 256), :] = blank
@@ -167,34 +231,13 @@
 
     lax.fori_loop(0, margin // 256, clear, 0)
     greet(fsdp_count, tp_count, f, t)
-
-    def weight_copy(i):
-        return remote(
-            weight_ref,
-            full_ref.at[pl.ds(f * depth, depth)],
-            weight_send.at[i],
-            weight_recv.at[i],
-            lax.rem(f + i, fsdp_count),
-            t,
-        )
-
-    def weight_start(i, carry):
-        weight_copy(i).start()
-        return carry
-
-    def weight_done(i, carry):
-        weight_copy(i).wait_send()
-        source = lax.rem(f + fsdp_count - i, fsdp_count)
-        remote(
-            weight_ref,
-            full_ref.at[pl.ds(source * depth, depth)],
-            weight_send.at[i],
-            weight_recv.at[i],
-            source,
-            t,
-        ).wait_recv()
-        return carry
-
+    start_weights, relay_weights, finish_weights, drain_weights = gather_copies(
+        f, t, fsdp_count, (weight_ref,), (full_ref,), depth, (weight_send,), (weight_recv,)
+    )
+    start_mlp, relay_mlp, finish_mlp, drain_mlp = gather_copies(
+        f, t, fsdp_count, (mlp_ref,), (mlp_full,), depth, (mlp_send,), (mlp_recv,)
+    )
+    start_weights()
     _, _, normed = normalize(x_ref[...], gain_ref[...], shift_ref[...])
     normed_ref[t] = normed.astype(jnp.bfloat16)
 
@@ -216,15 +259,69 @@
     def _():
         row_copy(t, tp_count + 1, t + 1).start()
 
-    lax.fori_loop(1, fsdp_count, weight_start, 0)
-    full_ref[pl.ds(f * depth, depth), :] = weight_ref[...]
-    lax.fori_loop(1, fsdp_count, weight_done, 0)
+    def heads_copy(j):
+        return remote(
+            out_ref,
+            heads_ref.at[t],
+            side_send.at[j],
+            side_recv.at[j],
+            f,
+            lax.rem(t + j, tp_count),
+        )
+
+    def heads_start(j, carry):
+        heads_copy(j).start()
+        return carry
+
+    def heads_done(j, carry):
+        heads_copy(j).wait_send()
+        source = lax.rem(t + tp_count - j, tp_count)
+        remote(
+            out_ref, heads_ref.at[source], side_send.at[j], side_recv.at[j], f, source
+        ).wait_recv()
+        return carry
+
+    heads_ref[t] = out_ref[...]
+    lax.fori_loop(1, tp_count, heads_start, 0)
+    relay_weights()
+    start_mlp()
+    finish_weights()
+
+    def halo_copy(source, side):
+        return remote(
+            pair_ref.at[pl.ds(margin + source * rows, rows)],
+            pair_ref.at[pl.ds((0 if side == 0 else margin + group) + source * rows, rows)],
+            halo_send.at[side, source],
+            halo_recv.at[side, source],
+            f + 1 if side == 0 else f - 1,
+            t,
+        )
+
+    def halo_sends(source):
+        late = source >= per_half
+        return (
+            above & ((phase == 0) | ((phase == 1) & late)),
+            below & ((phase == 2) | ((phase == 1) & jnp.logical_not(late))),
+        )
+
+    def halo_receives(source):
+        late = source >= per_half
+        return (
+            below & ((phase == 1) | ((phase == 2) & late)),
+            above & ((phase == 1) | ((phase == 0) & jnp.logical_not(late))),
+        )
 
     def compute(source):
-        out = jnp.dot(normed_ref[source], full_ref[...], preferred_element_type=jnp.float32)
+        out = jnp.dot(normed_ref[source], full_ref[0], preferred_element_type=jnp.float32)
         out = (out + bias_ref[t]).astype(jnp.bfloat16)
-        pair_ref[pl.ds(margin + source * rows, rows), :] = out[:, : 2 * width]
-        query_ref[pl.ds(source * rows, rows), :] = out[:, 2 * width :]
+        pair_ref[pl.ds(margin + source * rows, rows), :] = out[:, :pair_width]
+        for side, needed in enumerate(halo_sends(source)):
+
+            @pl.when(needed)
+            def _(side=side):
+                halo_copy(source, side).start()
+
+        query_ref[pl.ds(source * rows, rows), :] = out[:, pair_width:]
 
     compute(t)
 
@@ -252,22 +349,8 @@
         return carry
 
     lax.fori_loop(0, 2 * (tp_count - 1), receive, 0)
-
-    sends, receives = halo_plan(f, fsdp_count)
-    half = group // 2
-    for lane, (toward, part, needed) in enumerate(sends):
-        target = (margin + group if lane >= 2 else 0) + part * half
-
-        @pl.when(needed)
-        def _(lane=lane, toward=toward, part=part, target=target):
-            remote(
-                pair_ref.at[pl.ds(margin + part * half, half)],
-                pair_ref.at[pl.ds(target, half)],
-                halo_send.at[lane],
-                halo_recv.at[lane],
-                toward,
-                t,
-            ).start()
+    relay_mlp()
+    lax.fori_loop(1, tp_count, heads_done, 0)
 
     def sent(k, carry):
         source, onward, valid, forward = arrival(k)
@@ -288,57 +371,496 @@
     def _():
         row_copy(t, tp_count + 1, t + 1).wait_send()
 
-    for lane, (toward, part, needed) in enumerate(sends):
-        target = (margin + group if lane >= 2 else 0) + part * half
-        handle = remote(
-            pair_ref.at[pl.ds(margin + part * half, half)],
-            pair_ref.at[pl.ds(target, half)],
-            halo_send.at[lane],
-            halo_recv.at[lane],
-            toward,
-            t,
-        )
-
-        @pl.when(needed)
-        def _(handle=handle):
-            handle.wait_send()
-
-        @pl.when(receives[lane])
-        def _(handle=handle):
-            handle.wait_recv()
-
-
-def project(fsdp_count, tp_count, x, gain, shift, weights, bias, margin):
+    def halo_done(source, carry):
+        for side, (sends, receives) in enumerate(zip(halo_sends(source), halo_receives(source))):
+
+            @pl.when(sends)
+            def _(side=side):
+                halo_copy(source, side).wait_send()
+
+            @pl.when(receives)
+            def _(side=side):
+                halo_copy(source, side).wait_recv()
+
+        return carry
+
+    lax.fori_loop(0, tp_count, halo_done, 0)
+    drain_weights()
+    finish_mlp()
+    drain_mlp()
+
+
+def whole_specs(count):
+    return [pl.BlockSpec(memory_space=pltpu.VMEM)] * count
+
+
+def project(fsdp_count, tp_count, x, gain, shift, weights, bias, mlp, out_weight, pair_width, margin):
     bf16 = jnp.bfloat16
     rows, features = x.shape
-    width = weights.shape[1] // 3
     group = rows * tp_count
-    depth = weights.shape[0]
-    whole = pl.BlockSpec(memory_space=pltpu.VMEM)
+    depth = weights.shape[1]
     dma = pltpu.SemaphoreType.DMA
     return pl.pallas_call(
         functools.partial(project_kernel, fsdp_count, tp_count),
         out_shape=(
-            jax.ShapeDtypeStruct((group, width), bf16),
-            jax.ShapeDtypeStruct((group + 2 * margin, 2 * width), bf16),
+            jax.ShapeDtypeStruct((group, weights.shape[2] - pair_width), bf16),
+            jax.ShapeDtypeStruct((group + 2 * margin, pair_width), bf16),
             jax.ShapeDtypeStruct((tp_count, rows, features), bf16),
-            jax.ShapeDtypeStruct((depth * fsdp_count, 3 * width), bf16),
+            jax.ShapeDtypeStruct((1, depth * fsdp_count, weights.shape[2]), bf16),
+            jax.ShapeDtypeStruct((2, depth * fsdp_count, features), bf16),
+            jax.ShapeDtypeStruct((tp_count, *out_weight.shape), bf16),
         ),
-        in_specs=[whole] * 5,
-        out_specs=(whole,) * 4,
+        in_specs=whole_specs(7),
+        out_specs=tuple(whole_specs(6)),
         scratch_shapes=[
+            dma((tp_count,)),
+            dma((tp_count,)),
+            dma((fsdp_count,)),
+            dma((fsdp_count,)),
             dma((fsdp_count,)),
             dma((fsdp_count,)),
             dma((tp_count + 2,)),
             dma((tp_count,)),
-            dma((4,)),
-            dma((4,)),
+            dma((2, tp_count)),
+            dma((2, tp_count)),
         ],
         compiler_params=pltpu.CompilerParams(
             collective_id=1, has_side_effects=True, vmem_limit_bytes=VMEM_LIMIT
         ),
         name="project",
-    )(x, gain, shift, weights, bias)
+    )(x, gain, shift, weights, bias, mlp, out_weight)
+
+
+def block_clip(f, part, margin):
+    phase = lax.rem(f, 3)
+    start = jnp.where(
+        phase == 0,
+        margin,
+        jnp.where(phase == 2, margin - QB, jnp.where(part == 0, 0, margin + QB)),
+    )
+    return (pl.multiple_of(start, QB), (2 * f + part) // 3)
+
+
+def head_tiles(pair, length):
+    lane = lax.broadcasted_iota(jnp.int32, pair.shape, 1)
+    row = lax.broadcasted_iota(jnp.int32, pair.shape, 0)
+    extra = jnp.where(
+        lane == HD,
+        jnp.where(row < length, 0.0, far_negative),
+        jnp.where(lane <= HD + 3, 1.0, 0.0),
+    )
+    return jnp.where(lane < HD, pair, extra)
+
+
+def spread_heads(rows, head):
+    tile = rows[:, (head // 2) * LANES : (head // 2 + 1) * LANES]
+    return pltpu.roll(tile, HD, axis=1) if head % 2 else tile
+
+
+def three_parts(column):
+    high = column.astype(jnp.bfloat16).astype(jnp.float32)
+    rest = column - high
+    middle = rest.astype(jnp.bfloat16).astype(jnp.float32)
+    return (high, middle, rest - middle)
+
+
+def attend_kernel(
+    fsdp_count,
+    tp_count,
+    lengths_ref,
+    query_ref,
+    pair_ref,
+    mlp_ref,
+    out_ref,
+    spread_ref,
+    context_ref,
+    wide_ref,
+    mlp_full,
+    out_full,
+    mate_ref,
+    key_tiles,
+    value_tiles,
+    mate_send,
+    mate_recv,
+    context_send,
+    context_recv,
+    mlp_send,
+    mlp_recv,
+    out_send,
+    out_recv,
+):
+    f = lax.axis_index("fsdp")
+    t = lax.axis_index("tp")
+    bf16 = jnp.bfloat16
+    f32 = jnp.float32
+    rows = spread_ref.shape[1]
+    heads = wide_ref.shape[0]
+    group = rows * tp_count
+    margin = (pair_ref.shape[0] - group) // 2
+    greet(fsdp_count, tp_count, f, t)
+    depth = mlp_ref.shape[1]
+    start_out, relay_out, finish_out, drain_out = gather_copies(
+        f, t, fsdp_count, (out_ref,), (out_full,), depth, (out_send,), (out_recv,)
+    )
+    start_mlp, relay_mlp, finish_mlp, drain_mlp = gather_copies(
+        f, t, fsdp_count, (mate_ref,), (mlp_full,), depth, (mlp_send,), (mlp_recv,)
+    )
+    mate_copy = remote(
+        mlp_ref, mate_ref, mate_send, mate_recv, f, lax.rem(t + tp_count // 2, tp_count)
+    )
+    mate_copy.start()
+    start_out()
+    per_half = tp_count // 2
+
+    def context_copy(toward):
+        return remote(
+            context_ref.at[pl.ds(toward * rows, rows)],
+            spread_ref.at[t],
+            context_send.at[toward],
+            context_recv.at[t],
+            f,
+            toward,
+        )
+
+    lane = lax.broadcasted_iota(jnp.int32, (rows, LANES), 1)
+    row = lax.broadcasted_iota(jnp.int32, (LANES, rows), 0)
+    tall = lax.broadcasted_iota(jnp.int32, (LANES, CLIP), 0)
+
+    def half(step, carry):
+        part = lax.rem(t // per_half + 1 + step, 2)
+        first, clip = block_clip(f, part, margin)
+        length = lengths_ref[clip]
+        for head in range(heads):
+            pair = pair_ref[pl.ds(first, CLIP), head * LANES : (head + 1) * LANES].astype(f32)
+            key_tiles[head] = head_tiles(pair, length).astype(bf16)
+            value_tiles[head] = jnp.where(tall < HD, 1.0, pair.T).astype(bf16)
+
+        def block(i, inner):
+            within = lax.rem(lax.rem(t, per_half) + 1 + i, per_half)
+            index = part * per_half + within
+            here = pl.ds(pl.multiple_of(index * rows, rows), rows)
+            query = query_ref[here, :].astype(f32) * (1.0 / math.sqrt(HD))
+            parts = []
+            for head in range(heads):
+                wide = jnp.where(
+                    lane < HD, spread_heads(query, head), jnp.where(lane == HD, 1.0, 0.0)
+                )
+                scores = lax.dot_general(
+                    key_tiles[head],
+                    wide.astype(bf16),
+                    (((1,), (1,)), ((), ())),
+                    preferred_element_type=f32,
+                )
+                highest = jnp.max(scores, axis=0, keepdims=True)
+                weights = jnp.exp(scores - highest).astype(bf16)
+                summed = jnp.dot(value_tiles[head], weights, preferred_element_type=f32)
+                total = summed[0:1, :]
+                log_total = highest + jnp.log(total)
+                turned = jnp.where(row == 0, log_total, summed * (1.0 / total)).T
+                high, middle, low = three_parts(turned[:, 0:1])
+                wide_ref[head, here, :] = jnp.where(
+                    lane == HD + 1,
+                    -high,
+                    jnp.where(lane == HD + 2, -middle, jnp.where(lane == HD + 3, -low, wide)),
+                ).astype(bf16)
+                parts.append(turned)
+            context_ref[here, 0:LANES] = jnp.where(
+                lane < HD, pltpu.roll(parts[0], HD, axis=1), parts[1]
+            ).astype(bf16)
+            context_ref[here, LANES : LANES + HD] = pltpu.roll(parts[2], HD, axis=1)[
+                :, :HD
+            ].astype(bf16)
+
+            @pl.when(index == t)
+            def _():
+                spread_ref[t] = context_ref[here, :]
+
+            @pl.when(index != t)
+            def _():
+                context_copy(index).start()
+
+            return inner
+
+        lax.fori_loop(0, per_half, block, 0)
+
+        @pl.when(step == 0)
+        def _():
+            mate_copy.wait()
+            start_mlp()
+            relay_out()
+
+        return carry
+
+    lax.fori_loop(0, 2, half, 0)
+    relay_mlp()
+
+    def settle(j, carry):
+        toward = lax.rem(t + j, tp_count)
+        context_copy(toward).wait_send()
+        remote(
+            context_ref.at[pl.ds(0, rows)],
+            spread_ref.at[toward],
+            context_send.at[toward],
+            context_recv.at[toward],
+            f,
+            toward,
+        ).wait_recv()
+        return carry
+
+    lax.fori_loop(1, tp_count, settle, 0)
+    finish_out()
+    finish_mlp()
+    drain_out()
+    drain_mlp()
+
+
+def attend(fsdp_count, tp_count, lengths, query, pairs, mlp, out_weights, heads):
+    bf16 = jnp.bfloat16
+    group = query.shape[0]
+    rows = group // tp_count
+    width = heads * HD
+    dma = pltpu.SemaphoreType.DMA
+    depth = mlp.shape[1]
+    return pl.pallas_call(
+        functools.partial(attend_kernel, fsdp_count, tp_count),
+        out_shape=(
+            jax.ShapeDtypeStruct((tp_count, rows, width), bf16),
+            jax.ShapeDtypeStruct((group, width), bf16),
+            jax.ShapeDtypeStruct((heads, group, LANES), bf16),
+            jax.ShapeDtypeStruct((mlp.shape[0], depth * fsdp_count, mlp.shape[2]), bf16),
+            jax.ShapeDtypeStruct((tp_count, depth * fsdp_count, width), bf16),
+        ),
+        in_specs=[pl.BlockSpec(memory_space=pltpu.SMEM)] + whole_specs(4),
+        out_specs=tuple(whole_specs(5)),
+        scratch_shapes=[
+            pltpu.VMEM(mlp.shape, bf16),
+            pltpu.VMEM((heads, CLIP, LANES), bf16),
+            pltpu.VMEM((heads, LANES, CLIP), bf16),
+            dma,
+            dma,
+            dma((tp_count,)),
+            dma((tp_count,)),
+            dma((fsdp_count,)),
+            dma((fsdp_count,)),
+            dma((fsdp_count,)),
+            dma((fsdp_count,)),
+        ],
+        compiler_params=pltpu.CompilerParams(
+            collective_id=2, has_side_effects=True, vmem_limit_bytes=VMEM_LIMIT
+        ),
+        name="attend",
+    )(lengths, query, pairs, mlp, out_weights)
+
+
+def column_sum(rows):
+    return jnp.sum(rows, axis=0, keepdims=True)
+
+
+def rows_kernel(
+    fsdp_count,
+    tp_count,
+    x_ref,
+    spread_ref,
+    heads_ref,
+    vector_ref,
+    bias_ref,
+    own_ref,
+    mate_ref,
+    cotangent_ref,
+    gradient_ref,
+    outputs_ref,
+    mixed_ref,
+    context_ref,
+    own_grad,
+    mate_grad,
+    heads_grad,
+    bias_grad,
+    sums_ref,
+    upstream,
+    rounded,
+    hidden_ref,
+    unit_ref,
+    normed_ref,
+    active_ref,
+    slope_ref,
+    mixed_sum,
+    norm_sum,
+    norm_out,
+    norm_in,
+    load_sem,
+    row_send,
+    row_recv,
+    norm_send,
+    norm_recv,
+):
+    f = lax.axis_index("fsdp")
+    t = lax.axis_index("tp")
+    bf16 = jnp.bfloat16
+    f32 = jnp.float32
+    rows = x_ref.shape[0]
+    tile = 256
+    side = lax.rem(t, 2)
+    peer = t + 1 - 2 * side
+    load = pltpu.make_async_copy(
+        cotangent_ref.at[pl.ds((t - side) * rows, 2 * rows)], upstream, load_sem
+    )
+    load.start()
+    barrier = pltpu.get_barrier_semaphore()
+    pl.semaphore_signal(barrier, inc=1, device_id=(f, peer), device_id_type=MESH)
+    pl.semaphore_wait(barrier, 1)
+
+    hidden = x_ref[...] + vector_ref[0:1, :]
+    for j in range(tp_count):
+        hidden = hidden + lax.dot_general(
+            spread_ref[j], heads_ref[j], (((1,), (1,)), ((), ())), preferred_element_type=f32
+        )
+    hidden_ref[...] = hidden
+    unit, spread, normed = normalize(hidden, vector_ref[1:2, :], vector_ref[2:3, :])
+    unit_ref[...] = unit
+    normed_ref[side] = normed.astype(bf16)
+    row_copy = remote(normed_ref.at[side], normed_ref.at[side], row_send, row_recv, f, peer)
+    row_copy.start()
+    load.wait()
+
+    def rounding(i, carry):
+        rounded[pl.ds(i * rows, rows), :] = upstream[pl.ds(i * rows, rows), :].astype(bf16)
+        return carry
+
+    lax.fori_loop(0, 2, rounding, 0)
+    mixed_sum[...] = jnp.zeros(mixed_sum.shape, f32)
+    norm_sum[...] = jnp.zeros(norm_sum.shape, f32)
+    chunks = own_ref.shape[1] // tile
+    mate = lax.rem(t + tp_count // 2, tp_count)
+
+    def feed_forward(turn, carry):
+        which = lax.rem(side + turn, 2)
+
+        @pl.when(turn == 1)
+        def _():
+            row_copy.wait_recv()
+
+        here = pl.ds(pl.multiple_of(which * rows, rows), rows)
+        normed_rows = normed_ref[which]
+        upstream_rows = rounded[here, :]
+
+        for level, (weights, owner) in enumerate(((own_ref, t), (mate_ref, mate))):
+
+            def chunk(c, inner, weights=weights, owner=owner, level=level):
+                units = pl.ds(pl.multiple_of(c * tile, tile), tile)
+                up = weights[0, units, :]
+                down = weights[1, units, :]
+                preact = (
+                    lax.dot_general(
+                        normed_rows, up, (((1,), (1,)), ((), ())), preferred_element_type=f32
+                    )
+                    + bias_ref[owner, c]
+                )
+                cdf = 0.5 * (1.0 + lax.erf(preact * root_half))
+                active = (preact * cdf).astype(bf16)
+                slope = cdf + preact * jnp.exp(-0.5 * preact * preact) * inv_root_tau
+                dactive = lax.dot_general(
+                    upstream_rows, down, (((1,), (1,)), ((), ())), preferred_element_type=f32
+                )
+                dpreact = (dactive * slope).astype(bf16)
+                active_ref[level, c, here, :] = active
+                slope_ref[level, c, here, :] = dpreact
+                norm_sum[which] += jnp.dot(dpreact, up, preferred_element_type=f32)
+                mixed_sum[which] += jnp.dot(active, down, preferred_element_type=f32)
+                return inner
+
+            lax.fori_loop(0, chunks, chunk, 0)
+        return carry
+
+    lax.fori_loop(0, 2, feed_forward, 0)
+    norm_out[...] = norm_sum[1 - side].astype(bf16)
+    norm_copy = remote(norm_out, norm_in, norm_send, norm_recv, f, peer)
+    norm_copy.start()
+    mixed_ref[...] = mixed_sum[1 - side].astype(bf16)
+    outputs_ref[...] = hidden_ref[...] + mixed_sum[side] + vector_ref[3:4, :]
+
+    for level, grad in enumerate((own_grad, mate_grad)):
+
+        def weight_grads(c, carry, level=level, grad=grad):
+            units = pl.ds(pl.multiple_of(c * tile, tile), tile)
+            slopes = slope_ref[level, c]
+            both = jnp.concatenate([normed_ref[0], normed_ref[1]], axis=0)
+            grad[0, units, :] = contract_rows(slopes, both).astype(bf16)
+            grad[1, units, :] = contract_rows(active_ref[level, c], rounded[...]).astype(bf16)
+            bias_grad[level, c] = column_sum(slopes.astype(f32))
+            return carry
+
+        lax.fori_loop(0, chunks, weight_grads, 0)
+
+    norm_copy.wait()
+    dnorm = norm_sum[side] + norm_in[...].astype(f32)
+    unit = unit_ref[...]
+    cotangent = upstream[pl.ds(pl.multiple_of(side * rows, rows), rows), :]
+    gradient = cotangent + norm_back(dnorm, unit, spread, vector_ref[1:2, :])
+    gradient_ref[...] = gradient
+    sums_ref[0:1, :] = column_sum(dnorm * unit)
+    sums_ref[1:2, :] = column_sum(dnorm)
+    sums_ref[2:3, :] = column_sum(gradient)
+    sums_ref[3:4, :] = column_sum(cotangent)
+    gradient = gradient.astype(bf16)
+    for j in range(tp_count):
+        context_ref[j] = jnp.dot(gradient, heads_ref[j], preferred_element_type=f32).astype(bf16)
+        heads_grad[j] = contract_rows(gradient, spread_ref[j]).astype(bf16)
+    row_copy.wait_send()
+
+
+def by_rows(fsdp_count, tp_count, x, spread, heads, vectors, bias, own, mate, cotangent):
+    bf16 = jnp.bfloat16
+    f32 = jnp.float32
+    rows, features = x.shape
+    units = own.shape[1]
+    chunks = units // 256
+    dma = pltpu.SemaphoreType.DMA
+    return pl.pallas_call(
+        functools.partial(rows_kernel, fsdp_count, tp_count),
+        out_shape=(
+            jax.ShapeDtypeStruct((rows, features), f32),
+            jax.ShapeDtypeStruct((rows, features), f32),
+            jax.ShapeDtypeStruct((rows, features), bf16),
+            jax.ShapeDtypeStruct(spread.shape, bf16),
+            jax.ShapeDtypeStruct(own.shape, bf16),
+            jax.ShapeDtypeStruct(own.shape, bf16),
+            jax.ShapeDtypeStruct(heads.shape, bf16),
+            jax.ShapeDtypeStruct((2, chunks, 1, 256), f32),
+            jax.ShapeDtypeStruct((4, features), f32),
+        ),
+        in_specs=whole_specs(7) + [pl.BlockSpec(memory_space=pl.ANY)],
+        out_specs=tuple(whole_specs(9)),
+        scratch_shapes=[
+            pltpu.VMEM((2 * rows, features), f32),
+            pltpu.VMEM((2 * rows, features), bf16),
+            pltpu.VMEM((rows, features), f32),
+            pltpu.VMEM((rows, features), f32),
+            pltpu.VMEM((2, rows, features), bf16),
+            pltpu.VMEM((2, chunks, 2 * rows, 256), bf16),
+            pltpu.VMEM((2, chunks, 2 * rows, 256), bf16),
+            pltpu.VMEM((2, rows, features), f32),
+            pltpu.VMEM((2, rows, features), f32),
+            pltpu.VMEM((rows, features), bf16),
+            pltpu.VMEM((rows, features), bf16),
+            dma,
+            dma,
+            dma,
+            dma,
+            dma,
+        ],
+        compiler_params=pltpu.CompilerParams(
+            collective_id=4, has_side_effects=True, vmem_limit_bytes=VMEM_LIMIT
+        ),
+        name="by_rows",
+    )(x, spread, heads, vectors, bias, own, mate, cotangent)
+
+
+def pack_columns(key, value, query):
+    lead = key.shape[:-1]
+    heads = key.shape[-1] // HD
+    pairs = jnp.stack([key.reshape(*lead, heads, HD), value.reshape(*lead, heads, HD)], axis=-2)
+    spare = jnp.zeros((*lead, -key.shape[-1] % LANES), key.dtype)
+    return jnp.concatenate([pairs.reshape(*lead, -1), query, spare], axis=-1)
 
 
 def on_device(
@@ -372,28 +894,40 @@
     score_scale = 1.0 / math.sqrt(HD)
     margin = CLIP - QB
     tp_slot = (jnp.arange(tp_count) == tp_index).astype(f32)
-    own_cotangent = lax.dynamic_slice_in_dim(out_cotangent, tp_index * own_rows, own_rows, 0)
     unit1, spread1, _ = normalize(inputs, norm1_gain, norm1_shift)
     local_width = query_weight.shape[1]
     heads_here = local_width // HD
+    unit_count = fc1_weight.shape[0]
     by_tp = lambda bias: bias.reshape(tp_count, 1, local_width)
-    attention_bias = jnp.concatenate(
-        [jnp.zeros((tp_count, 1, local_width), f32), by_tp(value_bias), by_tp(query_bias)], axis=2
-    )
-    query, pairs, normed, attention_w = project(
+    pair_width = 2 * local_width
+    mlp_own = jnp.stack([fc1_weight, fc2_weight])
+    query, pairs, normed, attention_w, mlp_w, out_parts = project(
         fsdp_count,
         tp_count,
         inputs,
         norm1_gain.reshape(1, -1),
         norm1_shift.reshape(1, -1),
-        jnp.concatenate([key_weight, value_weight, query_weight], axis=1),
-        attention_bias,
+        pack_columns(key_weight, value_weight, query_weight)[None],
+        pack_columns(jnp.zeros((tp_count, 1, local_width), f32), by_tp(value_bias), by_tp(query_bias)),
+        mlp_own,
+        out_weight,
+        pair_width,
         margin,
     )
+    attention_w = attention_w[0]
+    spread, context, wide, mlp_other, out_full = attend(
+        fsdp_count, tp_count, clip_lengths, query, pairs, mlp_own, out_parts, heads_here
+    )
+    totals = -jnp.sum(wide[:, :, HD + 1 : HD + 4].astype(f32), axis=2)
+    query = query[:, :local_width]
     normed = normed.reshape(group_rows, -1)
-    key_w, value_w, query_w = jnp.split(attention_w, 3, axis=1)
-    padded = jnp.stack(jnp.split(pairs, 2, axis=1))
-    out_w = lax.all_gather(out_weight, "fsdp", axis=0, tiled=True)
+    key_w, value_w = jnp.moveaxis(attention_w[:, :pair_width].reshape(-1, heads_here, 2, HD), 2, 0)
+    key_w = key_w.reshape(-1, local_width)
+    value_w = value_w.reshape(-1, local_width)
+    query_w = attention_w[:, pair_width : pair_width + local_width]
+    padded = jnp.moveaxis(pairs.reshape(-1, heads_here, 2, HD), 2, 0).reshape(2, -1, local_width)
+    out_w = lax.dynamic_index_in_dim(out_full, tp_index, 0, False)
+    w_up, w_down = mlp_w
     group_base = fsdp_index * group_rows
     clip_ids = jnp.arange(clip_lengths.shape[0])
     block_count = group_rows // QB
@@ -412,65 +946,41 @@
         scores = jnp.where((jnp.arange(CLIP) < length)[None, None, :], scores, far_negative)
         return (first_row, key_start, query_block, pair[0], pair[1], scores)
 
-    def attend(block_index, carry):
-        context_rows, total_rows = carry
-        first_row, key_start, query_block, key_block, value_block, scores = block_scores(
-            block_index
-        )
-        highest = jnp.max(scores, axis=-1, keepdims=True)
-        log_total = highest[..., 0] + jnp.log(jnp.sum(jnp.exp(scores - highest), axis=-1))
-        weights = jnp.exp(scores - log_total[..., None]).astype(bf16)
-        block_out = jnp.einsum("hqk,khe->qhe", weights, value_block, preferred_element_type=f32)
-        block_out = block_out.astype(bf16).reshape(QB, local_width)
-        context_rows = lax.dynamic_update_slice_in_dim(context_rows, block_out, first_row, 0)
-        total_rows = lax.dynamic_update_slice_in_dim(total_rows, log_total, first_row, 1)
-        return (context_rows, total_rows)
-
-    context, totals = lax.fori_loop(
-        0,
-        block_count,
-        attend,
-        (jnp.zeros((group_rows, local_width), bf16), jnp.zeros((heads_here, group_rows), f32)),
-    )
-    attended = scatter_rows(contract_cols(context, out_w), "tp")
-    hidden = inputs + attended + out_bias
-    unit2, spread2, normed2_full = normalize(hidden, norm2_gain, norm2_shift)
-    normed2_own = normed2_full.astype(bf16)
-    normed2 = lax.all_gather(normed2_own, "tp", axis=0, tiled=True)
-    w_up, w_down = jnp.split(
-        lax.all_gather(
-            jnp.concatenate([fc1_weight, fc2_weight], axis=1), "fsdp", axis=0, tiled=True
-        ),
-        2,
-        axis=1,
-    )
-    unit_count = fc1_weight.shape[0]
-    bias_up = lax.dynamic_index_in_dim(
-        fc1_bias.reshape(fsdp_count, tp_count, unit_count), tp_index, 1, False
-    ).reshape(-1)
-    preact = contract_cols(normed2, w_up) + bias_up
-    activated = gelu_exact(preact).astype(bf16)
-    mixed = scatter_rows(jnp.dot(activated, w_down, preferred_element_type=f32), "tp")
-    outputs = hidden + mixed + fc2_bias
-    up_rounded = out_cotangent.astype(bf16)
-    dactivated = contract_cols(up_rounded, w_down)
-    dpreact = (dactivated * gelu_slope(preact)).astype(bf16)
-    grad_up_part = contract_rows(dpreact, normed2)
-    grad_down_part = contract_rows(activated, up_rounded)
-    upbias_part = jnp.sum(dpreact.astype(f32), axis=0)
-    grad_b1 = (upbias_part.reshape(fsdp_count, 1, unit_count) * tp_slot[None, :, None]).reshape(-1)
-    dnorm2 = scatter_rows(jnp.dot(dpreact, w_up, preferred_element_type=f32), "tp")
-    grad_fc1, grad_fc2 = jnp.split(
-        scatter_rows(jnp.concatenate([grad_up_part, grad_down_part], axis=1), "fsdp"), 2, axis=1
-    )
-    grad_b2 = jnp.sum(own_cotangent, axis=0)
-    grad_gain2 = jnp.sum(dnorm2 * unit2, axis=0)
-    grad_shift2 = jnp.sum(dnorm2, axis=0)
-    dhidden = own_cotangent + norm_back(dnorm2, unit2, spread2, norm2_gain)
-    grad_obias = jnp.sum(dhidden, axis=0)
-    dh_all = lax.all_gather(dhidden.astype(bf16), "tp", axis=0, tiled=True)
-    dcontext = jnp.dot(dh_all, out_w, preferred_element_type=f32).astype(bf16)
-    grad_out = contract_rows(dh_all, context)
+    unit_bias = jnp.swapaxes(fc1_bias.reshape(fsdp_count, tp_count, unit_count), 0, 1)
+    dhidden, outputs, mixed, dspread, own_grad, mate_grad, heads_grad, bias_part, sums = by_rows(
+        fsdp_count,
+        tp_count,
+        inputs,
+        spread,
+        out_full,
+        jnp.stack([out_bias, norm2_gain, norm2_shift, fc2_bias]),
+        unit_bias.reshape(tp_count, -1, 1, 256),
+        mlp_w,
+        mlp_other,
+        out_cotangent,
+    )
+    outputs = outputs + lax.ppermute(
+        mixed, "tp", [(i, i ^ 1) for i in range(tp_count)]
+    ).astype(f32)
+    halves = [(i, (i + tp_count // 2) % tp_count) for i in range(tp_count)]
+    grad_both = lax.psum_scatter(
+        jnp.concatenate([*own_grad, *mate_grad], axis=1),
+        "fsdp",
+        scatter_dimension=0,
+        tiled=True,
+    )
+    grad_own, grad_mate = jnp.split(grad_both, 2, axis=1)
+    grad_own = grad_own.astype(f32) + lax.ppermute(grad_mate, "tp", halves).astype(f32)
+    grad_fc1, grad_fc2 = jnp.split(grad_own, 2, axis=1)
+    grad_out = lax.psum_scatter(heads_grad, "fsdp", scatter_dimension=1, tiled=True)
+    grad_out = lax.psum_scatter(grad_out, "tp", scatter_dimension=0, tiled=True)[0].astype(f32)
+    grad_gain2, grad_shift2, grad_obias, grad_b2 = sums
+    mate_index = (tp_index + tp_count // 2) % tp_count
+    mate_slot = (jnp.arange(tp_count) == mate_index).astype(f32)
+    bias_part = bias_part.reshape(2, -1)
+    by_tp_sum = tp_slot[:, None] * bias_part[0] + mate_slot[:, None] * bias_part[1]
+    grad_b1 = jnp.swapaxes(by_tp_sum.reshape(tp_count, fsdp_count, unit_count), 0, 1).reshape(-1)
+    dcontext = lax.all_to_all(dspread, "tp", 0, 0, tiled=False).reshape(group_rows, local_width)
     delta = jnp.sum(
         (dcontext.astype(f32) * context.astype(f32)).reshape(group_rows, heads_here, HD), axis=-1
     ).T
@@ -529,11 +1039,9 @@
     grad_gain1 = jnp.sum(dnorm1 * unit1, axis=0)
     grad_shift1 = jnp.sum(dnorm1, axis=0)
     inputs_grad = dhidden + norm_back(dnorm1, unit1, spread1, norm1_gain)
-    grad_query, grad_key, grad_value, grad_out = jnp.split(
-        scatter_rows(
-            jnp.concatenate([grad_query, grad_key, grad_value, grad_out], axis=1), "fsdp"
-        ),
-        4,
+    grad_query, grad_key, grad_value = jnp.split(
+        scatter_rows(jnp.concatenate([grad_query, grad_key, grad_value], axis=1), "fsdp"),
+        3,
         axis=1,
     )
     (

time: 521 us -> 434 us (0.83)
  waiting for transfers between devices: 262 us -> 143 us
  Pallas kernels: 42.9 us -> 125 us
  matrix products: 58.3 us -> 25 us
  blocking collectives: 53.3 us -> 40.9 us
  other arithmetic: 38.5 us -> 28.3 us
  starting transfers between devices: 3.86 us -> 10.4 us
    reduce_scatter x4 -> x1, waiting for transfers between devices: 144 us -> 34.4 us  [scatter_rows(): lax.psum_scatter(partial_rows.astype(jnp.bfloat16), axis, scatter_dimensi...]
    pallas_call x0 -> x2, Pallas kernels: none -> 78.2 us  [the longest x1 43.8 us: attend(): pl.pallas_call(functools.partial(attend_kernel, fsdp_count, tp_count), ou...]
    all_gather x3 -> x0, waiting for transfers between devices: 57.3 us -> none  [the longest x1 32.8 us: on_device(): normed2 = lax.all_gather(normed2_own, 'tp', axis=0, tiled=True)]
    reduce_scatter x0 -> x3, waiting for transfers between devices: none -> 54.5 us  [the longest x1 54.5 us: on_device(): lax.psum_scatter(jnp.concatenate([*own_grad, *mate_grad], axis=1), 'fsdp'...]
    dot_general x5 -> x0, matrix products: 14.4 us -> none  [the longest x2 4.4 us: attend(): jnp.einsum('hqk,khe->qhe', weights, value_block, preferred_element_type=f32)]
    all_gather x1 -> x0, blocking collectives: 12.9 us -> none  [on_device(): out_w = lax.all_gather(out_weight, 'fsdp', axis=0, tiled=True)]
    unnamed x11 -> x6, waiting for transfers between devices: 56.2 us -> 43.8 us
    unnamed x76 -> x45, local copies, waits for them, and re-layouts: 21.1 us -> 9.79 us
  transfers between devices with their start and end apart: 11 -> 10, of which waited for: 9 -> 6; matrix products, arithmetic and copies ran while one was open for 16% -> 18% of each run, Pallas kernels for 0% -> 0%
where the time goes in v3:
time: 434 us; the launch traced here: 433 us
  waiting for transfers between devices  143 us (33%)
  Pallas kernels  125 us (29%)
  local copies, waits for them, and re-layouts  45.9 us (11%)
  blocking collectives  40.9 us (9%)
  other arithmetic  28.3 us (7%)
  matrix products  25 us (6%)
  between operations  14.2 us (3%)
  starting transfers between devices  10.4 us (2%)
    reduce_scatter x1, waiting for transfers between devices, on_device(): lax.psum_scatter(jnp.concatenate([*own_grad, *mate_grad], axis=1), 'fsdp'...  54.5 us
    pallas_call x1, Pallas kernels, project(): pl.pallas_call(functools.partial(project_kernel, fsdp_count, tp_count), o...  46.3 us
    unnamed x6, waiting for transfers between devices  43.8 us
    pallas_call x1, Pallas kernels, attend(): pl.pallas_call(functools.partial(attend_kernel, fsdp_count, tp_count), ou...  43.8 us
    psum x1, blocking collectives, on_device(): lax.psum((grad_gain1, grad_shift1, grad_qbias, grad_vbias, grad_obias, gr...  40.9 us
    pallas_call x1, Pallas kernels, by_rows(): pl.pallas_call(functools.partial(rows_kernel, fsdp_count, tp_count), out_...  34.5 us
    reduce_scatter x1, waiting for transfers between devices, scatter_rows(): lax.psum_scatter(partial_rows.astype(jnp.bfloat16), axis, scatter_dimensi...  34.4 us
    unnamed x45, local copies, waits for them, and re-layouts  9.79 us
  transfers between devices with their start and end apart: 10, of which 6 were waited for; matrix products, arithmetic and copies ran while one was open for 18% of the time, Pallas kernels for 0%

profile of v3, /device:TPU:0, one launch (start us, length us, event | category | flops | bytes accessed | tf_op | source)
XLA Modules:
  0.0 432.8 jit_solution(9731965812808399638)
XLA Ops:
  7.2 0.9 copy.70
  8.1 0.9 copy.71
  9.2 0.8 stack_reshape_reshape.3
  10.1 0.8 reshape.287
  10.8 1.3 reshape.283.gain_ref
  12.1 1.3 reshape.284.shift_ref
  13.4 0.8 reshape.288
  17.6 1.7 pad_maximum_fusion.2.mlp_ref
  19.5 1.5 maximum_bitcast_fusion.weight_ref
  21.6 46.3 %project.1 = (bf16[1024,256]{1,0:T(8,128)(2,1)}, bf16[3072,384]{1,0:T(8,128)(2,1)}, bf16[4,256,768]{2,1,0:T(8,128)(2,1)}, bf16[1,768,640]{2,1,0:T(8,128)(2,1)}, ...) custom-call(f32[256,768]{1,0:T(8,128)} %x_ref.3, f32[1,768]{1,0:T(1,128)} %reshape.283.gain_ref, ...), custom_call_target="tpu_custom_call" | custom-call | tf_op jit(solution)/shard_map/project/pallas_call | solution.py:403
  67.9 43.8 %attend.1 = (bf16[4,256,192]{2,1,0:T(8,128)(2,1)}, bf16[1024,192]{1,0:T(8,128)(2,1)}, bf16[3,1024,128]{2,1,0:T(8,128)(2,1)}, bf16[2,768,768]{2,1,0:T(8,128)(2,1)}, bf16[4,768,192]{2,1,0:T(8,128)(2,1)}) custom-call(s32[6]{0:T(128)} %lengths_ref.1, bf16[1024,256]{1,0:T(8,128)(2,1)} %get-tuple-element.344.query_ref, ...), custom_call_target="tpu_custom_call" | custom-call | tf_op jit(solution)/shard_map/attend/pallas_call | solution.py:624
  112.2 34.5 %by_rows.1 = (f32[256,768]{1,0:T(8,128)}, f32[256,768]{1,0:T(8,128)}, bf16[256,768]{1,0:T(8,128)(2,1)}, bf16[4,256,192]{2,1,0:T(8,128)(2,1)}, bf16[2,768,768]{2,...) custom-call(f32[256,768]{1,0:T(8,128)} %x_ref.3, ...), custom_call_target="tpu_custom_call" | custom-call | tf_op jit(solution)/shard_map/by_rows/pallas_call | solution.py:818
  146.7 2.1 copy.77
  148.9 3.5 all-to-all-start
  153.3 2.7 copy.75
  156.0 1.7 convert_reduce_fusion
  158.3 1.8 copy.76
  160.2 0.9 copy.80
  161.1 2.6 all-to-all-done
  163.9 2.1 convert_multiply_fusion.2
  166.0 2.5 copy.79
  168.5 1.2 reduce_sum.109
  169.7 1.0 copy.81
  170.7 2.8 broadcast_in_dim.83
  173.4 0.8 broadcast_in_dim.82
  174.2 28.0 %while.22 = (s32[]{:T(128)}, bf16[1024,192]{0,1:T(8,128)(2,1)}, f32[2,3072,192]{1,2,0:T(8,128)}, s32[]{:T(128)}, bf16[2,3072,192]{1,2,0:T(8,128)(2,1)S(1)}, /*in...) while((s32[]{:T(128)}, bf16[1024,192]{0,1:T(8,128)(2,1)}, ...), condition=%wide.region_6.7_spmd.clone, body=%wide.region_4.6_spmd.clone.sunk | while | flops 1537181184 | bytes 94469328 | solution.py:1015
  174.3 1.1 constant_dynamic-slice_fusion.10
  175.4 1.4 fusion.73
  178.2 3.4 multiply_convert_fusion.2
  181.6 0.9 fusion.76
  182.6 2.1 fusion.75
  185.3 1.5 convolution_convert_fusion.5
  188.3 1.1 constant_dynamic-slice_fusion.10
  189.4 1.4 fusion.73
  192.2 3.4 multiply_convert_fusion.2
  195.6 0.9 fusion.76
  196.6 2.1 fusion.75
  199.3 1.5 convolution_convert_fusion.5
  201.5 0.7 copy-done.5
  202.2 4.1 fusion.26
  206.4 2.5 collective-permute-start.1
  208.8 1.3 collective-permute-start.2
  210.5 1.2 convolution_convert_fusion.3
  211.8 3.4 collective-permute-done.2
  215.1 2.7 add_add_fusion
  218.9 1.4 copy.86
  220.6 1.6 fusion.19
  222.9 1.8 add_convert_fusion
  224.8 1.9 slice_bitcast_fusion.1
  226.8 2.5 pad_maximum_fusion
  229.4 1.0 copy-done.1
  232.8 4.7 %collective-permute-done = bf16[256,768]{1,0:T(8,128)(2,1)} collective-permute-done((bf16[256,768]{1,0:T(8,128)(2,1)}, bf16[256,768]{1,0:T(8,128)(2,1)}, u32[]{:S(2)}, u32[]{:S(2)}) %collective-permute-start) | collective-permute-done | bytes 393248 | tf_op jit(solution)/shard_map/ppermute | solution.py:962
  237.5 1.9 convert_add_fusion
  239.6 1.4 bitcast_convert_fusion
  242.0 43.1 %reduce-scatter.16.cloned.1.call-done = bf16[96,576]{1,0:T(8,128)(2,1)} async-done(((bf16[768,576]{1,0:T(8,128)(2,1)}), bf16[96,576]{1,0:T(8,128)(2,1)}) %reduce-scatter.16.cloned.1.call-update) | async-done | bytes 110608
  285.1 1.0 copy.87
  288.4 34.4 %reduce-scatter.8.cloned.1.call-done = bf16[256,768]{1,0:T(8,128)(2,1)} async-done(((bf16[1024,768]{1,0:T(8,128)(2,1)}), bf16[256,768]{1,0:T(8,128)(2,1)}) %reduce-scatter.8.cloned.1.call-update) | async-done | bytes 393232 | tf_op jit(solution)/shard_map/reduce_scatter | solution.py:76
  322.8 1.4 fusion.17
  324.2 54.5 %reduce-scatter.14.cloned.1.call-done = bf16[96,3072]{1,0:T(8,128)(2,1)} async-done(((bf16[768,3072]{1,0:T(8,128)(2,1)}), bf16[96,3072]{1,0:T(8,128)(2,1)}) %reduce-scatter.14.cloned.1.call-update) | async-done | bytes 589840 | tf_op jit(solution)/shard_map/reduce_scatter | solution.py:966
  378.7 1.1 split.32
  379.8 2.5 collective-permute-start.3
  382.2 40.9 %all-reduce.1 = (f32[768]{0:T(1024)}, f32[768]{0:T(1024)}, f32[768]{0:T(1024)}, f32[768]{0:T(1024)}, f32[768]{0:T(1024)}, /*index=5*/f32[768]{0:T(1024)}, f32[768]{0:T(1024)}, f32[3072]{0:T(1024)}, f32[768]{0:T(1024)}) all-reduce(f32[768]{0:T(1024)S(1)} %get-tuple-element.496, ...), channel_id=1, replica_groups=mesh['fsdp'=8,'tp'=4] {'fsdp','tp'}, use_global_device_ids=true, to_apply=%region_11.12 | all-reduce | flops 9216 | bytes 73728 | tf_op jit(solution)/shard_map/psum | solution.py:1057
  423.1 2.2 fusion.15
  425.4 0.9 fusion.27
  (140 shorter events, 21.2 us)
Async XLA Ops:
  146.7 6.6 %copy-start.3 = (bf16[3072,384]{1,0:T(8,128)(2,1)S(1)}, bf16[3072,384]{1,0:T(8,128)(2,1)}, u32[]{:S(2)}) copy-start(bf16[3072,384]{1,0:T(8,128)(2,1)} %get-tuple-element.345.pair_ref) | copy-start | bytes 7077892
  148.9 14.8 %all-to-all-start = ((bf16[4,256,192]{1,2,0:T(8,128)(2,1)}), bf16[4,256,192]{1,2,0:T(8,128)(2,1)S(1)}, u32[]{:S(2)}, u32[]{:S(2)}) async-start(bf16[4,256,192]{1,2,0:T(8,128)(2,1)} %copy.77), calls=%async_computation | async-start | bytes 786432 | tf_op jit(solution)/shard_map/all_to_all | solution.py:983
  152.3 59.4 %reduce-scatter.10.cloned.1.call-start = ((), (), s32[]{:S(2)}) async-start(), calls=%async_computation.7 | async-start | bytes 1769472 | tf_op jit(solution)/shard_map/reduce_scatter | solution.py:975
  153.1 86.5 %reduce-scatter.12.cloned.1.call-start = ((), (), s32[]{:S(2)}) async-start(), calls=%async_computation.8 | async-start | bytes 245760 | tf_op jit(solution)/shard_map/reduce_scatter | solution.py:976
  156.0 4.2 copy-start.8
  175.4 1.5 copy-start.22
  175.4 2.7 copy-start.14
  181.6 3.0 slice-start
  182.6 2.1 slice-start.1
  185.2 2.2 copy-start
  185.3 2.2 copy-start.4
  187.5 0.7 copy-start.5
  189.4 1.5 copy-start.22
  189.4 2.7 copy-start.14
  195.6 3.0 slice-start
  196.6 2.1 slice-start.1
  199.2 2.2 copy-start
  199.3 2.2 copy-start.4
  201.5 0.7 copy-start.5
  202.2 7.9 %copy-start.10 = (bf16[1,768,640]{2,1,0:T(8,128)(2,1)S(1)}, bf16[1,768,640]{2,1,0:T(8,128)(2,1)}, u32[]{:S(2)}) copy-start(bf16[1,768,640]{2,1,0:T(8,128)(2,1)} %get-tuple-element.358) | copy-start | bytes 2949124
  202.2 8.2 %copy-start.2 = (bf16[4,256,768]{2,1,0:T(8,128)(2,1)S(1)}, bf16[4,256,768]{2,1,0:T(8,128)(2,1)}, u32[]{:S(2)}) copy-start(bf16[4,256,768]{2,1,0:T(8,128)(2,1)} %get-tuple-element.360) | copy-start | bytes 4718596
  202.2 8.2 %copy-start.6 = (bf16[1024,192]{0,1:T(8,128)(2,1)S(1)}, bf16[1024,192]{0,1:T(8,128)(2,1)}, u32[]{:S(2)}) copy-start(bf16[1024,192]{0,1:T(8,128)(2,1)} %get-tuple-element.357) | copy-start | bytes 1179652
  206.4 5.4 %collective-permute-start.1 = (f32[2,1024,192]{1,2,0:T(8,128)}, f32[2,1024,192]{1,2,0:T(8,128)}, u32[]{:S(2)}, u32[]{:S(2)}) collective-permute-start(f32[2,1024,192]{1,2,0:T(8,128)} %get-tuple-element.541), channel_id=1, source_target_pairs={{0,4},{4,8},{8,12},{12,16},{16,20},{20,24},{24,28},{1,5},{5,9},{9,... | collective-permute-start | bytes 4718600 | tf_op jit(solution)/shard_map/ppermute | solution.py:29
  208.8 6.3 %collective-permute-start.2 = (f32[2,1024,192]{1,2,0:T(8,128)}, f32[2,1024,192]{1,2,0:T(8,128)}, u32[]{:S(2)}, u32[]{:S(2)}) collective-permute-start(f32[2,1024,192]{1,2,0:T(8,128)} %get-tuple-element.542), channel_id=1, source_target_pairs={{4,0},{8,4},{12,8},{16,12},{20,16},{24,20},{28,24},{5,1},{9,5},{13... | collective-permute-start | bytes 4718600 | tf_op jit(solution)/shard_map/ppermute | solution.py:30
  211.7 73.4 %reduce-scatter.16.cloned.1.call-start = ((), (), s32[]{:S(2)}) async-start(), calls=%async_computation.10 | async-start | bytes 1105920
  217.9 1.0 copy-start.9
  220.3 102.4 %reduce-scatter.8.cloned.1.call-start = ((), (), s32[]{:S(2)}) async-start(), calls=%async_computation.6 | async-start | bytes 1966080 | tf_op jit(solution)/shard_map/reduce_scatter | solution.py:76
  222.9 1.9 copy-start.7
  224.8 153.9 %reduce-scatter.14.cloned.1.call-start = ((), (), s32[]{:S(2)}) async-start(), calls=%async_computation.9 | async-start | bytes 5308416 | tf_op jit(solution)/shard_map/reduce_scatter | solution.py:966
  229.3 1.1 copy-start.1
  229.3 1.3 copy-start.20
  229.3 2.0 copy-start.18
  229.3 8.2 %copy-start.12 = (f32[256,768]{1,0:T(8,128)S(1)}, f32[256,768]{1,0:T(8,128)}, u32[]{:S(2)}) copy-start(f32[256,768]{1,0:T(8,128)} %get-tuple-element.351) | copy-start | bytes 2359300
  229.3 93.5 %copy-start.15 = (f32[768]{0:T(1024)S(1)}, f32[768]{0:T(1024)}, u32[]{:S(2)}) copy-start(f32[768]{0:T(1024)} %param.31) | copy-start | bytes 9220
  229.3 8.2 %collective-permute-start = (bf16[256,768]{1,0:T(8,128)(2,1)}, bf16[256,768]{1,0:T(8,128)(2,1)}, u32[]{:S(2)}, u32[]{:S(2)}) collective-permute-start(bf16[256,768]{1,0:T(8,128)(2,1)} %get-tuple-element.352), channel_id=1, source_target_pairs={{0,1},{1,0},{2,3},{3,2},{4,5},{5,4},{6,7},{7,6},{8,9},{9,8},{10,11... | collective-permute-start | bytes 1179656 | tf_op jit(solution)/shard_map/ppermute | solution.py:962
  230.7 0.5 copy-start.21
  230.8 1.2 copy-start.16
  232.2 191.0 %copy-start.11 = (f32[256,768]{1,0:T(8,128)S(1)}, f32[256,768]{1,0:T(8,128)}, u32[]{:S(2)}) copy-start(f32[256,768]{1,0:T(8,128)} %get-tuple-element.353) | copy-start | bytes 2359300
  239.4 183.7 %copy-start.17 = (f32[256]{0:T(256)S(1)}, f32[256]{0:T(256)}, u32[]{:S(2)}) copy-start(f32[256]{0:T(256)} %copy-done.16) | copy-start | bytes 3076
  239.4 183.7 %copy-start.19 = (f32[256]{0:T(256)S(1)}, f32[256]{0:T(256)}, u32[]{:S(2)}) copy-start(f32[256]{0:T(256)} %add_rsqrt_fusion) | copy-start | bytes 3076
  378.7 46.6 %copy-start.13 = (bf16[96,3072]{1,0:T(8,128)(2,1)S(1)}, bf16[96,3072]{1,0:T(8,128)(2,1)}, u32[]{:S(2)}) copy-start(bf16[96,3072]{1,0:T(8,128)(2,1)} %reduce-scatter.14.cloned.1.call-done) | copy-start | bytes 1769476
  379.8 45.5 %collective-permute-start.3 = (bf16[96,1536]{1,0:T(8,128)(2,1)S(1)}, bf16[96,1536]{1,0:T(8,128)(2,1)S(1)}, u32[]{:S(2)}, u32[]{:S(2)}) collective-permute-start(bf16[96,1536]{1,0:T(8,128)(2,1)S(1)} %split.32), channel_id=1, source_target_pairs={{0,2},{1,3},{2,0},{3,1},{4,6},{5,7},{6,4},{7,5},{8,10},{9,11},{10,... | collective-permute-start | bytes 884744 | tf_op jit(solution)/shard_map/ppermute | solution.py:973
Sparse Core Ops, SparseCore 0:
  156.4 39.9 reduce-scatter.9
  211.8 20.7 reduce-scatter.11
  235.9 49.1 reduce-scatter.15
  287.3 35.4 reduce-scatter.7
  326.0 52.6 reduce-scatter.13

commit v4 on v3

--- a/solution.py
+++ b/solution.py
@@ -671,8 +671,7 @@
     outputs_ref,
     mixed_ref,
     context_ref,
-    own_grad,
-    mate_grad,
+    mlp_grad,
     heads_grad,
     bias_grad,
     sums_ref,
@@ -778,14 +777,14 @@
     mixed_ref[...] = mixed_sum[1 - side].astype(bf16)
     outputs_ref[...] = hidden_ref[...] + mixed_sum[side] + vector_ref[3:4, :]
 
-    for level, grad in enumerate((own_grad, mate_grad)):
-
-        def weight_grads(c, carry, level=level, grad=grad):
+    for level in range(2):
+
+        def weight_grads(c, carry, level=level):
             units = pl.ds(pl.multiple_of(c * tile, tile), tile)
             slopes = slope_ref[level, c]
             both = jnp.concatenate([normed_ref[0], normed_ref[1]], axis=0)
-            grad[0, units, :] = contract_rows(slopes, both).astype(bf16)
-            grad[1, units, :] = contract_rows(active_ref[level, c], rounded[...]).astype(bf16)
+            mlp_grad[2 * level, units, :] = contract_rows(slopes, both).astype(bf16)
+            mlp_grad[2 * level + 1, units, :] = contract_rows(active_ref[level, c], rounded[...]).astype(bf16)
             bias_grad[level, c] = column_sum(slopes.astype(f32))
             return carry
 
@@ -822,14 +821,13 @@
             jax.ShapeDtypeStruct((rows, features), f32),
             jax.ShapeDtypeStruct((rows, features), bf16),
             jax.ShapeDtypeStruct(spread.shape, bf16),
-            jax.ShapeDtypeStruct(own.shape, bf16),
-            jax.ShapeDtypeStruct(own.shape, bf16),
+            jax.ShapeDtypeStruct((4, units, features), bf16),
             jax.ShapeDtypeStruct(heads.shape, bf16),
             jax.ShapeDtypeStruct((2, chunks, 1, 256), f32),
             jax.ShapeDtypeStruct((4, features), f32),
         ),
         in_specs=whole_specs(7) + [pl.BlockSpec(memory_space=pl.ANY)],
-        out_specs=tuple(whole_specs(9)),
+        out_specs=tuple(whole_specs(8)),
         scratch_shapes=[
             pltpu.VMEM((2 * rows, features), f32),
             pltpu.VMEM((2 * rows, features), bf16),
@@ -853,6 +851,409 @@
         ),
         name="by_rows",
     )(x, spread, heads, vectors, bias, own, mate, cotangent)
+
+
+def margin_plan(f, fsdp_count, part):
+    phase = lax.rem(f, 3)
+    above = f + 1 < fsdp_count
+    below = f > 0
+    sends = (
+        below & ((phase == 1) | ((phase == 2) & (part == 1))),
+        above & ((phase == 1) | ((phase == 0) & (part == 0))),
+    )
+    receives = (
+        above & ((phase == 0) | ((phase == 1) & (part == 1))),
+        below & ((phase == 2) | ((phase == 1) & (part == 0))),
+    )
+    return (sends, receives)
+
+
+def scatter_copies(f, t, fsdp_count, grads, firsts, seconds, one_send, one_recv, sends, recvs):
+    parity = lax.rem(f, 2)
+    partner = f + 1 - 2 * parity
+    place = f // 2
+    count = fsdp_count // 2
+
+    def first_copies():
+        return [
+            remote(
+                grad.at[:, :, 1 - parity], first, one_send.at[i], one_recv.at[i], partner, t
+            )
+            for i, (grad, first) in enumerate(zip(grads, firsts))
+        ]
+
+    def second_copies(i):
+        toward = lax.rem(f + 2 * i, fsdp_count)
+        return [
+            remote(
+                first.at[:, toward // 2],
+                second.at[place],
+                send.at[toward // 2],
+                recv.at[place],
+                toward,
+                t,
+            )
+            for first, second, send, recv in zip(firsts, seconds, sends, recvs)
+        ]
+
+    def start():
+        for handle in first_copies():
+            handle.start()
+
+    def add_first():
+        for handle in first_copies():
+            handle.wait_recv()
+        for grad, first in zip(grads, firsts):
+
+            def body(k, carry, grad=grad, first=first):
+                i, j = (k // count, lax.rem(k, count))
+                mine = grad[i, j, parity].astype(jnp.float32)
+                first[i, j] = (mine + first[i, j].astype(jnp.float32)).astype(jnp.bfloat16)
+                return carry
+
+            lax.fori_loop(0, grad.shape[0] * count, body, 0)
+
+        def send(i, carry):
+            for handle in second_copies(i):
+                handle.start()
+            return carry
+
+        lax.fori_loop(1, count, send, 0)
+
+    def finish(totals):
+        for first, total in zip(firsts, totals):
+            total[...] = first[:, place].astype(jnp.float32)
+
+        def body(i, carry):
+            source = lax.rem(f + fsdp_count - 2 * i, fsdp_count)
+            for first, second, send, recv, total in zip(firsts, seconds, sends, recvs, totals):
+                remote(
+                    first.at[:, place],
+                    second.at[source // 2],
+                    send.at[0],
+                    recv.at[source // 2],
+                    source,
+                    t,
+                ).wait_recv()
+                total[...] += second[source // 2].astype(jnp.float32)
+            return carry
+
+        lax.fori_loop(1, count, body, 0)
+
+        def drain(i, carry):
+            for handle in second_copies(i):
+                handle.wait_send()
+            return carry
+
+        lax.fori_loop(1, count, drain, 0)
+        for handle in first_copies():
+            handle.wait_send()
+
+    return (start, add_first, finish)
+
+
+def attend_back_kernel(
+    fsdp_count,
+    tp_count,
+    lengths_ref,
+    dspread_ref,
+    wide_ref,
+    pair_ref,
+    context_ref,
+    mlp_grad,
+    heads_grad,
+    mixed_ref,
+    dproj_ref,
+    mlp_total,
+    heads_total,
+    mixed_in,
+    sums_ref,
+    dcontext,
+    key_tiles,
+    value_tiles,
+    turned_tiles,
+    totals,
+    halo_out,
+    halo_in,
+    mlp_first,
+    mlp_second,
+    heads_first,
+    heads_second,
+    context_send,
+    context_recv,
+    mixed_send,
+    mixed_recv,
+    halo_send,
+    halo_recv,
+    one_send,
+    one_recv,
+    mlp_send,
+    mlp_recv,
+    heads_send,
+    heads_recv,
+):
+    f = lax.axis_index("fsdp")
+    t = lax.axis_index("tp")
+    bf16 = jnp.bfloat16
+    f32 = jnp.float32
+    rows = dspread_ref.shape[1]
+    heads = wide_ref.shape[0]
+    group = rows * tp_count
+    margin = (pair_ref.shape[0] - group) // 2
+    per_half = tp_count // 2
+    pair_width = heads * LANES
+    scale = 1.0 / math.sqrt(HD)
+    greet(fsdp_count, tp_count, f, t)
+
+    def context_copy(j):
+        toward = lax.rem(t + j, tp_count)
+        return remote(
+            dspread_ref.at[toward],
+            dcontext.at[t],
+            context_send.at[j],
+            context_recv.at[t],
+            f,
+            toward,
+        )
+
+    def context_start(j, carry):
+        context_copy(j).start()
+        return carry
+
+    lax.fori_loop(1, tp_count, context_start, 0)
+    start_grads, add_grads, finish_grads = scatter_copies(
+        f,
+        t,
+        fsdp_count,
+        (mlp_grad, heads_grad),
+        (mlp_first, heads_first),
+        (mlp_second, heads_second),
+        one_send,
+        one_recv,
+        (mlp_send, heads_send),
+        (mlp_recv, heads_recv),
+    )
+    start_grads()
+    dcontext[t] = dspread_ref[t]
+    mixed_copy = remote(
+        mixed_ref, mixed_in, mixed_send, mixed_recv, f, t + 1 - 2 * lax.rem(t, 2)
+    )
+
+    def clear(i, carry):
+        for head in range(heads):
+            totals[head, pl.ds(i * QB, QB), :] = jnp.zeros((QB, LANES), f32)
+        return carry
+
+    lax.fori_loop(0, pair_ref.shape[0] // QB, clear, 0)
+    add_grads()
+    lane = lax.broadcasted_iota(jnp.int32, (rows, LANES), 1)
+    tall = lax.broadcasted_iota(jnp.int32, (CLIP, LANES), 1)
+
+    def half(step, carry):
+        part = lax.rem(t // per_half + step, 2)
+        first, clip = block_clip(f, part, margin)
+        length = lengths_ref[clip]
+        for head in range(heads):
+            pair = pair_ref[pl.ds(first, CLIP), head * LANES : (head + 1) * LANES].astype(f32)
+            key_tiles[head] = head_tiles(pair, length).astype(bf16)
+            value_tiles[head] = jnp.where(
+                tall < HD, jnp.where(tall < 3, 1.0, 0.0), pair
+            ).astype(bf16)
+            turned_tiles[head] = pair.T.astype(bf16)
+
+        def block(i, inner):
+            within = lax.rem(lax.rem(t, per_half) + i, per_half)
+            index = part * per_half + within
+
+            @pl.when(index != t)
+            def _():
+                remote(
+                    dspread_ref.at[0],
+                    dcontext.at[index],
+                    context_send.at[0],
+                    context_recv.at[index],
+                    f,
+                    index,
+                ).wait_recv()
+
+            here = pl.ds(pl.multiple_of(index * rows, rows), rows)
+            empty = jnp.zeros((rows, HD), f32)
+
+            def two_tiles(ref, at):
+                return (
+                    ref[at + (slice(0, LANES),)].astype(f32),
+                    jnp.concatenate(
+                        [ref[at + (slice(LANES, LANES + HD),)].astype(f32), empty], axis=1
+                    ),
+                )
+
+            upstream = two_tiles(dcontext, (index, slice(None)))
+            forward = two_tiles(context_ref, (here,))
+            queries = []
+            for head in range(heads):
+                tile = upstream[head // 2]
+                odd = head % 2
+                kept = jnp.where((lane >= HD) if odd else (lane < HD), tile * forward[head // 2], 0.0)
+                delta = jnp.sum(kept, axis=1, keepdims=True) * scale
+                high, middle, low = three_parts(delta)
+                grad = (tile if odd else pltpu.roll(tile, HD, axis=1)) * scale
+                grad = jnp.where(
+                    lane >= HD,
+                    grad,
+                    jnp.where(
+                        lane == 0,
+                        -high,
+                        jnp.where(lane == 1, -middle, jnp.where(lane == 2, -low, 0.0)),
+                    ),
+                ).astype(bf16)
+                wide = wide_ref[head, here, :]
+                probs = jnp.exp(contract_cols(key_tiles[head], wide))
+                dscores = (probs * contract_cols(value_tiles[head], grad)).astype(bf16)
+                both = jnp.concatenate([dscores, probs.astype(bf16)], axis=1)
+                fold = jnp.concatenate(
+                    [
+                        jnp.where(lane < HD, wide.astype(f32), 0.0),
+                        jnp.where(lane < HD, 0.0, grad.astype(f32)),
+                    ],
+                    axis=0,
+                ).astype(bf16)
+                totals[head, pl.ds(first, CLIP), :] += jnp.dot(
+                    both, fold, preferred_element_type=f32
+                )
+                queries.append(
+                    jnp.dot(turned_tiles[head], dscores, preferred_element_type=f32).T
+                )
+            dproj_ref[here, pair_width : pair_width + LANES] = jnp.where(
+                lane < HD, queries[0], pltpu.roll(queries[1], HD, axis=1)
+            ).astype(bf16)
+            dproj_ref[here, pair_width + LANES :] = jnp.where(lane < HD, queries[2], 0.0).astype(
+                bf16
+            )
+            return inner
+
+        lax.fori_loop(0, per_half, block, 0)
+
+        @pl.when(step == 0)
+        def _():
+            mixed_copy.start()
+
+        return carry
+
+    lax.fori_loop(0, 2, half, 0)
+
+    def halo_copy(side, part):
+        return remote(
+            halo_out.at[side, part],
+            halo_in.at[side, part],
+            halo_send.at[side, part],
+            halo_recv.at[side, part],
+            f - 1 if side == 0 else f + 1,
+            t,
+        )
+
+    halves = group // QB
+    for part in range(halves):
+        sends, _ = margin_plan(f, fsdp_count, part)
+        for side in range(2):
+
+            @pl.when(sends[side])
+            def _(side=side, part=part):
+                base = (0 if side == 0 else margin + group) + part * QB
+                for head in range(heads):
+                    halo_out[side, part, head] = totals[head, pl.ds(base, QB), :].astype(bf16)
+                halo_copy(side, part).start()
+
+    for part in range(halves):
+        _, receives = margin_plan(f, fsdp_count, part)
+        here = pl.ds(margin + part * QB, QB)
+        for side in range(2):
+
+            @pl.when(receives[side])
+            def _(side=side, part=part, here=here):
+                halo_copy(side, part).wait_recv()
+                for head in range(heads):
+                    totals[head, here, :] += halo_in[side, part, head].astype(f32)
+
+        for head in range(heads):
+            dproj_ref[part * QB : (part + 1) * QB, head * LANES : (head + 1) * LANES] = (
+                totals[head, here, :] * (1.0 / scale)
+            ).astype(bf16)
+
+    def add_rows(i, carry):
+        return carry + column_sum(dproj_ref[pl.ds(i * rows, rows), :].astype(f32))
+
+    sums_ref[...] = lax.fori_loop(
+        0, tp_count, add_rows, jnp.zeros((1, dproj_ref.shape[1]), f32)
+    )
+    finish_grads((mlp_total, heads_total))
+    mixed_copy.wait()
+
+    def settle(j, carry):
+        context_copy(j).wait_send()
+        return carry
+
+    lax.fori_loop(1, tp_count, settle, 0)
+    for part in range(halves):
+        sends, _ = margin_plan(f, fsdp_count, part)
+        for side in range(2):
+
+            @pl.when(sends[side])
+            def _(side=side, part=part):
+                halo_copy(side, part).wait_send()
+
+
+def attend_back(
+    fsdp_count, tp_count, lengths, dspread, wide, pairs, context, mlp_grad, heads_grad, mixed
+):
+    bf16 = jnp.bfloat16
+    f32 = jnp.float32
+    heads, group, _ = wide.shape
+    _, rows, width = dspread.shape
+    count = fsdp_count // 2
+    depth, features = mlp_grad.shape[3:]
+    dma = pltpu.SemaphoreType.DMA
+    mlp_kinds = mlp_grad.shape[0]
+    return pl.pallas_call(
+        functools.partial(attend_back_kernel, fsdp_count, tp_count),
+        out_shape=(
+            jax.ShapeDtypeStruct((group, heads * LANES + 2 * LANES), bf16),
+            jax.ShapeDtypeStruct((mlp_kinds, depth, features), f32),
+            jax.ShapeDtypeStruct((tp_count, depth, width), f32),
+            jax.ShapeDtypeStruct(mixed.shape, bf16),
+            jax.ShapeDtypeStruct((1, heads * LANES + 2 * LANES), f32),
+        ),
+        in_specs=[pl.BlockSpec(memory_space=pltpu.SMEM)] + whole_specs(7),
+        out_specs=tuple(whole_specs(5)),
+        scratch_shapes=[
+            pltpu.VMEM((tp_count, rows, width), bf16),
+            pltpu.VMEM((heads, CLIP, LANES), bf16),
+            pltpu.VMEM((heads, CLIP, LANES), bf16),
+            pltpu.VMEM((heads, LANES, CLIP), bf16),
+            pltpu.VMEM((heads, pairs.shape[0], LANES), f32),
+            pltpu.VMEM((2, group // QB, heads, QB, LANES), bf16),
+            pltpu.VMEM((2, group // QB, heads, QB, LANES), bf16),
+            pltpu.VMEM((mlp_kinds, count, depth, features), bf16),
+            pltpu.VMEM((count, mlp_kinds, depth, features), bf16),
+            pltpu.VMEM((tp_count, count, depth, width), bf16),
+            pltpu.VMEM((count, tp_count, depth, width), bf16),
+            dma((tp_count,)),
+            dma((tp_count,)),
+            dma,
+            dma,
+            dma((2, group // QB)),
+            dma((2, group // QB)),
+            dma((2,)),
+            dma((2,)),
+            dma((count,)),
+            dma((count,)),
+            dma((count,)),
+            dma((count,)),
+        ],
+        compiler_params=pltpu.CompilerParams(
+            collective_id=5, has_side_effects=True, vmem_limit_bytes=VMEM_LIMIT
+        ),
+        name="attend_back",
+    )(lengths, dspread, wide, pairs, context, mlp_grad, heads_grad, mixed)
 
 
 def pack_columns(key, value, query):
@@ -918,36 +1319,13 @@
     spread, context, wide, mlp_other, out_full = attend(
         fsdp_count, tp_count, clip_lengths, query, pairs, mlp_own, out_parts, heads_here
     )
-    totals = -jnp.sum(wide[:, :, HD + 1 : HD + 4].astype(f32), axis=2)
-    query = query[:, :local_width]
     normed = normed.reshape(group_rows, -1)
     key_w, value_w = jnp.moveaxis(attention_w[:, :pair_width].reshape(-1, heads_here, 2, HD), 2, 0)
     key_w = key_w.reshape(-1, local_width)
     value_w = value_w.reshape(-1, local_width)
     query_w = attention_w[:, pair_width : pair_width + local_width]
-    padded = jnp.moveaxis(pairs.reshape(-1, heads_here, 2, HD), 2, 0).reshape(2, -1, local_width)
-    out_w = lax.dynamic_index_in_dim(out_full, tp_index, 0, False)
-    w_up, w_down = mlp_w
-    group_base = fsdp_index * group_rows
-    clip_ids = jnp.arange(clip_lengths.shape[0])
-    block_count = group_rows // QB
-
-    def block_scores(block_index):
-        first_row = block_index * QB
-        clip_index = (group_base + first_row) // CLIP
-        key_start = clip_index * CLIP - group_base + margin
-        length = jnp.sum(jnp.where(clip_ids == clip_index, clip_lengths, 0))
-        query_block = lax.dynamic_slice_in_dim(query, first_row, QB, 0).reshape(QB, heads_here, HD)
-        pair = lax.dynamic_slice_in_dim(padded, key_start, CLIP, 1).reshape(2, CLIP, heads_here, HD)
-        scores = (
-            jnp.einsum("qhe,khe->hqk", query_block, pair[0], preferred_element_type=f32)
-            * score_scale
-        )
-        scores = jnp.where((jnp.arange(CLIP) < length)[None, None, :], scores, far_negative)
-        return (first_row, key_start, query_block, pair[0], pair[1], scores)
-
     unit_bias = jnp.swapaxes(fc1_bias.reshape(fsdp_count, tp_count, unit_count), 0, 1)
-    dhidden, outputs, mixed, dspread, own_grad, mate_grad, heads_grad, bias_part, sums = by_rows(
+    dhidden, outputs, mixed, dspread, mlp_grad, heads_grad, bias_part, sums = by_rows(
         fsdp_count,
         tp_count,
         inputs,
@@ -959,72 +1337,37 @@
         mlp_other,
         out_cotangent,
     )
-    outputs = outputs + lax.ppermute(
-        mixed, "tp", [(i, i ^ 1) for i in range(tp_count)]
+    count = fsdp_count // 2
+    dproj, mlp_total, heads_total, mixed, proj_sums = attend_back(
+        fsdp_count,
+        tp_count,
+        clip_lengths,
+        dspread,
+        wide,
+        pairs,
+        context,
+        mlp_grad.reshape(4, count, 2, unit_count, -1),
+        heads_grad.reshape(tp_count, count, 2, unit_count, -1),
+        mixed,
+    )
+    outputs = outputs + mixed.astype(f32)
+    halves = [(i, (i + tp_count // 2) % tp_count) for i in range(tp_count)]
+    grad_fc1, grad_fc2 = mlp_total[:2] + lax.ppermute(
+        mlp_total[2:].astype(bf16), "tp", halves
     ).astype(f32)
-    halves = [(i, (i + tp_count // 2) % tp_count) for i in range(tp_count)]
-    grad_both = lax.psum_scatter(
-        jnp.concatenate([*own_grad, *mate_grad], axis=1),
-        "fsdp",
-        scatter_dimension=0,
-        tiled=True,
-    )
-    grad_own, grad_mate = jnp.split(grad_both, 2, axis=1)
-    grad_own = grad_own.astype(f32) + lax.ppermute(grad_mate, "tp", halves).astype(f32)
-    grad_fc1, grad_fc2 = jnp.split(grad_own, 2, axis=1)
-    grad_out = lax.psum_scatter(heads_grad, "fsdp", scatter_dimension=1, tiled=True)
-    grad_out = lax.psum_scatter(grad_out, "tp", scatter_dimension=0, tiled=True)[0].astype(f32)
+    grad_out = lax.psum_scatter(
+        heads_total.astype(bf16), "tp", scatter_dimension=0, tiled=True
+    )[0].astype(f32)
     grad_gain2, grad_shift2, grad_obias, grad_b2 = sums
     mate_index = (tp_index + tp_count // 2) % tp_count
     mate_slot = (jnp.arange(tp_count) == mate_index).astype(f32)
     bias_part = bias_part.reshape(2, -1)
     by_tp_sum = tp_slot[:, None] * bias_part[0] + mate_slot[:, None] * bias_part[1]
     grad_b1 = jnp.swapaxes(by_tp_sum.reshape(tp_count, fsdp_count, unit_count), 0, 1).reshape(-1)
-    dcontext = lax.all_to_all(dspread, "tp", 0, 0, tiled=False).reshape(group_rows, local_width)
-    delta = jnp.sum(
-        (dcontext.astype(f32) * context.astype(f32)).reshape(group_rows, heads_here, HD), axis=-1
-    ).T
-
-    def attend_back(block_index, carry):
-        dquery_rows, dpair = carry
-        first_row, key_start, query_block, key_block, value_block, scores = block_scores(
-            block_index
-        )
-        grad_block = lax.dynamic_slice_in_dim(dcontext, first_row, QB, 0).reshape(
-            QB, heads_here, HD
-        )
-        probs = jnp.exp(scores - lax.dynamic_slice_in_dim(totals, first_row, QB, 1)[..., None])
-        delta_block = lax.dynamic_slice_in_dim(delta, first_row, QB, 1)
-        dprobs = jnp.einsum("qhe,khe->hqk", grad_block, value_block, preferred_element_type=f32)
-        dscores = (probs * (dprobs - delta_block[..., None]) * score_scale).astype(bf16)
-        dquery_block = jnp.einsum("hqk,khe->qhe", dscores, key_block, preferred_element_type=f32)
-        dquery_block = dquery_block.astype(bf16).reshape(QB, local_width)
-        dkey_block = jnp.einsum(
-            "hqk,qhe->khe", dscores, query_block, preferred_element_type=f32
-        ).reshape(CLIP, local_width)
-        dvalue_block = jnp.einsum(
-            "hqk,qhe->khe", probs.astype(bf16), grad_block, preferred_element_type=f32
-        ).reshape(CLIP, local_width)
-        current = lax.dynamic_slice_in_dim(dpair, key_start, CLIP, 1)
-        dpair = lax.dynamic_update_slice_in_dim(
-            dpair, current + jnp.stack([dkey_block, dvalue_block]), key_start, 1
-        )
-        dquery_rows = lax.dynamic_update_slice_in_dim(dquery_rows, dquery_block, first_row, 0)
-        return (dquery_rows, dpair)
-
-    dquery, dpair = lax.fori_loop(
-        0,
-        block_count,
-        attend_back,
-        (jnp.zeros((group_rows, local_width), bf16), jnp.zeros(padded.shape, f32)),
-    )
-    rims = jnp.concatenate([dpair[:, :margin], dpair[:, margin + group_rows :]], axis=1)
-    received = extended(rims, (("fsdp", 1),), margin)
-    inner_part = dpair[:, margin : margin + group_rows]
-    inner_part = inner_part.at[:, :margin].add(received[:, :margin])
-    inner_part = inner_part.at[:, group_rows - margin :].add(received[:, 3 * margin :])
-    dkey = inner_part[0].astype(bf16)
-    dvalue = inner_part[1].astype(bf16)
+    dquery = dproj[:, pair_width : pair_width + local_width]
+    dkey, dvalue = jnp.moveaxis(dproj[:, :pair_width].reshape(-1, heads_here, 2, HD), 2, 0).reshape(
+        2, -1, local_width
+    )
     grad_query = contract_rows(normed, dquery)
     grad_key = contract_rows(normed, dkey)
     grad_value = contract_rows(normed, dvalue)

time: 434 us -> 359 us (0.83)
  waiting for transfers between devices: 143 us -> 83.9 us
  Pallas kernels: 125 us -> 176 us
  local copies, waits for them, and re-layouts: 45.9 us -> 22.8 us
  matrix products: 25 us -> 6.55 us
  other arithmetic: 28.3 us -> 13.2 us
  starting transfers between devices: 10.4 us -> 1.3 us
    pallas_call x0 -> x1, Pallas kernels: none -> 51.3 us  [attend_back(): pl.pallas_call(functools.partial(attend_back_kernel, fsdp_count, tp_count...]
    reduce_scatter x3 -> x1, waiting for transfers between devices: 54.5 us -> 10.8 us  [on_device(): lax.psum_scatter(heads_total.astype(bf16), 'tp', scatter_dimension=0, til...]
    dot_general x10 -> x0, matrix products: 18.8 us -> none  [the longest x2 6.89 us: attend_back(): jnp.einsum('qhe,khe->hqk', grad_block, value_block, preferred_element_typ...]
    ppermute x4 -> x1, waiting for transfers between devices: 8.07 us -> 0.82 us  [on_device(): lax.ppermute(mlp_total[2:].astype(bf16), 'tp', halves).astype(f32)]
    unnamed x6 -> x4, waiting for transfers between devices: 43.8 us -> 37.7 us
    ppermute x4 -> x1, starting transfers between devices: 6.3 us -> 1.18 us  [on_device(): lax.ppermute(mlp_total[2:].astype(bf16), 'tp', halves).astype(f32)]
    pallas_call x2 -> x0, local copies, waits for them, and re-layouts: 4.8 us -> none  [the longest x1 2.65 us: project(): pl.pallas_call(functools.partial(project_kernel, fsdp_count, tp_count), o...]
    unnamed x45 -> x31, local copies, waits for them, and re-layouts: 9.79 us -> 8.76 us
  transfers between devices with their start and end apart: 10 -> 4, of which waited for: 6 -> 4; matrix products, arithmetic and copies ran while one was open for 18% -> 6% of each run, Pallas kernels for 0% -> 0%
where the time goes in v4:
time: 359 us; the launch traced here: 358 us
  Pallas kernels  176 us (49%)
  waiting for transfers between devices  83.9 us (23%)
  blocking collectives  40.4 us (11%)
  local copies, waits for them, and re-layouts  22.8 us (6%)
  between operations  14 us (4%)
  other arithmetic  13.2 us (4%)
  matrix products  6.55 us (2%)
    pallas_call x1, Pallas kernels, attend_back(): pl.pallas_call(functools.partial(attend_back_kernel, fsdp_count, tp_count...  51.3 us
    pallas_call x1, Pallas kernels, project(): pl.pallas_call(functools.partial(project_kernel, fsdp_count, tp_count), o...  46.2 us
    pallas_call x1, Pallas kernels, attend(): pl.pallas_call(functools.partial(attend_kernel, fsdp_count, tp_count), ou...  43.8 us
    psum x1, blocking collectives, on_device(): lax.psum((grad_gain1, grad_shift1, grad_qbias, grad_vbias, grad_obias, gr...  40.4 us
    unnamed x4, waiting for transfers between devices  37.7 us
    reduce_scatter x1, waiting for transfers between devices, scatter_rows(): lax.psum_scatter(partial_rows.astype(jnp.bfloat16), axis, scatter_dimensi...  34.5 us
    pallas_call x1, Pallas kernels, by_rows(): pl.pallas_call(functools.partial(rows_kernel, fsdp_count, tp_count), out_...  34.5 us
    reduce_scatter x1, waiting for transfers between devices, on_device(): lax.psum_scatter(heads_total.astype(bf16), 'tp', scatter_dimension=0, til...  10.8 us
  transfers between devices with their start and end apart: 4, of which 4 were waited for; matrix products, arithmetic and copies ran while one was open for 6% of the time, Pallas kernels for 0%

profile of v4, /device:TPU:0, one launch (start us, length us, event | category | flops | bytes accessed | tf_op | source)
XLA Modules:
  0.0 358.0 jit_solution(5958004780415374611)
XLA Ops:
  7.2 0.9 copy.54
  8.2 0.9 copy.55
  9.1 0.1 copy.57
  9.2 0.8 stack_reshape_reshape.3
  10.0 0.1 reshape.169
  10.1 0.8 reshape.170
  10.9 1.3 reshape.166.gain_ref
  12.1 1.3 reshape.167.shift_ref
  13.4 0.8 reshape.171
  14.2 0.7 reshape.172.bias_ref
  14.9 0.7 stack.35
  15.6 0.7 stack.36
  16.3 0.7 stack.37
  17.0 0.7 stack.38
  17.6 1.7 pad_maximum_fusion.1.mlp_ref
  19.4 0.1 pad.15.clone
  19.5 0.7 maximum_bitcast_fusion.weight_ref
  20.2 0.6 maximum_maximum_fusion.bias_ref
  20.8 46.2 %project.1 = (bf16[1024,256]{1,0:T(8,128)(2,1)}, bf16[3072,384]{1,0:T(8,128)(2,1)}, bf16[4,256,768]{2,1,0:T(8,128)(2,1)}, bf16[1,768,640]{2,1,0:T(8,128)(2,1)}, ...) custom-call(f32[256,768]{1,0:T(8,128)} %x_ref.3, f32[1,768]{1,0:T(1,128)} %reshape.166.gain_ref, ...), custom_call_target="tpu_custom_call" | custom-call | tf_op jit(solution)/shard_map/project/pallas_call | solution.py:403
  67.1 43.8 %attend.1 = (bf16[4,256,192]{2,1,0:T(8,128)(2,1)}, bf16[1024,192]{1,0:T(8,128)(2,1)}, bf16[3,1024,128]{2,1,0:T(8,128)(2,1)}, bf16[2,768,768]{2,1,0:T(8,128)(2,1)}, bf16[4,768,192]{2,1,0:T(8,128)(2,1)}) custom-call(s32[6]{0:T(128)} %lengths_ref.3, bf16[1024,256]{1,0:T(8,128)(2,1)} %get-tuple-element.40.query_ref, ...), custom_call_target="tpu_custom_call" | custom-call | tf_op jit(solution)/shard_map/attend/pallas_call | solution.py:624
  110.8 0.6 pad_maximum_fusion.3.vector_ref
  111.4 34.5 %by_rows.1 = (f32[256,768]{1,0:T(8,128)}, f32[256,768]{1,0:T(8,128)}, bf16[256,768]{1,0:T(8,128)(2,1)}, bf16[4,256,192]{2,1,0:T(8,128)(2,1)}, bf16[4,768,768]{2,...) custom-call(f32[256,768]{1,0:T(8,128)} %x_ref.3, ...), custom_call_target="tpu_custom_call" | custom-call | tf_op jit(solution)/shard_map/by_rows/pallas_call | solution.py:817
  145.9 51.3 %attend_back.1 = (bf16[1024,640]{1,0:T(8,128)(2,1)}, f32[4,96,768]{2,1,0:T(8,128)}, f32[4,96,192]{2,1,0:T(8,128)}, bf16[256,768]{1,0:T(8,128)(2,1)}, f32[1,640]{1,0:T(1,128)}) custom-call(s32[6]{0:T(128)} %lengths_ref.3, bf16[4,256,192]{2,1,0:T(8,128)(2,1)} %get-tuple-element.48.dspread_ref, bf16[3,1024,128]{2,1,0:T(8,128)(2,1)} %get-tuple-element.49.wide_ref, ...), custom_call_target="tpu_custom_call" | custom-call | tf_op jit(solution)/shard_map/attend_back/pallas_call | solution.py:1216
  197.3 1.7 convert_element_type.54
  199.0 1.2 slice.31
  200.2 0.3 copy.59
  200.7 1.3 copy-done.1
  201.9 1.6 convolution_convert_fusion.2
  203.5 0.5 convolution_convert_fusion
  204.0 0.5 convolution_convert_fusion.1
  204.6 1.3 copy.66
  206.0 0.3 copy.61
  206.4 0.6 fusion.14
  207.0 0.7 copy-done.2
  207.7 1.6 fusion.10
  209.3 1.8 fusion
  211.1 1.9 slice.51
  213.0 1.2 collective-permute-start
  214.2 0.1 reduce_sum.72
  214.4 0.1 mul.130
  214.5 0.1 mul.134
  214.5 0.1 multiply_add_fusion
  214.6 0.1 add.78
  214.7 0.1 convert_reduce_fusion.2
  214.8 0.1 mul.125
  214.9 0.2 convert_reduce_fusion.1
  215.2 0.1 mul.124
  215.3 0.2 multiply_reduce_fusion
  215.6 0.4 copy-done.5
  216.0 0.9 convert_add_fusion
  217.0 10.8 %reduce-scatter.8.cloned.1.call-done = bf16[1,96,192]{2,1,0:T(8,128)(2,1)} async-done(((bf16[4,96,192]{2,1,0:T(8,128)(2,1)}), bf16[1,96,192]{2,1,0:T(8,128)(2,1)}) %reduce-scatter.8.cloned.1.call-update) | async-done | bytes 36880 | tf_op jit(solution)/shard_map/reduce_scatter | solution.py:1358
  227.7 1.4 bitcast_convert_fusion
  229.2 0.8 collective-permute-done
  230.0 1.0 convert_add_fusion.1
  231.0 0.8 slice_bitcast_fusion
  231.9 37.7 %reduce-scatter.10.cloned.1.call-done = bf16[96,576]{1,0:T(8,128)(2,1)} async-done(((bf16[768,576]{1,0:T(8,128)(2,1)}), bf16[96,576]{1,0:T(8,128)(2,1)}) %reduce-scatter.10.cloned.1.call-update) | async-done | bytes 110608
  269.6 1.0 copy.67
  270.7 0.7 copy.63
  271.4 0.7 copy.64
  272.1 0.7 copy.65
  272.9 34.5 %reduce-scatter.6.cloned.1.call-done = bf16[256,768]{1,0:T(8,128)(2,1)} async-done(((bf16[1024,768]{1,0:T(8,128)(2,1)}), bf16[256,768]{1,0:T(8,128)(2,1)}) %reduce-scatter.6.cloned.1.call-update) | async-done | bytes 393232 | tf_op jit(solution)/shard_map/reduce_scatter | solution.py:76
  307.4 1.4 fusion.8
  308.8 40.4 %all-reduce.1 = (f32[768]{0:T(1024)}, f32[768]{0:T(1024)}, f32[768]{0:T(1024)}, f32[768]{0:T(1024)}, f32[768]{0:T(1024)}, /*index=5*/f32[768]{0:T(1024)}, f32[768]{0:T(1024)}, f32[3072]{0:T(1024)}, f32[768]{0:T(1024)}) all-reduce(f32[768]{0:T(1024)S(1)} %get-tuple-element.114, ...), channel_id=1, replica_groups=mesh['fsdp'=8,'tp'=4] {'fsdp','tp'}, use_global_device_ids=true, to_apply=%region_6.7 | all-reduce | flops 9216 | bytes 73728 | tf_op jit(solution)/shard_map/psum | solution.py:1400
  349.3 2.2 fusion.6
  (48 shorter events, 0.9 us)
Async XLA Ops:
  7.2 12.3 %copy-start.8 = (bf16[96,192]{1,0:T(8,128)(2,1)S(1)}, bf16[96,192]{1,0:T(8,128)(2,1)}, u32[]{:S(2)}) copy-start(bf16[96,192]{1,0:T(8,128)(2,1)} %param.23) | copy-start | bytes 110596
  7.2 220.5 %reduce-scatter.8.cloned.1.call-start = ((), (), s32[]{:S(2)}) async-start(), calls=%async_computation.4 | async-start | bytes 245760 | tf_op jit(solution)/shard_map/reduce_scatter | solution.py:1358
  199.0 70.6 %reduce-scatter.10.cloned.1.call-start = ((), (), s32[]{:S(2)}) async-start(), calls=%async_computation.5 | async-start | bytes 1105920
  200.5 1.4 copy-start.1
  204.6 1.4 copy-start.3
  205.9 101.5 %reduce-scatter.6.cloned.1.call-start = ((), (), s32[]{:S(2)}) async-start(), calls=%async_computation.3 | async-start | bytes 1966080 | tf_op jit(solution)/shard_map/reduce_scatter | solution.py:76
  206.3 1.3 copy-start.2
  211.1 3.1 copy-start
  211.1 3.3 copy-start.11
  211.1 4.4 %copy-start.7 = (bf16[256,768]{1,0:T(8,128)(2,1)S(1)}, bf16[256,768]{1,0:T(8,128)(2,1)}, u32[]{:S(2)}) copy-start(bf16[256,768]{1,0:T(8,128)(2,1)} %get-tuple-element.54) | copy-start | bytes 1179652
  213.0 17.0 %collective-permute-start = (bf16[2,96,768]{2,1,0:T(8,128)(2,1)}, bf16[2,96,768]{2,1,0:T(8,128)(2,1)}, u32[]{:S(2)}, u32[]{:S(2)}) collective-permute-start(bf16[2,96,768]{2,1,0:T(8,128)(2,1)} %slice.51), channel_id=1, source_target_pairs={{0,2},{1,3},{2,0},{3,1},{4,6},{5,7},{6,4},{7,5},{8,10},{9,11},{10,... | collective-permute-start | bytes 884744 | tf_op jit(solution)/shard_map/ppermute | solution.py:1355
  214.8 1.1 copy-start.5
  214.9 2.0 copy-start.10
  215.1 14.9 %copy-start.6 = (f32[4,96,768]{2,1,0:T(8,128)S(1)}, f32[4,96,768]{2,1,0:T(8,128)}, u32[]{:S(2)}) copy-start(f32[4,96,768]{2,1,0:T(8,128)} %get-tuple-element.61) | copy-start | bytes 3538948
  231.0 76.4 %copy-start.9 = (f32[768]{0:T(1024)S(1)}, f32[768]{0:T(1024)}, u32[]{:S(2)}) copy-start(f32[768]{0:T(1024)} %param.21) | copy-start | bytes 9220
  231.9 117.4 %copy-start.4 = (f32[256,768]{1,0:T(8,128)S(1)}, f32[256,768]{1,0:T(8,128)}, u32[]{:S(2)}) copy-start(f32[256,768]{1,0:T(8,128)} %get-tuple-element.55) | copy-start | bytes 2359300
Sparse Core Ops, SparseCore 0:
  199.1 28.6 reduce-scatter.7
  231.0 38.5 reduce-scatter.9
  271.9 35.4 reduce-scatter.5

commit v5 on v4

--- a/solution.py
+++ b/solution.py
@@ -19,19 +19,6 @@
 far_negative = -1e30
 
 
-def extended(value, sides, width):
-    for axis, dim in sides:
-        size, length = (lax.axis_size(axis), value.shape[dim])
-        up = [(i, (i + 1) % size) for i in range(size - 1)]
-        down = [(j, i) for i, j in up]
-        last = lax.slice_in_dim(value, length - width, length, axis=dim)
-        initial = lax.slice_in_dim(value, 0, width, axis=dim)
-        before = lax.ppermute(last, axis, up)
-        after = lax.ppermute(initial, axis, down)
-        value = jnp.concatenate([before, value, after], axis=dim)
-    return value
-
-
 def normalize(rows, gain, shift):
     centre = jnp.mean(rows, axis=-1, keepdims=True)
     centred = rows - centre
@@ -49,17 +36,6 @@
     )
 
 
-def gelu_exact(values):
-    return 0.5 * values * (1.0 + lax.erf(values * root_half))
-
-
-def gelu_slope(values):
-    return (
-        0.5 * (1.0 + lax.erf(values * root_half))
-        + values * jnp.exp(-0.5 * values * values) * inv_root_tau
-    )
-
-
 def contract_rows(left_rows, right_rows):
     return lax.dot_general(
         left_rows, right_rows, (((0,), (0,)), ((), ())), preferred_element_type=jnp.float32
@@ -70,12 +46,6 @@
     return lax.dot_general(
         left_rows, right_rows, (((1,), (1,)), ((), ())), preferred_element_type=jnp.float32
     )
-
-
-def scatter_rows(partial_rows, axis):
-    return lax.psum_scatter(
-        partial_rows.astype(jnp.bfloat16), axis, scatter_dimension=0, tiled=True
-    ).astype(jnp.float32)
 
 
 MESH = pl.DeviceIdType.MESH
@@ -1256,6 +1226,416 @@
     )(lengths, dspread, wide, pairs, context, mlp_grad, heads_grad, mixed)
 
 
+def reduce_copies(f, t, fsdp_count, tp_count, vector, by_fsdp, by_tp, sends, recvs):
+    def fsdp_copy(i):
+        return remote(
+            vector, by_fsdp.at[f], sends.at[i], recvs.at[f], lax.rem(f + i, fsdp_count), t
+        )
+
+    def tp_copy(j):
+        return remote(
+            by_tp.at[t],
+            by_tp.at[t],
+            sends.at[fsdp_count + j],
+            recvs.at[fsdp_count + t],
+            f,
+            lax.rem(t + j, tp_count),
+        )
+
+    def start():
+        def body(i, carry):
+            fsdp_copy(i).start()
+            return carry
+
+        by_fsdp[f] = vector[...]
+        lax.fori_loop(1, fsdp_count, body, 0)
+
+    def middle():
+        def wait(i, carry):
+            source = lax.rem(f + i, fsdp_count)
+            remote(
+                vector, by_fsdp.at[source], sends.at[i], recvs.at[source], source, t
+            ).wait_recv()
+            return carry
+
+        def add(i, total):
+            return total + by_fsdp[i]
+
+        def body(j, carry):
+            tp_copy(j).start()
+            return carry
+
+        lax.fori_loop(1, fsdp_count, wait, 0)
+        by_tp[t] = lax.fori_loop(0, fsdp_count, add, jnp.zeros(vector.shape, jnp.float32))
+        lax.fori_loop(1, tp_count, body, 0)
+
+    def finish():
+        def wait(j, carry):
+            source = lax.rem(t + j, tp_count)
+            remote(
+                vector,
+                by_tp.at[source],
+                sends.at[fsdp_count + j],
+                recvs.at[fsdp_count + source],
+                f,
+                source,
+            ).wait_recv()
+            tp_copy(j).wait_send()
+            return carry
+
+        def drain(i, carry):
+            fsdp_copy(i).wait_send()
+            return carry
+
+        lax.fori_loop(1, tp_count, wait, 0)
+        lax.fori_loop(1, fsdp_count, drain, 0)
+
+    return (start, middle, finish)
+
+
+def finish_kernel(
+    fsdp_count,
+    tp_count,
+    x_ref,
+    gain_ref,
+    shift_ref,
+    dproj_ref,
+    full_ref,
+    normed_ref,
+    gradient_ref,
+    partial_ref,
+    mixed_ref,
+    mlp_ref,
+    heads_ref,
+    sums_ref,
+    bias_ref,
+    proj_ref,
+    inputs_grad,
+    outputs_ref,
+    weight_total,
+    mlp_total,
+    heads_total,
+    late_total,
+    early_total,
+    proj_total,
+    bias_total,
+    weight_grad,
+    weight_first,
+    weight_second,
+    weight_sum,
+    part_ref,
+    row_out,
+    row_in,
+    mlp_out,
+    mlp_in,
+    heads_out,
+    heads_in,
+    early,
+    early_fsdp,
+    early_tp,
+    late,
+    late_fsdp,
+    late_tp,
+    row_send,
+    row_recv,
+    side_send,
+    side_recv,
+    one_send,
+    one_recv,
+    weight_send,
+    weight_recv,
+    early_send,
+    early_recv,
+    late_send,
+    late_recv,
+):
+    f = lax.axis_index("fsdp")
+    t = lax.axis_index("tp")
+    bf16 = jnp.bfloat16
+    f32 = jnp.float32
+    rows, features = x_ref.shape
+    proj_width = dproj_ref.shape[1]
+    last = tp_count - 1
+    units = bias_ref.shape[3]
+    early[0:4, :] = sums_ref[...]
+    early[4:5, :] = jnp.zeros((1, features), f32)
+    early[4:5, 0:proj_width] = proj_ref[...]
+    for level in range(2):
+        for c in range(bias_ref.shape[1]):
+            early[5 + level : 6 + level, c * units : (c + 1) * units] = bias_ref[level, c]
+    mlp_out[...] = mlp_ref[2:4].astype(bf16)
+    heads_out[...] = heads_ref[...].astype(bf16)
+    greet(fsdp_count, tp_count, f, t)
+    start_early, middle_early, finish_early = reduce_copies(
+        f, t, fsdp_count, tp_count, early, early_fsdp, early_tp, early_send, early_recv
+    )
+    start_late, middle_late, finish_late = reduce_copies(
+        f, t, fsdp_count, tp_count, late, late_fsdp, late_tp, late_send, late_recv
+    )
+    start_weights, add_weights, finish_weights = scatter_copies(
+        f,
+        t,
+        fsdp_count,
+        (weight_grad,),
+        (weight_first,),
+        (weight_second,),
+        one_send,
+        one_recv,
+        (weight_send,),
+        (weight_recv,),
+    )
+
+    def row_copy(block, side):
+        return remote(
+            row_out.at[block],
+            row_in.at[side, block],
+            row_send.at[block],
+            row_recv.at[side, block],
+            f,
+            t + 1 if side == 0 else t - 1,
+        )
+
+    def partial_rows(k, carry):
+        block = jnp.where(t < tp_count // 2, last - k, k)
+        product = contract_cols(
+            dproj_ref[pl.ds(pl.multiple_of(block * rows, rows), rows), :], full_ref[0]
+        )
+        part_ref[block] = product
+
+        @pl.when((t == 0) & (block > t))
+        def _():
+            row_out[block] = product.astype(bf16)
+            row_copy(block, 0).start()
+
+        @pl.when((t == last) & (block < t))
+        def _():
+            row_out[block] = product.astype(bf16)
+            row_copy(block, 1).start()
+
+        return carry
+
+    lax.fori_loop(0, tp_count, partial_rows, 0)
+    start_early()
+    depth = weight_grad.shape[3]
+
+    mlp_copy = remote(
+        mlp_out, mlp_in, side_send.at[0], side_recv.at[0], f, lax.rem(t + tp_count // 2, tp_count)
+    )
+    mlp_copy.start()
+
+    def heads_copy(j):
+        toward = lax.rem(t + j, tp_count)
+        return remote(
+            heads_out.at[toward],
+            heads_in.at[t],
+            side_send.at[j],
+            side_recv.at[tp_count + t],
+            f,
+            toward,
+        )
+
+    def heads_start(j, carry):
+        heads_copy(j).start()
+        return carry
+
+    lax.fori_loop(1, tp_count, heads_start, 0)
+    tall = 256
+
+    def weight_part(c, carry):
+        columns = pl.ds(pl.multiple_of(c * tall, tall), tall)
+        total = jnp.zeros((tall, proj_width), f32)
+        for block in range(tp_count):
+            total = total + contract_rows(
+                normed_ref[block, :, columns],
+                dproj_ref[block * rows : (block + 1) * rows, :],
+            )
+        weight_sum[columns, :] = total.astype(bf16)
+        return carry
+
+    lax.fori_loop(0, features // tall, weight_part, 0)
+
+    def arrange(i, carry):
+        weight_grad[0, i // 2, lax.rem(i, 2)] = weight_sum[
+            pl.ds(pl.multiple_of(i * depth, 8), depth), :
+        ]
+        return carry
+
+    lax.fori_loop(0, fsdp_count, arrange, 0)
+    start_weights()
+    outputs_ref[...] = partial_ref[...] + mixed_ref[...].astype(f32)
+    unit, spread, _ = normalize(x_ref[...], gain_ref[...], shift_ref[...])
+    add_weights()
+    middle_early()
+
+    def relay(k, carry):
+        for side, (block, valid) in enumerate(
+            ((last - k, (last - k > t) & (t > 0)), (k, (k < t) & (t < last)))
+        ):
+
+            @pl.when(valid)
+            def _(side=side, block=block):
+                row_copy(block, side).wait_recv()
+                row_out[block] = (part_ref[block] + row_in[side, block].astype(f32)).astype(bf16)
+                row_copy(block, side).start()
+
+        return carry
+
+    lax.fori_loop(0, last, relay, 0)
+    finish_weights((weight_total,))
+    heads_total[...] = heads_ref[t]
+
+    def heads_done(j, carry):
+        source = lax.rem(t + j, tp_count)
+        remote(
+            heads_out.at[source],
+            heads_in.at[source],
+            side_send.at[j],
+            side_recv.at[tp_count + source],
+            f,
+            source,
+        ).wait_recv()
+        heads_total[...] += heads_in[source].astype(f32)
+        heads_copy(j).wait_send()
+        return carry
+
+    lax.fori_loop(1, tp_count, heads_done, 0)
+    mlp_copy.wait()
+    mlp_total[...] = mlp_ref[0:2] + mlp_in[...].astype(f32)
+    finish_early()
+    early_total[...] = jnp.sum(early_tp[:, 0:4, :], axis=0)
+    for j in range(tp_count):
+        proj_total[j : j + 1, :] = early_tp[j, 4:5, 0:proj_width]
+        bias_total[j : j + 1, :] = (
+            early_tp[j, 5:6, :] + early_tp[(j + tp_count // 2) % tp_count, 6:7, :]
+        )
+
+    @pl.when(t > 0)
+    def _():
+        row_copy(t, 0).wait_recv()
+        part_ref[t] += row_in[0, t].astype(f32)
+
+    @pl.when(t < last)
+    def _():
+        row_copy(t, 1).wait_recv()
+        part_ref[t] += row_in[1, t].astype(f32)
+
+    dnorm = part_ref[t]
+    late[0:1, :] = column_sum(dnorm * unit)
+    late[1:2, :] = column_sum(dnorm)
+    start_late()
+    inputs_grad[...] = gradient_ref[...] + norm_back(dnorm, unit, spread, gain_ref[...])
+    middle_late()
+
+    def settle(block, carry):
+        @pl.when(block > t)
+        def _():
+            row_copy(block, 0).wait_send()
+
+        @pl.when(block < t)
+        def _():
+            row_copy(block, 1).wait_send()
+
+        return carry
+
+    lax.fori_loop(0, tp_count, settle, 0)
+    finish_late()
+    late_total[...] = jnp.sum(late_tp[...], axis=0)
+
+
+def finish(
+    fsdp_count,
+    tp_count,
+    x,
+    gain,
+    shift,
+    dproj,
+    full,
+    normed,
+    gradient,
+    partial,
+    mixed,
+    mlp,
+    heads,
+    sums,
+    bias,
+    proj,
+):
+    bf16 = jnp.bfloat16
+    f32 = jnp.float32
+    rows, features = x.shape
+    _, depth, width = heads.shape
+    proj_width = dproj.shape[1]
+    count = fsdp_count // 2
+    dma = pltpu.SemaphoreType.DMA
+    peers = fsdp_count + tp_count
+    return pl.pallas_call(
+        functools.partial(finish_kernel, fsdp_count, tp_count),
+        out_shape=(
+            jax.ShapeDtypeStruct((rows, features), f32),
+            jax.ShapeDtypeStruct((rows, features), f32),
+            jax.ShapeDtypeStruct((1, depth, proj_width), f32),
+            jax.ShapeDtypeStruct((2, depth, features), f32),
+            jax.ShapeDtypeStruct((depth, width), f32),
+            jax.ShapeDtypeStruct((2, features), f32),
+            jax.ShapeDtypeStruct((4, features), f32),
+            jax.ShapeDtypeStruct((tp_count, proj_width), f32),
+            jax.ShapeDtypeStruct((tp_count, features), f32),
+        ),
+        in_specs=whole_specs(14),
+        out_specs=tuple(whole_specs(9)),
+        scratch_shapes=[
+            pltpu.VMEM((1, count, 2, depth, proj_width), bf16),
+            pltpu.VMEM((1, count, depth, proj_width), bf16),
+            pltpu.VMEM((count, 1, depth, proj_width), bf16),
+            pltpu.VMEM((features, proj_width), bf16),
+            pltpu.VMEM((tp_count, rows, features), f32),
+            pltpu.VMEM((tp_count, rows, features), bf16),
+            pltpu.VMEM((2, tp_count, rows, features), bf16),
+            pltpu.VMEM((2, depth, features), bf16),
+            pltpu.VMEM((2, depth, features), bf16),
+            pltpu.VMEM((tp_count, depth, width), bf16),
+            pltpu.VMEM((tp_count, depth, width), bf16),
+            pltpu.VMEM((7, features), f32),
+            pltpu.VMEM((fsdp_count, 7, features), f32),
+            pltpu.VMEM((tp_count, 7, features), f32),
+            pltpu.VMEM((2, features), f32),
+            pltpu.VMEM((fsdp_count, 2, features), f32),
+            pltpu.VMEM((tp_count, 2, features), f32),
+            dma((tp_count,)),
+            dma((2, tp_count)),
+            dma((tp_count,)),
+            dma((2 * tp_count,)),
+            dma((1,)),
+            dma((1,)),
+            dma((count,)),
+            dma((count,)),
+            dma((peers,)),
+            dma((peers,)),
+            dma((peers,)),
+            dma((peers,)),
+        ],
+        compiler_params=pltpu.CompilerParams(
+            collective_id=6, has_side_effects=True, vmem_limit_bytes=VMEM_LIMIT
+        ),
+        name="finish",
+    )(
+        x,
+        gain,
+        shift,
+        dproj,
+        full,
+        normed,
+        gradient,
+        partial,
+        mixed,
+        mlp,
+        heads,
+        sums,
+        bias,
+        proj,
+    )
+
+
 def pack_columns(key, value, query):
     lead = key.shape[:-1]
     heads = key.shape[-1] // HD
@@ -1284,18 +1664,10 @@
     fc2_weight,
     fc2_bias,
 ):
-    bf16 = jnp.bfloat16
     f32 = jnp.float32
     tp_count = lax.axis_size("tp")
     fsdp_count = lax.axis_size("fsdp")
-    tp_index = lax.axis_index("tp")
-    fsdp_index = lax.axis_index("fsdp")
-    own_rows = inputs.shape[0]
-    group_rows = out_cotangent.shape[0]
-    score_scale = 1.0 / math.sqrt(HD)
     margin = CLIP - QB
-    tp_slot = (jnp.arange(tp_count) == tp_index).astype(f32)
-    unit1, spread1, _ = normalize(inputs, norm1_gain, norm1_shift)
     local_width = query_weight.shape[1]
     heads_here = local_width // HD
     unit_count = fc1_weight.shape[0]
@@ -1315,15 +1687,9 @@
         pair_width,
         margin,
     )
-    attention_w = attention_w[0]
     spread, context, wide, mlp_other, out_full = attend(
         fsdp_count, tp_count, clip_lengths, query, pairs, mlp_own, out_parts, heads_here
     )
-    normed = normed.reshape(group_rows, -1)
-    key_w, value_w = jnp.moveaxis(attention_w[:, :pair_width].reshape(-1, heads_here, 2, HD), 2, 0)
-    key_w = key_w.reshape(-1, local_width)
-    value_w = value_w.reshape(-1, local_width)
-    query_w = attention_w[:, pair_width : pair_width + local_width]
     unit_bias = jnp.swapaxes(fc1_bias.reshape(fsdp_count, tp_count, unit_count), 0, 1)
     dhidden, outputs, mixed, dspread, mlp_grad, heads_grad, bias_part, sums = by_rows(
         fsdp_count,
@@ -1350,67 +1716,42 @@
         heads_grad.reshape(tp_count, count, 2, unit_count, -1),
         mixed,
     )
-    outputs = outputs + mixed.astype(f32)
-    halves = [(i, (i + tp_count // 2) % tp_count) for i in range(tp_count)]
-    grad_fc1, grad_fc2 = mlp_total[:2] + lax.ppermute(
-        mlp_total[2:].astype(bf16), "tp", halves
-    ).astype(f32)
-    grad_out = lax.psum_scatter(
-        heads_total.astype(bf16), "tp", scatter_dimension=0, tiled=True
-    )[0].astype(f32)
-    grad_gain2, grad_shift2, grad_obias, grad_b2 = sums
-    mate_index = (tp_index + tp_count // 2) % tp_count
-    mate_slot = (jnp.arange(tp_count) == mate_index).astype(f32)
-    bias_part = bias_part.reshape(2, -1)
-    by_tp_sum = tp_slot[:, None] * bias_part[0] + mate_slot[:, None] * bias_part[1]
-    grad_b1 = jnp.swapaxes(by_tp_sum.reshape(tp_count, fsdp_count, unit_count), 0, 1).reshape(-1)
-    dquery = dproj[:, pair_width : pair_width + local_width]
-    dkey, dvalue = jnp.moveaxis(dproj[:, :pair_width].reshape(-1, heads_here, 2, HD), 2, 0).reshape(
-        2, -1, local_width
-    )
-    grad_query = contract_rows(normed, dquery)
-    grad_key = contract_rows(normed, dkey)
-    grad_value = contract_rows(normed, dvalue)
-    grad_qbias = (tp_slot[:, None] * jnp.sum(dquery.astype(f32), axis=0)[None, :]).reshape(-1)
-    grad_vbias = (tp_slot[:, None] * jnp.sum(dvalue.astype(f32), axis=0)[None, :]).reshape(-1)
-    dnorm1 = scatter_rows(
-        contract_cols(dquery, query_w)
-        + contract_cols(dkey, key_w)
-        + contract_cols(dvalue, value_w),
-        "tp",
-    )
-    grad_gain1 = jnp.sum(dnorm1 * unit1, axis=0)
-    grad_shift1 = jnp.sum(dnorm1, axis=0)
-    inputs_grad = dhidden + norm_back(dnorm1, unit1, spread1, norm1_gain)
-    grad_query, grad_key, grad_value = jnp.split(
-        scatter_rows(jnp.concatenate([grad_query, grad_key, grad_value], axis=1), "fsdp"),
-        3,
-        axis=1,
-    )
-    (
-        grad_gain1,
-        grad_shift1,
-        grad_qbias,
-        grad_vbias,
-        grad_obias,
-        grad_gain2,
-        grad_shift2,
-        grad_b1,
-        grad_b2,
-    ) = lax.psum(
-        (
-            grad_gain1,
-            grad_shift1,
-            grad_qbias,
-            grad_vbias,
-            grad_obias,
-            grad_gain2,
-            grad_shift2,
-            grad_b1,
-            grad_b2,
-        ),
-        ("fsdp", "tp"),
-    )
+    inputs_grad, outputs, weight_total, mlp_total, grad_out, late, early, proj_total, bias_total = (
+        finish(
+            fsdp_count,
+            tp_count,
+            inputs,
+            norm1_gain.reshape(1, -1),
+            norm1_shift.reshape(1, -1),
+            dproj,
+            attention_w,
+            normed,
+            dhidden,
+            outputs,
+            mixed,
+            mlp_total,
+            heads_total,
+            sums,
+            bias_part,
+            proj_sums,
+        )
+    )
+    grad_gain1, grad_shift1 = late
+    grad_gain2, grad_shift2, grad_obias, grad_b2 = early
+    grad_fc1, grad_fc2 = mlp_total
+    grad_b1 = jnp.swapaxes(bias_total.reshape(tp_count, fsdp_count, unit_count), 0, 1).reshape(-1)
+
+    def unpack_columns(values):
+        lead = values.shape[0]
+        pair = values[:, :pair_width].reshape(lead, heads_here, 2, HD)
+        return (
+            pair[:, :, 0].reshape(lead, local_width),
+            pair[:, :, 1].reshape(lead, local_width),
+            values[:, pair_width : pair_width + local_width],
+        )
+
+    grad_key, grad_value, grad_query = unpack_columns(weight_total[0])
+    _, grad_vbias, grad_qbias = (part.reshape(-1) for part in unpack_columns(proj_total))
     return (
         outputs,
         inputs_grad,

time: 359 us -> 281 us (0.78)
  waiting for transfers between devices: 83.9 us -> 0 us
  Pallas kernels: 176 us -> 250 us
  blocking collectives: 40.4 us -> 0 us
  between operations: 14 us -> 0.8 us
  other arithmetic: 13.2 us -> 4.46 us
  matrix products: 6.55 us -> 0 us
    pallas_call x0 -> x1, Pallas kernels: none -> 74 us  [finish(): pl.pallas_call(functools.partial(finish_kernel, fsdp_count, tp_count), ou...]
    reduce_scatter x2 -> x0, waiting for transfers between devices: 45.3 us -> none  [the longest x1 34.5 us: scatter_rows(): lax.psum_scatter(partial_rows.astype(jnp.bfloat16), axis, scatter_dimensi...]
    psum x1 -> x0, blocking collectives: 40.4 us -> none  [on_device(): lax.psum((grad_gain1, grad_shift1, grad_qbias, grad_vbias, grad_obias, gr...]
    unnamed x4 -> x0, waiting for transfers between devices: 37.7 us -> none
    dot_general x6 -> x0, matrix products: 6.55 us -> none  [the longest x3 4.04 us: contract_cols(): lax.dot_general(left_rows, right_rows, (((1,), (1,)), ((), ())), preferre...]
    add x4 -> x0, other arithmetic: 4.2 us -> none  [the longest x1 2.16 us: on_device(): inputs_grad = dhidden + norm_back(dnorm1, unit1, spread1, norm1_gain)]
    unnamed x31 -> x13, local copies, waits for them, and re-layouts: 8.76 us -> 5.69 us
  transfers between devices with their start and end apart: 4 -> 0, of which waited for: 4 -> 0; matrix products, arithmetic and copies ran while one was open for 6% -> 0% of each run, Pallas kernels for 0% -> 0%
where the time goes in v5:
time: 281 us; the launch traced here: 280 us
  Pallas kernels  250 us (89%)
  local copies, waits for them, and re-layouts  24.7 us (9%)
  other arithmetic  4.46 us (2%)
    pallas_call x1, Pallas kernels, finish(): pl.pallas_call(functools.partial(finish_kernel, fsdp_count, tp_count), ou...  74 us
    pallas_call x1, Pallas kernels, attend_back(): pl.pallas_call(functools.partial(attend_back_kernel, fsdp_count, tp_count...  51.3 us
    pallas_call x1, Pallas kernels, project(): pl.pallas_call(functools.partial(project_kernel, fsdp_count, tp_count), o...  46.2 us
    pallas_call x1, Pallas kernels, attend(): pl.pallas_call(functools.partial(attend_kernel, fsdp_count, tp_count), ou...  43.8 us
    pallas_call x1, Pallas kernels, by_rows(): pl.pallas_call(functools.partial(rows_kernel, fsdp_count, tp_count), out_...  34.5 us
    unnamed x13, local copies, waits for them, and re-layouts  5.69 us

profile of v5, /device:TPU:0, one launch (start us, length us, event | category | flops | bytes accessed | tf_op | source)
XLA Modules:
  0.0 279.8 jit_solution(12311129766857399703)
XLA Ops:
  0.7 0.1 pad.12.clone
  0.7 1.3 reshape.78.gain_ref
  2.0 1.3 reshape.79.shift_ref
  3.3 0.7 stack.35
  4.0 0.7 stack.36
  4.7 0.7 stack.37
  5.3 0.7 stack.38
  6.0 0.6 pad_maximum_fusion.2.vector_ref
  6.7 0.1 pad.9.clone
  6.7 0.8 reshape.82
  7.5 0.8 stack_reshape_reshape.3
  8.3 0.1 reshape.81
  8.4 0.6 maximum_maximum_fusion.bias_ref
  9.0 0.8 reshape.83
  9.8 0.7 reshape.84.bias_ref
  10.5 0.9 copy.37
  11.4 0.9 copy.38
  12.3 0.1 copy.40
  12.4 1.5 maximum_bitcast_fusion.weight_ref
  13.9 1.7 pad_maximum_fusion.mlp_ref
  15.6 46.2 %project.1 = (bf16[1024,256]{1,0:T(8,128)(2,1)}, bf16[3072,384]{1,0:T(8,128)(2,1)}, bf16[4,256,768]{2,1,0:T(8,128)(2,1)}, bf16[1,768,640]{2,1,0:T(8,128)(2,1)}, ...) custom-call(f32[256,768]{1,0:T(8,128)} %x_ref.5, f32[1,768]{1,0:T(1,128)} %reshape.78.gain_ref, ...), custom_call_target="tpu_custom_call" | custom-call | tf_op jit(solution)/shard_map/project/pallas_call | solution.py:373
  61.9 43.8 %attend.1 = (bf16[4,256,192]{2,1,0:T(8,128)(2,1)}, bf16[1024,192]{1,0:T(8,128)(2,1)}, bf16[3,1024,128]{2,1,0:T(8,128)(2,1)}, bf16[2,768,768]{2,1,0:T(8,128)(2,1)}, bf16[4,768,192]{2,1,0:T(8,128)(2,1)}) custom-call(s32[6]{0:T(128)} %lengths_ref.3, bf16[1024,256]{1,0:T(8,128)(2,1)} %get-tuple-element.50.query_ref, ...), custom_call_target="tpu_custom_call" | custom-call | tf_op jit(solution)/shard_map/attend/pallas_call | solution.py:594
  105.6 34.5 %by_rows.1 = (f32[256,768]{1,0:T(8,128)}, f32[256,768]{1,0:T(8,128)}, bf16[256,768]{1,0:T(8,128)(2,1)}, bf16[4,256,192]{2,1,0:T(8,128)(2,1)}, bf16[4,768,768]{2,...) custom-call(f32[256,768]{1,0:T(8,128)} %x_ref.5, ...), custom_call_target="tpu_custom_call" | custom-call | tf_op jit(solution)/shard_map/by_rows/pallas_call | solution.py:787
  140.2 51.3 %attend_back.1 = (bf16[1024,640]{1,0:T(8,128)(2,1)}, f32[4,96,768]{2,1,0:T(8,128)}, f32[4,96,192]{2,1,0:T(8,128)}, bf16[256,768]{1,0:T(8,128)(2,1)}, f32[1,640]{1,0:T(1,128)}) custom-call(s32[6]{0:T(128)} %lengths_ref.3, bf16[4,256,192]{2,1,0:T(8,128)(2,1)} %get-tuple-element.57.dspread_ref, bf16[3,1024,128]{2,1,0:T(8,128)(2,1)} %get-tuple-element.58.wide_ref, ...), custom_call_target="tpu_custom_call" | custom-call | tf_op jit(solution)/shard_map/attend_back/pallas_call | solution.py:1186
  191.5 74.0 %finish.1 = (f32[256,768]{1,0:T(8,128)}, f32[256,768]{1,0:T(8,128)}, f32[1,96,640]{2,1,0:T(8,128)}, f32[2,96,768]{2,1,0:T(8,128)}, f32[96,192]{1,0:T(8,128)}, /*...) custom-call(f32[256,768]{1,0:T(8,128)} %x_ref.5, f32[1,768]{1,0:T(1,128)} %reshape.78.gain_ref, ...), custom_call_target="tpu_custom_call" | custom-call | tf_op jit(solution)/shard_map/finish/pallas_call | solution.py:1571
  265.5 0.0 copy-start.1
  265.5 0.0 copy-start
  265.5 0.7 slice.22
  266.3 0.7 slice.26
  266.9 0.7 reshape.87
  267.6 0.1 reshape.89
  267.7 0.7 reshape_reshape_squeeze.3
  268.4 0.8 reshape.90
  269.2 0.7 reshape.91
  269.9 1.5 slice_reduce_fusion.1
  271.4 1.5 slice.28
  272.9 0.9 slice.29
  273.9 0.1 copy.42
  274.0 0.0 copy-start.2
  274.0 0.7 copy.45
  274.8 0.7 copy.44
  275.5 1.9 slice_bitcast_fusion
  277.4 0.0 copy-done.1
  277.4 0.9 copy.51
  278.3 0.0 copy-done
  278.3 0.9 copy.52
  279.2 0.0 copy-done.2
  279.2 0.6 copy.53
  (9 shorter events, 0.1 us)
Async XLA Ops:
  265.5 11.9 %copy-start.1 = (f32[256,768]{1,0:T(8,128)S(1)}, f32[256,768]{1,0:T(8,128)}, u32[]{:S(2)}) copy-start(f32[256,768]{1,0:T(8,128)} %get-tuple-element.129) | copy-start | bytes 2359300
  265.5 12.8 %copy-start = (f32[256,768]{1,0:T(8,128)S(1)}, f32[256,768]{1,0:T(8,128)}, u32[]{:S(2)}) copy-start(f32[256,768]{1,0:T(8,128)} %get-tuple-element.130) | copy-start | bytes 2359300
  274.0 5.1 %copy-start.2 = (f32[96,192]{1,0:T(8,128)S(1)}, f32[96,192]{1,0:T(8,128)}, u32[]{:S(2)}) copy-start(f32[96,192]{1,0:T(8,128)} %get-tuple-element.138) | copy-start | bytes 221188

commit v6 on v5

--- a/solution.py
+++ b/solution.py
@@ -49,8 +49,12 @@
 
 
 MESH = pl.DeviceIdType.MESH
-VMEM_LIMIT = 60 * 1024 * 1024
+VMEM_LIMIT = 32 * 1024 * 1024
 LANES = 128
+
+
+def row_of(ref):
+    return ref[...].reshape(1, -1)
 
 
 def remote(source, target, send_sem, recv_sem, fsdp_to, tp_to):
@@ -208,7 +212,7 @@
         f, t, fsdp_count, (mlp_ref,), (mlp_full,), depth, (mlp_send,), (mlp_recv,)
     )
     start_weights()
-    _, _, normed = normalize(x_ref[...], gain_ref[...], shift_ref[...])
+    _, _, normed = normalize(x_ref[...], row_of(gain_ref), row_of(shift_ref))
     normed_ref[t] = normed.astype(jnp.bfloat16)
 
     def row_copy(source, lane, toward):
@@ -632,7 +636,10 @@
     x_ref,
     spread_ref,
     heads_ref,
-    vector_ref,
+    out_bias_ref,
+    gain_ref,
+    shift_ref,
+    last_bias_ref,
     bias_ref,
     own_ref,
     mate_ref,
@@ -641,7 +648,8 @@
     outputs_ref,
     mixed_ref,
     context_ref,
-    mlp_grad,
+    own_grad,
+    mate_grad,
     heads_grad,
     bias_grad,
     sums_ref,
@@ -678,13 +686,13 @@
     pl.semaphore_signal(barrier, inc=1, device_id=(f, peer), device_id_type=MESH)
     pl.semaphore_wait(barrier, 1)
 
-    hidden = x_ref[...] + vector_ref[0:1, :]
+    hidden = x_ref[...] + row_of(out_bias_ref)
     for j in range(tp_count):
         hidden = hidden + lax.dot_general(
             spread_ref[j], heads_ref[j], (((1,), (1,)), ((), ())), preferred_element_type=f32
         )
     hidden_ref[...] = hidden
-    unit, spread, normed = normalize(hidden, vector_ref[1:2, :], vector_ref[2:3, :])
+    unit, spread, normed = normalize(hidden, row_of(gain_ref), row_of(shift_ref))
     unit_ref[...] = unit
     normed_ref[side] = normed.astype(bf16)
     row_copy = remote(normed_ref.at[side], normed_ref.at[side], row_send, row_recv, f, peer)
@@ -745,16 +753,16 @@
     norm_copy = remote(norm_out, norm_in, norm_send, norm_recv, f, peer)
     norm_copy.start()
     mixed_ref[...] = mixed_sum[1 - side].astype(bf16)
-    outputs_ref[...] = hidden_ref[...] + mixed_sum[side] + vector_ref[3:4, :]
-
-    for level in range(2):
-
-        def weight_grads(c, carry, level=level):
+    outputs_ref[...] = hidden_ref[...] + mixed_sum[side] + row_of(last_bias_ref)
+
+    for level, grad in enumerate((own_grad, mate_grad)):
+
+        def weight_grads(c, carry, level=level, grad=grad):
             units = pl.ds(pl.multiple_of(c * tile, tile), tile)
             slopes = slope_ref[level, c]
             both = jnp.concatenate([normed_ref[0], normed_ref[1]], axis=0)
-            mlp_grad[2 * level, units, :] = contract_rows(slopes, both).astype(bf16)
-            mlp_grad[2 * level + 1, units, :] = contract_rows(active_ref[level, c], rounded[...]).astype(bf16)
+            grad[0, units, :] = contract_rows(slopes, both).astype(bf16)
+            grad[1, units, :] = contract_rows(active_ref[level, c], rounded[...]).astype(bf16)
             bias_grad[level, c] = column_sum(slopes.astype(f32))
             return carry
 
@@ -764,7 +772,7 @@
     dnorm = norm_sum[side] + norm_in[...].astype(f32)
     unit = unit_ref[...]
     cotangent = upstream[pl.ds(pl.multiple_of(side * rows, rows), rows), :]
-    gradient = cotangent + norm_back(dnorm, unit, spread, vector_ref[1:2, :])
+    gradient = cotangent + norm_back(dnorm, unit, spread, row_of(gain_ref))
     gradient_ref[...] = gradient
     sums_ref[0:1, :] = column_sum(dnorm * unit)
     sums_ref[1:2, :] = column_sum(dnorm)
@@ -791,13 +799,14 @@
             jax.ShapeDtypeStruct((rows, features), f32),
             jax.ShapeDtypeStruct((rows, features), bf16),
             jax.ShapeDtypeStruct(spread.shape, bf16),
-            jax.ShapeDtypeStruct((4, units, features), bf16),
+            jax.ShapeDtypeStruct(own.shape, bf16),
+            jax.ShapeDtypeStruct(own.shape, bf16),
             jax.ShapeDtypeStruct(heads.shape, bf16),
             jax.ShapeDtypeStruct((2, chunks, 1, 256), f32),
             jax.ShapeDtypeStruct((4, features), f32),
         ),
-        in_specs=whole_specs(7) + [pl.BlockSpec(memory_space=pl.ANY)],
-        out_specs=tuple(whole_specs(8)),
+        in_specs=whole_specs(10) + [pl.BlockSpec(memory_space=pl.ANY)],
+        out_specs=tuple(whole_specs(9)),
         scratch_shapes=[
             pltpu.VMEM((2 * rows, features), f32),
             pltpu.VMEM((2 * rows, features), bf16),
@@ -820,7 +829,7 @@
             collective_id=4, has_side_effects=True, vmem_limit_bytes=VMEM_LIMIT
         ),
         name="by_rows",
-    )(x, spread, heads, vectors, bias, own, mate, cotangent)
+    )(x, spread, heads, *vectors, bias, own, mate, cotangent)
 
 
 def margin_plan(f, fsdp_count, part):
@@ -930,12 +939,10 @@
     wide_ref,
     pair_ref,
     context_ref,
-    mlp_grad,
-    heads_grad,
+    mate_grad,
     mixed_ref,
     dproj_ref,
-    mlp_total,
-    heads_total,
+    mate_in,
     mixed_in,
     sums_ref,
     dcontext,
@@ -945,22 +952,22 @@
     totals,
     halo_out,
     halo_in,
-    mlp_first,
-    mlp_second,
-    heads_first,
-    heads_second,
+    mate_first,
+    mate_second,
+    mate_total,
+    mate_out,
     context_send,
     context_recv,
     mixed_send,
     mixed_recv,
+    mate_send,
+    mate_recv,
     halo_send,
     halo_recv,
     one_send,
     one_recv,
-    mlp_send,
-    mlp_recv,
-    heads_send,
-    heads_recv,
+    two_send,
+    two_recv,
 ):
     f = lax.axis_index("fsdp")
     t = lax.axis_index("tp")
@@ -995,13 +1002,13 @@
         f,
         t,
         fsdp_count,
-        (mlp_grad, heads_grad),
-        (mlp_first, heads_first),
-        (mlp_second, heads_second),
+        (mate_grad,),
+        (mate_first,),
+        (mate_second,),
         one_send,
         one_recv,
-        (mlp_send, heads_send),
-        (mlp_recv, heads_recv),
+        (two_send,),
+        (two_recv,),
     )
     start_grads()
     dcontext[t] = dspread_ref[t]
@@ -1110,6 +1117,9 @@
         return carry
 
     lax.fori_loop(0, 2, half, 0)
+    mate_copy = remote(
+        mate_out, mate_in, mate_send, mate_recv, f, lax.rem(t + tp_count // 2, tp_count)
+    )
 
     def halo_copy(side, part):
         return remote(
@@ -1133,6 +1143,10 @@
                     halo_out[side, part, head] = totals[head, pl.ds(base, QB), :].astype(bf16)
                 halo_copy(side, part).start()
 
+    finish_grads((mate_total,))
+    mate_out[...] = mate_total[...].astype(bf16)
+    mate_copy.start()
+
     for part in range(halves):
         _, receives = margin_plan(f, fsdp_count, part)
         here = pl.ds(margin + part * QB, QB)
@@ -1155,7 +1169,6 @@
     sums_ref[...] = lax.fori_loop(
         0, tp_count, add_rows, jnp.zeros((1, dproj_ref.shape[1]), f32)
     )
-    finish_grads((mlp_total, heads_total))
     mixed_copy.wait()
 
     def settle(j, carry):
@@ -1171,29 +1184,27 @@
             def _(side=side, part=part):
                 halo_copy(side, part).wait_send()
 
-
-def attend_back(
-    fsdp_count, tp_count, lengths, dspread, wide, pairs, context, mlp_grad, heads_grad, mixed
-):
+    mate_copy.wait()
+
+
+def attend_back(fsdp_count, tp_count, lengths, dspread, wide, pairs, context, mate_grad, mixed):
     bf16 = jnp.bfloat16
     f32 = jnp.float32
     heads, group, _ = wide.shape
     _, rows, width = dspread.shape
     count = fsdp_count // 2
-    depth, features = mlp_grad.shape[3:]
+    kinds, _, _, depth, features = mate_grad.shape
     dma = pltpu.SemaphoreType.DMA
-    mlp_kinds = mlp_grad.shape[0]
     return pl.pallas_call(
         functools.partial(attend_back_kernel, fsdp_count, tp_count),
         out_shape=(
             jax.ShapeDtypeStruct((group, heads * LANES + 2 * LANES), bf16),
-            jax.ShapeDtypeStruct((mlp_kinds, depth, features), f32),
-            jax.ShapeDtypeStruct((tp_count, depth, width), f32),
+            jax.ShapeDtypeStruct((kinds, depth, features), bf16),
             jax.ShapeDtypeStruct(mixed.shape, bf16),
             jax.ShapeDtypeStruct((1, heads * LANES + 2 * LANES), f32),
         ),
-        in_specs=[pl.BlockSpec(memory_space=pltpu.SMEM)] + whole_specs(7),
-        out_specs=tuple(whole_specs(5)),
+        in_specs=[pl.BlockSpec(memory_space=pltpu.SMEM)] + whole_specs(6),
+        out_specs=tuple(whole_specs(4)),
         scratch_shapes=[
             pltpu.VMEM((tp_count, rows, width), bf16),
             pltpu.VMEM((heads, CLIP, LANES), bf16),
@@ -1202,20 +1213,20 @@
             pltpu.VMEM((heads, pairs.shape[0], LANES), f32),
             pltpu.VMEM((2, group // QB, heads, QB, LANES), bf16),
             pltpu.VMEM((2, group // QB, heads, QB, LANES), bf16),
-            pltpu.VMEM((mlp_kinds, count, depth, features), bf16),
-            pltpu.VMEM((count, mlp_kinds, depth, features), bf16),
-            pltpu.VMEM((tp_count, count, depth, width), bf16),
-            pltpu.VMEM((count, tp_count, depth, width), bf16),
+            pltpu.VMEM((kinds, count, depth, features), bf16),
+            pltpu.VMEM((count, kinds, depth, features), bf16),
+            pltpu.VMEM((kinds, depth, features), f32),
+            pltpu.VMEM((kinds, depth, features), bf16),
             dma((tp_count,)),
             dma((tp_count,)),
             dma,
             dma,
+            dma,
+            dma,
             dma((2, group // QB)),
             dma((2, group // QB)),
-            dma((2,)),
-            dma((2,)),
-            dma((count,)),
-            dma((count,)),
+            dma((1,)),
+            dma((1,)),
             dma((count,)),
             dma((count,)),
         ],
@@ -1223,7 +1234,7 @@
             collective_id=5, has_side_effects=True, vmem_limit_bytes=VMEM_LIMIT
         ),
         name="attend_back",
-    )(lengths, dspread, wide, pairs, context, mlp_grad, heads_grad, mixed)
+    )(lengths, dspread, wide, pairs, context, mate_grad, mixed)
 
 
 def reduce_copies(f, t, fsdp_count, tp_count, vector, by_fsdp, by_tp, sends, recvs):
@@ -1305,29 +1316,43 @@
     gradient_ref,
     partial_ref,
     mixed_ref,
-    mlp_ref,
-    heads_ref,
+    own_grad,
+    heads_grad,
+    mate_ref,
     sums_ref,
     bias_ref,
     proj_ref,
     inputs_grad,
     outputs_ref,
-    weight_total,
-    mlp_total,
+    key_total,
+    value_total,
+    query_total,
+    up_total,
+    down_total,
     heads_total,
-    late_total,
-    early_total,
-    proj_total,
+    gain1_total,
+    shift1_total,
+    gain2_total,
+    shift2_total,
+    out_bias_total,
+    last_bias_total,
+    query_bias_total,
+    value_bias_total,
     bias_total,
     weight_grad,
     weight_first,
     weight_second,
     weight_sum,
+    weight_total,
+    own_first,
+    own_second,
+    own_total,
+    heads_first,
+    heads_second,
+    heads_sum,
     part_ref,
     row_out,
     row_in,
-    mlp_out,
-    mlp_in,
     heads_out,
     heads_in,
     early,
@@ -1344,6 +1369,12 @@
     one_recv,
     weight_send,
     weight_recv,
+    two_send,
+    two_recv,
+    own_send,
+    own_recv,
+    three_send,
+    three_recv,
     early_send,
     early_recv,
     late_send,
@@ -1356,6 +1387,7 @@
     rows, features = x_ref.shape
     proj_width = dproj_ref.shape[1]
     last = tp_count - 1
+    sub = rows // 2
     units = bias_ref.shape[3]
     early[0:4, :] = sums_ref[...]
     early[4:5, :] = jnp.zeros((1, features), f32)
@@ -1363,9 +1395,20 @@
     for level in range(2):
         for c in range(bias_ref.shape[1]):
             early[5 + level : 6 + level, c * units : (c + 1) * units] = bias_ref[level, c]
-    mlp_out[...] = mlp_ref[2:4].astype(bf16)
-    heads_out[...] = heads_ref[...].astype(bf16)
     greet(fsdp_count, tp_count, f, t)
+    start_own, add_own, finish_own = scatter_copies(
+        f,
+        t,
+        fsdp_count,
+        (own_grad, heads_grad),
+        (own_first, heads_first),
+        (own_second, heads_second),
+        two_send,
+        two_recv,
+        (own_send, three_send),
+        (own_recv, three_recv),
+    )
+    start_own()
     start_early, middle_early, finish_early = reduce_copies(
         f, t, fsdp_count, tp_count, early, early_fsdp, early_tp, early_send, early_recv
     )
@@ -1385,60 +1428,66 @@
         (weight_recv,),
     )
 
-    def row_copy(block, side):
+    def row_copy(piece, side):
         return remote(
-            row_out.at[block],
-            row_in.at[side, block],
-            row_send.at[block],
-            row_recv.at[side, block],
+            row_out.at[piece],
+            row_in.at[side, piece],
+            row_send.at[piece],
+            row_recv.at[side, piece],
             f,
             t + 1 if side == 0 else t - 1,
         )
 
+    def relay(unit, carry):
+        k, low = (unit // 2, lax.rem(unit, 2))
+        for side, (block, valid, inner) in enumerate(
+            ((last - k, last - k > t, t > 0), (k, k < t, t < last))
+        ):
+            piece = 2 * block + low
+            here = pl.ds(pl.multiple_of(low * sub, sub), sub)
+
+            @pl.when(valid & (inner | (unit >= 2)))
+            def _(side=side, block=block, inner=inner, piece=piece, here=here):
+                @pl.when(inner)
+                def _():
+                    row_copy(piece, side).wait_recv()
+                    row_out[piece] = (
+                        part_ref[block, here, :] + row_in[side, piece].astype(f32)
+                    ).astype(bf16)
+
+                @pl.when(jnp.logical_not(inner))
+                def _():
+                    row_out[piece] = part_ref[block, here, :].astype(bf16)
+
+                @pl.when(unit >= 2)
+                def _():
+                    row_copy(piece + 2 - 4 * side, side).wait_send()
+
+                row_copy(piece, side).start()
+
+        return carry
+
     def partial_rows(k, carry):
         block = jnp.where(t < tp_count // 2, last - k, k)
-        product = contract_cols(
+        part_ref[block] = contract_cols(
             dproj_ref[pl.ds(pl.multiple_of(block * rows, rows), rows), :], full_ref[0]
         )
-        part_ref[block] = product
-
-        @pl.when((t == 0) & (block > t))
-        def _():
-            row_out[block] = product.astype(bf16)
-            row_copy(block, 0).start()
-
-        @pl.when((t == last) & (block < t))
-        def _():
-            row_out[block] = product.astype(bf16)
-            row_copy(block, 1).start()
+        for side, (first, end) in enumerate(((last, 0), (0, last))):
+
+            @pl.when((k == 0) & (t == end))
+            def _(side=side, first=first):
+                for low in range(2):
+                    row_out[2 * first + low] = part_ref[
+                        first, low * sub : (low + 1) * sub, :
+                    ].astype(bf16)
+                    row_copy(2 * first + low, side).start()
 
         return carry
 
     lax.fori_loop(0, tp_count, partial_rows, 0)
     start_early()
     depth = weight_grad.shape[3]
-
-    mlp_copy = remote(
-        mlp_out, mlp_in, side_send.at[0], side_recv.at[0], f, lax.rem(t + tp_count // 2, tp_count)
-    )
-    mlp_copy.start()
-
-    def heads_copy(j):
-        toward = lax.rem(t + j, tp_count)
-        return remote(
-            heads_out.at[toward],
-            heads_in.at[t],
-            side_send.at[j],
-            side_recv.at[tp_count + t],
-            f,
-            toward,
-        )
-
-    def heads_start(j, carry):
-        heads_copy(j).start()
-        return carry
-
-    lax.fori_loop(1, tp_count, heads_start, 0)
+    add_own()
     tall = 256
 
     def weight_part(c, carry):
@@ -1463,26 +1512,81 @@
     lax.fori_loop(0, fsdp_count, arrange, 0)
     start_weights()
     outputs_ref[...] = partial_ref[...] + mixed_ref[...].astype(f32)
-    unit, spread, _ = normalize(x_ref[...], gain_ref[...], shift_ref[...])
+    unit, spread, _ = normalize(x_ref[...], row_of(gain_ref), row_of(shift_ref))
     add_weights()
     middle_early()
 
-    def relay(k, carry):
-        for side, (block, valid) in enumerate(
-            ((last - k, (last - k > t) & (t > 0)), (k, (k < t) & (t < last)))
-        ):
-
-            @pl.when(valid)
-            def _(side=side, block=block):
-                row_copy(block, side).wait_recv()
-                row_out[block] = (part_ref[block] + row_in[side, block].astype(f32)).astype(bf16)
-                row_copy(block, side).start()
-
-        return carry
-
-    lax.fori_loop(0, last, relay, 0)
+    lax.fori_loop(0, 2 * last, relay, 0)
+    finish_own((own_total, heads_sum))
+    heads_out[...] = heads_sum[...].astype(bf16)
+
+    def heads_copy(j):
+        toward = lax.rem(t + j, tp_count)
+        return remote(
+            heads_out.at[toward],
+            heads_in.at[t],
+            side_send.at[j],
+            side_recv.at[t],
+            f,
+            toward,
+        )
+
+    def heads_start(j, carry):
+        heads_copy(j).start()
+        return carry
+
+    lax.fori_loop(1, tp_count, heads_start, 0)
     finish_weights((weight_total,))
-    heads_total[...] = heads_ref[t]
+    lane = lax.broadcasted_iota(jnp.int32, (depth, LANES), 1)
+    tiles = [weight_total[0, :, j * LANES : (j + 1) * LANES] for j in range(5)]
+    turned = [pltpu.roll(tile, HD, axis=1) for tile in tiles[:3]]
+    key_total[:, 0:LANES] = jnp.where(lane < HD, tiles[0], turned[1])
+    key_total[:, LANES:] = tiles[2][:, :HD]
+    value_total[:, 0:LANES] = jnp.where(lane < HD, turned[0], tiles[1])
+    value_total[:, LANES:] = turned[2][:, :HD]
+    query_total[:, 0:LANES] = tiles[3]
+    query_total[:, LANES:] = tiles[4][:, :HD]
+    up_total[...] = own_total[0] + mate_ref[0].astype(f32)
+    down_total[...] = own_total[1] + mate_ref[1].astype(f32)
+    finish_early()
+    for row, total in enumerate((gain2_total, shift2_total, out_bias_total, last_bias_total)):
+        total[...] = jnp.sum(early_tp[:, row, :], axis=0)
+    for j in range(tp_count):
+        tiles = [early_tp[j, 4:5, i * LANES : (i + 1) * LANES] for i in range(5)]
+        turned = [pltpu.roll(tile, HD, axis=1) for tile in tiles[:3]]
+        value_bias_total[j : j + 1, 0:LANES] = jnp.where(lane[0:1] < HD, turned[0], tiles[1])
+        value_bias_total[j : j + 1, LANES:] = turned[2][:, :HD]
+        query_bias_total[j : j + 1, 0:LANES] = tiles[3]
+        query_bias_total[j : j + 1, LANES:] = tiles[4][:, :HD]
+        bias_total[j : j + 1, :] = (
+            early_tp[j, 5:6, :] + early_tp[(j + tp_count // 2) % tp_count, 6:7, :]
+        )
+
+    for side, inner in enumerate((t > 0, t < last)):
+
+        @pl.when(inner)
+        def _(side=side):
+            for low in range(2):
+                row_copy(2 * t + low, side).wait_recv()
+                part_ref[t, low * sub : (low + 1) * sub, :] += row_in[side, 2 * t + low].astype(
+                    f32
+                )
+
+    dnorm = part_ref[t]
+    late[0:1, :] = column_sum(dnorm * unit)
+    late[1:2, :] = column_sum(dnorm)
+    start_late()
+    inputs_grad[...] = gradient_ref[...] + norm_back(dnorm, unit, spread, row_of(gain_ref))
+    middle_late()
+
+    for side, outer in enumerate((t < last, t > 0)):
+
+        @pl.when(outer)
+        def _(side=side):
+            for low in range(2):
+                row_copy(2 * (t + 1 - 2 * side) + low, side).wait_send()
+
+    heads_total[...] = heads_sum[t]
 
     def heads_done(j, carry):
         source = lax.rem(t + j, tp_count)
@@ -1490,7 +1594,7 @@
             heads_out.at[source],
             heads_in.at[source],
             side_send.at[j],
-            side_recv.at[tp_count + source],
+            side_recv.at[source],
             f,
             source,
         ).wait_recv()
@@ -1499,47 +1603,9 @@
         return carry
 
     lax.fori_loop(1, tp_count, heads_done, 0)
-    mlp_copy.wait()
-    mlp_total[...] = mlp_ref[0:2] + mlp_in[...].astype(f32)
-    finish_early()
-    early_total[...] = jnp.sum(early_tp[:, 0:4, :], axis=0)
-    for j in range(tp_count):
-        proj_total[j : j + 1, :] = early_tp[j, 4:5, 0:proj_width]
-        bias_total[j : j + 1, :] = (
-            early_tp[j, 5:6, :] + early_tp[(j + tp_count // 2) % tp_count, 6:7, :]
-        )
-
-    @pl.when(t > 0)
-    def _():
-        row_copy(t, 0).wait_recv()
-        part_ref[t] += row_in[0, t].astype(f32)
-
-    @pl.when(t < last)
-    def _():
-        row_copy(t, 1).wait_recv()
-        part_ref[t] += row_in[1, t].astype(f32)
-
-    dnorm = part_ref[t]
-    late[0:1, :] = column_sum(dnorm * unit)
-    late[1:2, :] = column_sum(dnorm)
-    start_late()
-    inputs_grad[...] = gradient_ref[...] + norm_back(dnorm, unit, spread, gain_ref[...])
-    middle_late()
-
-    def settle(block, carry):
-        @pl.when(block > t)
-        def _():
-            row_copy(block, 0).wait_send()
-
-        @pl.when(block < t)
-        def _():
-            row_copy(block, 1).wait_send()
-
-        return carry
-
-    lax.fori_loop(0, tp_count, settle, 0)
     finish_late()
-    late_total[...] = jnp.sum(late_tp[...], axis=0)
+    gain1_total[...] = jnp.sum(late_tp[:, 0, :], axis=0)
+    shift1_total[...] = jnp.sum(late_tp[:, 1, :], axis=0)
 
 
 def finish(
@@ -1554,8 +1620,9 @@
     gradient,
     partial,
     mixed,
-    mlp,
-    heads,
+    own_grad,
+    heads_grad,
+    mate,
     sums,
     bias,
     proj,
@@ -1563,7 +1630,8 @@
     bf16 = jnp.bfloat16
     f32 = jnp.float32
     rows, features = x.shape
-    _, depth, width = heads.shape
+    kinds = own_grad.shape[0]
+    _, _, _, depth, width = heads_grad.shape
     proj_width = dproj.shape[1]
     count = fsdp_count // 2
     dma = pltpu.SemaphoreType.DMA
@@ -1573,26 +1641,34 @@
         out_shape=(
             jax.ShapeDtypeStruct((rows, features), f32),
             jax.ShapeDtypeStruct((rows, features), f32),
-            jax.ShapeDtypeStruct((1, depth, proj_width), f32),
-            jax.ShapeDtypeStruct((2, depth, features), f32),
             jax.ShapeDtypeStruct((depth, width), f32),
-            jax.ShapeDtypeStruct((2, features), f32),
-            jax.ShapeDtypeStruct((4, features), f32),
-            jax.ShapeDtypeStruct((tp_count, proj_width), f32),
+            jax.ShapeDtypeStruct((depth, width), f32),
+            jax.ShapeDtypeStruct((depth, width), f32),
+            jax.ShapeDtypeStruct((depth, features), f32),
+            jax.ShapeDtypeStruct((depth, features), f32),
+            jax.ShapeDtypeStruct((depth, width), f32),
+            *[jax.ShapeDtypeStruct((features,), f32)] * 6,
+            jax.ShapeDtypeStruct((tp_count, width), f32),
+            jax.ShapeDtypeStruct((tp_count, width), f32),
             jax.ShapeDtypeStruct((tp_count, features), f32),
         ),
-        in_specs=whole_specs(14),
-        out_specs=tuple(whole_specs(9)),
+        in_specs=whole_specs(15),
+        out_specs=tuple(whole_specs(17)),
         scratch_shapes=[
             pltpu.VMEM((1, count, 2, depth, proj_width), bf16),
             pltpu.VMEM((1, count, depth, proj_width), bf16),
             pltpu.VMEM((count, 1, depth, proj_width), bf16),
             pltpu.VMEM((features, proj_width), bf16),
+            pltpu.VMEM((1, depth, proj_width), f32),
+            pltpu.VMEM((kinds, count, depth, features), bf16),
+            pltpu.VMEM((count, kinds, depth, features), bf16),
+            pltpu.VMEM((kinds, depth, features), f32),
+            pltpu.VMEM((tp_count, count, depth, width), bf16),
+            pltpu.VMEM((count, tp_count, depth, width), bf16),
+            pltpu.VMEM((tp_count, depth, width), f32),
             pltpu.VMEM((tp_count, rows, features), f32),
-            pltpu.VMEM((tp_count, rows, features), bf16),
-            pltpu.VMEM((2, tp_count, rows, features), bf16),
-            pltpu.VMEM((2, depth, features), bf16),
-            pltpu.VMEM((2, depth, features), bf16),
+            pltpu.VMEM((2 * tp_count, rows // 2, features), bf16),
+            pltpu.VMEM((2, 2 * tp_count, rows // 2, features), bf16),
             pltpu.VMEM((tp_count, depth, width), bf16),
             pltpu.VMEM((tp_count, depth, width), bf16),
             pltpu.VMEM((7, features), f32),
@@ -1601,12 +1677,18 @@
             pltpu.VMEM((2, features), f32),
             pltpu.VMEM((fsdp_count, 2, features), f32),
             pltpu.VMEM((tp_count, 2, features), f32),
+            dma((2 * tp_count,)),
+            dma((2, 2 * tp_count)),
             dma((tp_count,)),
-            dma((2, tp_count)),
             dma((tp_count,)),
-            dma((2 * tp_count,)),
             dma((1,)),
             dma((1,)),
+            dma((count,)),
+            dma((count,)),
+            dma((2,)),
+            dma((2,)),
+            dma((count,)),
+            dma((count,)),
             dma((count,)),
             dma((count,)),
             dma((peers,)),
@@ -1628,8 +1710,9 @@
         gradient,
         partial,
         mixed,
-        mlp,
-        heads,
+        own_grad,
+        heads_grad,
+        mate,
         sums,
         bias,
         proj,
@@ -1678,8 +1761,8 @@
         fsdp_count,
         tp_count,
         inputs,
-        norm1_gain.reshape(1, -1),
-        norm1_shift.reshape(1, -1),
+        norm1_gain,
+        norm1_shift,
         pack_columns(key_weight, value_weight, query_weight)[None],
         pack_columns(jnp.zeros((tp_count, 1, local_width), f32), by_tp(value_bias), by_tp(query_bias)),
         mlp_own,
@@ -1691,20 +1774,31 @@
         fsdp_count, tp_count, clip_lengths, query, pairs, mlp_own, out_parts, heads_here
     )
     unit_bias = jnp.swapaxes(fc1_bias.reshape(fsdp_count, tp_count, unit_count), 0, 1)
-    dhidden, outputs, mixed, dspread, mlp_grad, heads_grad, bias_part, sums = by_rows(
+    (
+        dhidden,
+        outputs,
+        mixed,
+        dspread,
+        own_grad,
+        mate_grad,
+        heads_grad,
+        bias_part,
+        sums,
+    ) = by_rows(
         fsdp_count,
         tp_count,
         inputs,
         spread,
         out_full,
-        jnp.stack([out_bias, norm2_gain, norm2_shift, fc2_bias]),
+        (out_bias, norm2_gain, norm2_shift, fc2_bias),
         unit_bias.reshape(tp_count, -1, 1, 256),
         mlp_w,
         mlp_other,
         out_cotangent,
     )
     count = fsdp_count // 2
-    dproj, mlp_total, heads_total, mixed, proj_sums = attend_back(
+    by_owner = lambda grad: grad.reshape(grad.shape[0], count, 2, unit_count, -1)
+    dproj, mate_total, mixed, proj_sums = attend_back(
         fsdp_count,
         tp_count,
         clip_lengths,
@@ -1712,46 +1806,49 @@
         wide,
         pairs,
         context,
-        mlp_grad.reshape(4, count, 2, unit_count, -1),
-        heads_grad.reshape(tp_count, count, 2, unit_count, -1),
+        by_owner(mate_grad),
         mixed,
     )
-    inputs_grad, outputs, weight_total, mlp_total, grad_out, late, early, proj_total, bias_total = (
-        finish(
-            fsdp_count,
-            tp_count,
-            inputs,
-            norm1_gain.reshape(1, -1),
-            norm1_shift.reshape(1, -1),
-            dproj,
-            attention_w,
-            normed,
-            dhidden,
-            outputs,
-            mixed,
-            mlp_total,
-            heads_total,
-            sums,
-            bias_part,
-            proj_sums,
-        )
-    )
-    grad_gain1, grad_shift1 = late
-    grad_gain2, grad_shift2, grad_obias, grad_b2 = early
-    grad_fc1, grad_fc2 = mlp_total
+    (
+        inputs_grad,
+        outputs,
+        grad_key,
+        grad_value,
+        grad_query,
+        grad_fc1,
+        grad_fc2,
+        grad_out,
+        grad_gain1,
+        grad_shift1,
+        grad_gain2,
+        grad_shift2,
+        grad_obias,
+        grad_b2,
+        grad_qbias,
+        grad_vbias,
+        bias_total,
+    ) = finish(
+        fsdp_count,
+        tp_count,
+        inputs,
+        norm1_gain,
+        norm1_shift,
+        dproj,
+        attention_w,
+        normed,
+        dhidden,
+        outputs,
+        mixed,
+        by_owner(own_grad),
+        by_owner(heads_grad),
+        mate_total,
+        sums,
+        bias_part,
+        proj_sums,
+    )
+    grad_qbias = grad_qbias.reshape(-1)
+    grad_vbias = grad_vbias.reshape(-1)
     grad_b1 = jnp.swapaxes(bias_total.reshape(tp_count, fsdp_count, unit_count), 0, 1).reshape(-1)
-
-    def unpack_columns(values):
-        lead = values.shape[0]
-        pair = values[:, :pair_width].reshape(lead, heads_here, 2, HD)
-        return (
-            pair[:, :, 0].reshape(lead, local_width),
-            pair[:, :, 1].reshape(lead, local_width),
-            values[:, pair_width : pair_width + local_width],
-        )
-
-    grad_key, grad_value, grad_query = unpack_columns(weight_total[0])
-    _, grad_vbias, grad_qbias = (part.reshape(-1) for part in unpack_columns(proj_total))
     return (
         outputs,
         inputs_grad,

time: 281 us -> 222 us (0.79)
  Pallas kernels: 250 us -> 197 us
  local copies, waits for them, and re-layouts: 24.7 us -> 21.4 us
    pallas_call x1, Pallas kernels: 74 us -> 50.7 us  [finish(): pl.pallas_call(functools.partial(finish_kernel, fsdp_count, tp_count), ou...]
    pallas_call x1, Pallas kernels: 51.3 us -> 36.5 us  [attend_back(): pl.pallas_call(functools.partial(attend_back_kernel, fsdp_count, tp_count...]
    unnamed x13 -> x40, local copies, waits for them, and re-layouts: 5.69 us -> 16.5 us
    another operation x7 -> x0, local copies, waits for them, and re-layouts: 6.85 us -> none  [the longest x4 2.76 us: on_device(): jnp.stack([out_bias, norm2_gain, norm2_shift, fc2_bias])]
    pallas_call x1, Pallas kernels: 34.5 us -> 27.8 us  [by_rows(): pl.pallas_call(functools.partial(rows_kernel, fsdp_count, tp_count), out_...]
    pallas_call x1, Pallas kernels: 46.2 us -> 41.8 us  [project(): pl.pallas_call(functools.partial(project_kernel, fsdp_count, tp_count), o...]
    slice x7 -> x0, local copies, waits for them, and re-layouts: 4.06 us -> none  [the longest x2 2.28 us: unpack_columns(): values[:, pair_width:pair_width + local_width]]
    pallas_call x1, Pallas kernels: 43.8 us -> 40 us  [attend(): pl.pallas_call(functools.partial(attend_kernel, fsdp_count, tp_count), ou...]
where the time goes in v6:
time: 222 us; the launch traced here: 221 us
  Pallas kernels  197 us (89%)
  local copies, waits for them, and re-layouts  21.4 us (10%)
    pallas_call x1, Pallas kernels, finish(): pl.pallas_call(functools.partial(finish_kernel, fsdp_count, tp_count), ou...  50.7 us
    pallas_call x1, Pallas kernels, project(): pl.pallas_call(functools.partial(project_kernel, fsdp_count, tp_count), o...  41.8 us
    pallas_call x1, Pallas kernels, attend(): pl.pallas_call(functools.partial(attend_kernel, fsdp_count, tp_count), ou...  40 us
    pallas_call x1, Pallas kernels, attend_back(): pl.pallas_call(functools.partial(attend_back_kernel, fsdp_count, tp_count...  36.5 us
    pallas_call x1, Pallas kernels, by_rows(): pl.pallas_call(functools.partial(rows_kernel, fsdp_count, tp_count), out_...  27.8 us
    unnamed x40, local copies, waits for them, and re-layouts  16.5 us

profile of v6, /device:TPU:0, one launch (start us, length us, event | category | flops | bytes accessed | tf_op | source)
XLA Modules:
  0.0 221.0 jit_solution(1137733376831614700)
XLA Ops:
  0.7 0.0 copy-start.11
  0.7 0.1 pad.8.clone
  0.8 0.1 pad.5.clone
  0.8 0.8 reshape.72
  1.6 0.8 stack_reshape_reshape.3
  2.4 0.1 reshape.71
  2.5 0.8 reshape.73
  3.3 0.1 reshape.74.bias_ref
  3.4 0.9 copy.37
  4.3 0.9 copy.38
  5.2 0.1 copy.40
  5.4 0.8 maximum_bitcast_fusion.weight_ref
  6.2 1.0 pad_maximum_fusion.mlp_ref
  7.2 0.0 copy-start
  7.2 1.1 copy-done
  8.4 0.0 copy-start.4
  8.4 0.8 copy-done.4
  9.2 0.0 copy-start.5
  9.2 0.7 copy-done.5
  9.8 0.0 copy-start.6
  9.8 0.7 copy-done.6
  10.5 0.0 copy-start.1
  10.5 0.0 copy-start.2
  10.5 0.0 copy-start.7
  10.5 0.0 copy-start.8
  10.5 0.0 copy-start.9
  10.5 0.0 copy-start.10
  10.6 41.8 %project.1 = (bf16[1024,256]{1,0:T(8,128)(2,1)S(1)}, bf16[3072,384]{1,0:T(8,128)(2,1)S(1)}, bf16[4,256,768]{2,1,0:T(8,128)(2,1)S(1)}, bf16[1,768,640]{2,1,0:T(8,...) custom-call(f32[256,768]{1,0:T(8,128)S(1)} %copy-done, f32[768]{0:T(1024)S(1)} %copy-done.5, ...), custom_call_target="tpu_custom_call" | custom-call | tf_op jit(solution)/shard_map/project/pallas_call | solution.py:377
  52.4 0.0 copy-done.11
  52.4 40.0 %attend.1 = (bf16[4,256,192]{2,1,0:T(8,128)(2,1)S(1)}, bf16[1024,192]{1,0:T(8,128)(2,1)S(1)}, bf16[3,1024,128]{2,1,0:T(8,128)(2,1)S(1)}, bf16[2,768,768]{2,1,0:T(8,128)(2,1)S(1)}, bf16[4,768,192]{2,1,0:T(8,128)(2,1)S(1)}) custom-call(s32[6]{0:T(128)S(1)} %copy-done.11, bf16[1024,256]{1,0:T(8,128)(2,1)S(1)} %get-tuple-element.58.query_ref, ...), custom_call_target="tpu_custom_call" | custom-call | tf_op jit(solution)/shard_map/attend/pallas_call | solution.py:598
  92.4 0.0 copy-done.1
  92.4 0.0 copy-done.2
  92.4 0.0 copy-done.7
  92.4 0.0 copy-done.8
  92.4 0.0 copy-done.9
  92.4 0.0 copy-done.10
  92.5 27.8 %by_rows.1 = (f32[256,768]{1,0:T(8,128)S(1)}, f32[256,768]{1,0:T(8,128)S(1)}, bf16[256,768]{1,0:T(8,128)(2,1)S(1)}, bf16[4,256,192]{2,1,0:T(8,128)(2,1)S(1)}, bf...) custom-call(f32[256,768]{1,0:T(8,128)S(1)} %copy-done.1, ...), custom_call_target="tpu_custom_call" | custom-call | tf_op jit(solution)/shard_map/by_rows/pallas_call | solution.py:795
  120.3 36.5 %attend_back.1 = (bf16[1024,640]{1,0:T(8,128)(2,1)S(1)}, bf16[2,96,768]{2,1,0:T(8,128)(2,1)S(1)}, bf16[256,768]{1,0:T(8,128)(2,1)S(1)}, f32[1,640]{1,0:T(1,128)S(1)}) custom-call(s32[6]{0:T(128)S(1)} %copy-done.11, bf16[4,256,192]{2,1,0:T(8,128)(2,1)S(1)} %get-tuple-element.65.dspread_ref, bf16[3,1024,128]{2,1,0:T(8,128)(2,1)S(1)} %get-tuple-element.66.wide_ref, ...), custom_call_target="tpu_custom_call" | custom-call | tf_op jit(solution)/shard_map/attend_back/pallas_call | solution.py:1198
  156.8 50.7 %finish.1 = (f32[256,768]{1,0:T(8,128)S(1)}, f32[256,768]{1,0:T(8,128)S(1)}, f32[96,192]{1,0:T(8,128)S(1)}, f32[96,192]{1,0:T(8,128)S(1)}, f32[96,192]{1,0:T(8,1...) custom-call(f32[256,768]{1,0:T(8,128)S(1)} %copy-done.1, ...), custom_call_target="tpu_custom_call" | custom-call | tf_op jit(solution)/shard_map/finish/pallas_call | solution.py:1639
  207.5 0.0 copy-start.3
  207.5 0.9 copy-done.3
  208.4 0.7 reshape.78
  209.1 0.7 reshape.79
  209.8 0.1 reshape.80
  209.8 0.7 reshape.81
  210.5 2.1 copy.59
  212.6 0.9 copy.60
  213.5 0.6 copy.61
  214.1 0.6 copy.62
  214.7 0.6 copy.63
  215.3 0.6 copy.64
  215.9 0.6 copy.65
  216.6 0.6 copy.66
  217.2 0.6 copy.67
  217.8 0.6 copy.68
  218.4 0.6 copy.69
  219.0 0.7 copy.70
  219.7 0.7 copy.71
  220.4 0.6 copy.72
  (8 shorter events, 0.1 us)
Async XLA Ops:
  0.7 51.7 %copy-start.11 = (s32[6]{0:T(128)S(1)}, s32[6]{0:T(128)}, u32[]{:S(2)}) copy-start(s32[6]{0:T(128)} %lengths_ref.3) | copy-start | bytes 76
  7.2 1.1 copy-start
  8.4 0.8 copy-start.4
  9.2 0.7 copy-start.5
  9.8 0.7 copy-start.6
  10.5 81.9 %copy-start.1 = (f32[256,768]{1,0:T(8,128)S(1)}, f32[256,768]{1,0:T(8,128)}, u32[]{:S(2)}) copy-start(f32[256,768]{1,0:T(8,128)} %x_ref.5) | copy-start | bytes 2359300
  10.5 81.9 %copy-start.2 = (f32[1024,768]{1,0:T(8,128)S(1)}, f32[1024,768]{1,0:T(8,128)}, u32[]{:S(2)}) copy-start(f32[1024,768]{1,0:T(8,128)} %cotangent_ref.1) | copy-start | bytes 9437188
  10.5 81.9 %copy-start.7 = (f32[768]{0:T(1024)S(1)}, f32[768]{0:T(1024)}, u32[]{:S(2)}) copy-start(f32[768]{0:T(1024)} %out_bias_ref.1) | copy-start | bytes 9220
  10.5 81.9 %copy-start.8 = (f32[768]{0:T(1024)S(1)}, f32[768]{0:T(1024)}, u32[]{:S(2)}) copy-start(f32[768]{0:T(1024)} %gain_ref.4) | copy-start | bytes 9220
  10.5 81.9 %copy-start.9 = (f32[768]{0:T(1024)S(1)}, f32[768]{0:T(1024)}, u32[]{:S(2)}) copy-start(f32[768]{0:T(1024)} %shift_ref.4) | copy-start | bytes 9220
  10.5 81.9 %copy-start.10 = (f32[768]{0:T(1024)S(1)}, f32[768]{0:T(1024)}, u32[]{:S(2)}) copy-start(f32[768]{0:T(1024)} %last_bias_ref.1) | copy-start | bytes 9220
  207.5 0.9 copy-start.3

commit v7 on v6

--- a/solution.py
+++ b/solution.py
@@ -158,22 +158,84 @@
     return (start, relay, finish, drain)
 
 
+def swapped(tile):
+    return pltpu.roll(tile, HD, axis=1)
+
+
+def joined(low, high):
+    lane = lax.broadcasted_iota(jnp.int32, low.shape, 1)
+    return jnp.where(lane < HD, low, high)
+
+
+def pack_weights(key_ref, value_ref, query_ref, packed_ref):
+    def tiles(ref):
+        spare = jnp.zeros((ref.shape[0], HD), jnp.float32)
+        return (
+            ref[:, :LANES].astype(jnp.float32),
+            jnp.concatenate([ref[:, LANES:].astype(jnp.float32), spare], axis=1),
+        )
+
+    key, value, query = tiles(key_ref), tiles(value_ref), tiles(query_ref)
+    packed = (
+        joined(key[0], swapped(value[0])),
+        joined(swapped(key[0]), value[0]),
+        joined(key[1], swapped(value[1])),
+        *query,
+    )
+    for j, tile in enumerate(packed):
+        packed_ref[0, :, j * LANES : (j + 1) * LANES] = tile.astype(jnp.bfloat16)
+
+
+def pack_bias(t, tp_count, value, query):
+    def half(row, head, high):
+        tile = row[:, (head // 2) * LANES : (head // 2 + 1) * LANES]
+        return tile if head % 2 == high else swapped(tile)
+
+    heads = value.shape[1] // HD // tp_count
+    none = jnp.zeros((1, LANES), jnp.float32)
+    total = jnp.zeros((1, (heads + 2) * LANES), jnp.float32)
+    for j in range(tp_count):
+        first = j * heads
+        tiles = [joined(none, half(value, first + h, 1)) for h in range(heads)]
+        tiles.append(joined(half(query, first, 0), half(query, first + 1, 1)))
+        tiles.append(joined(half(query, first + 2, 0), none))
+        total = total + jnp.where(t == j, jnp.concatenate(tiles, axis=1), 0.0)
+    return total
+
+
 def project_kernel(
     fsdp_count,
     tp_count,
-    x_ref,
-    gain_ref,
-    shift_ref,
-    weight_ref,
-    bias_ref,
-    mlp_ref,
-    out_ref,
+    x_hbm,
+    gain_hbm,
+    shift_hbm,
+    key_hbm,
+    value_hbm,
+    query_hbm,
+    value_bias_hbm,
+    query_bias_hbm,
+    up_hbm,
+    down_hbm,
+    out_hbm,
     query_ref,
     pair_ref,
     normed_ref,
     full_ref,
     mlp_full,
     heads_ref,
+    mlp_ref,
+    x_ref,
+    gain_ref,
+    shift_ref,
+    key_weight,
+    value_weight,
+    query_weight,
+    value_bias,
+    query_bias,
+    out_ref,
+    weight_ref,
+    bias_ref,
+    load_sem,
     side_send,
     side_recv,
     weight_send,
@@ -197,6 +259,26 @@
     above = f + 1 < fsdp_count
     below = f > 0
     blank = jnp.zeros((256, pair_width), jnp.bfloat16)
+    loads = [
+        pltpu.make_async_copy(source, target, load_sem.at[i])
+        for i, (source, target) in enumerate(
+            (
+                (key_hbm, key_weight),
+                (value_hbm, value_weight),
+                (query_hbm, query_weight),
+                (x_hbm, x_ref),
+                (gain_hbm, gain_ref),
+                (shift_hbm, shift_ref),
+                (value_bias_hbm, value_bias),
+                (query_bias_hbm, query_bias),
+                (out_hbm, out_ref),
+                (up_hbm, mlp_ref.at[0]),
+                (down_hbm, mlp_ref.at[1]),
+            )
+        )
+    ]
+    for load in loads:
+        load.start()
 
     def clear(i, carry):
         pair_ref[pl.ds(i * 256, 256), :] = blank
@@ -204,7 +286,11 @@
         return carry
 
     lax.fori_loop(0, margin // 256, clear, 0)
+    for load in loads:
+        load.wait()
+    pack_weights(key_weight, value_weight, query_weight, weight_ref)
     greet(fsdp_count, tp_count, f, t)
+    bias_ref[...] = pack_bias(t, tp_count, row_of(value_bias), row_of(query_bias))
     start_weights, relay_weights, finish_weights, drain_weights = gather_copies(
         f, t, fsdp_count, (weight_ref,), (full_ref,), depth, (weight_send,), (weight_recv,)
     )
@@ -287,7 +373,7 @@
 
     def compute(source):
         out = jnp.dot(normed_ref[source], full_ref[0], preferred_element_type=jnp.float32)
-        out = (out + bias_ref[t]).astype(jnp.bfloat16)
+        out = (out + bias_ref[...]).astype(jnp.bfloat16)
         pair_ref[pl.ds(margin + source * rows, rows), :] = out[:, :pair_width]
         for side, needed in enumerate(halo_sends(source)):
 
@@ -307,22 +393,30 @@
         valid = (source >= 0) & (source < tp_count)
         return (source, onward, valid, valid & (onward >= 0) & (onward < tp_count))
 
-    def receive(k, carry):
-        source, onward, valid, forward = arrival(k)
-
-        @pl.when(valid)
-        def _():
-            row_copy(source, 0, t).wait_recv()
-
-            @pl.when(forward)
+    def receive(step, carry):
+        for side in range(2):
+            source, onward, valid, forward = arrival(2 * step + side)
+
+            @pl.when(valid)
+            def _(source=source, onward=onward, forward=forward):
+                row_copy(source, 0, t).wait_recv()
+
+                @pl.when(forward)
+                def _():
+                    row_copy(source, source, onward).start()
+
+        def work(side, inner):
+            source, _, valid, _ = arrival(2 * step + side)
+
+            @pl.when(valid)
             def _():
-                row_copy(source, source, onward).start()
-
-            compute(source)
-
-        return carry
-
-    lax.fori_loop(0, 2 * (tp_count - 1), receive, 0)
+                compute(source)
+
+            return inner
+
+        return lax.fori_loop(0, 2, work, carry)
+
+    lax.fori_loop(0, tp_count - 1, receive, 0)
     relay_mlp()
     lax.fori_loop(1, tp_count, heads_done, 0)
 
@@ -368,25 +462,35 @@
     return [pl.BlockSpec(memory_space=pltpu.VMEM)] * count
 
 
-def project(fsdp_count, tp_count, x, gain, shift, weights, bias, mlp, out_weight, pair_width, margin):
+def project(fsdp_count, tp_count, x, gain, shift, weights, biases, mlp, out_weight, margin):
     bf16 = jnp.bfloat16
     rows, features = x.shape
     group = rows * tp_count
-    depth = weights.shape[1]
+    depth, width = out_weight.shape
+    pair_width = width // HD * LANES
+    packed_width = pair_width + 2 * LANES
     dma = pltpu.SemaphoreType.DMA
     return pl.pallas_call(
         functools.partial(project_kernel, fsdp_count, tp_count),
         out_shape=(
-            jax.ShapeDtypeStruct((group, weights.shape[2] - pair_width), bf16),
+            jax.ShapeDtypeStruct((group, 2 * LANES), bf16),
             jax.ShapeDtypeStruct((group + 2 * margin, pair_width), bf16),
             jax.ShapeDtypeStruct((tp_count, rows, features), bf16),
-            jax.ShapeDtypeStruct((1, depth * fsdp_count, weights.shape[2]), bf16),
+            jax.ShapeDtypeStruct((1, depth * fsdp_count, packed_width), bf16),
             jax.ShapeDtypeStruct((2, depth * fsdp_count, features), bf16),
             jax.ShapeDtypeStruct((tp_count, *out_weight.shape), bf16),
+            jax.ShapeDtypeStruct((2, depth, features), bf16),
         ),
-        in_specs=whole_specs(7),
-        out_specs=tuple(whole_specs(6)),
+        in_specs=[pl.BlockSpec(memory_space=pltpu.MemorySpace.HBM)] * 11,
+        out_specs=tuple(whole_specs(7)),
         scratch_shapes=[
+            *[
+                pltpu.VMEM(v.shape, v.dtype)
+                for v in (x, gain, shift, *weights, *biases, out_weight)
+            ],
+            pltpu.VMEM((1, depth, packed_width), bf16),
+            pltpu.VMEM((1, packed_width), jnp.float32),
+            dma((11,)),
             dma((tp_count,)),
             dma((tp_count,)),
             dma((fsdp_count,)),
@@ -402,7 +506,7 @@
             collective_id=1, has_side_effects=True, vmem_limit_bytes=VMEM_LIMIT
         ),
         name="project",
-    )(x, gain, shift, weights, bias, mlp, out_weight)
+    )(x, gain, shift, *weights, *biases, *mlp, out_weight)
 
 
 def block_clip(f, part, margin):
@@ -476,14 +580,33 @@
     start_out, relay_out, finish_out, drain_out = gather_copies(
         f, t, fsdp_count, (out_ref,), (out_full,), depth, (out_send,), (out_recv,)
     )
-    start_mlp, relay_mlp, finish_mlp, drain_mlp = gather_copies(
-        f, t, fsdp_count, (mate_ref,), (mlp_full,), depth, (mlp_send,), (mlp_recv,)
-    )
-    mate_copy = remote(
-        mlp_ref, mate_ref, mate_send, mate_recv, f, lax.rem(t + tp_count // 2, tp_count)
-    )
-    mate_copy.start()
+    mates = [
+        remote(
+            mlp_ref.at[i],
+            mate_ref.at[i],
+            mate_send.at[i],
+            mate_recv.at[i],
+            f,
+            lax.rem(t + tp_count // 2, tp_count),
+        )
+        for i in range(2)
+    ]
+    gathers = [
+        gather_copies(
+            f,
+            t,
+            fsdp_count,
+            (mate_ref.at[pl.ds(i, 1)],),
+            (mlp_full.at[pl.ds(i, 1)],),
+            depth,
+            (mlp_send.at[i],),
+            (mlp_recv.at[i],),
+        )
+        for i in range(2)
+    ]
     start_out()
+    mates[0].start()
+    mates[1].start()
     per_half = tp_count // 2
 
     def context_copy(toward):
@@ -553,20 +676,28 @@
             def _():
                 context_copy(index).start()
 
+            for turn in range(2):
+
+                @pl.when((step == 0) & (i == turn))
+                def _(turn=turn):
+                    mates[turn].wait()
+                    gathers[turn][0]()
+
+                @pl.when((step == 1) & (i == turn))
+                def _(turn=turn):
+                    gathers[turn][1]()
+
             return inner
 
         lax.fori_loop(0, per_half, block, 0)
 
         @pl.when(step == 0)
         def _():
-            mate_copy.wait()
-            start_mlp()
             relay_out()
 
         return carry
 
     lax.fori_loop(0, 2, half, 0)
-    relay_mlp()
 
     def settle(j, carry):
         toward = lax.rem(t + j, tp_count)
@@ -583,9 +714,10 @@
 
     lax.fori_loop(1, tp_count, settle, 0)
     finish_out()
-    finish_mlp()
     drain_out()
-    drain_mlp()
+    for _, _, finish_mlp, drain_mlp in gathers:
+        finish_mlp()
+        drain_mlp()
 
 
 def attend(fsdp_count, tp_count, lengths, query, pairs, mlp, out_weights, heads):
@@ -610,12 +742,12 @@
             pltpu.VMEM(mlp.shape, bf16),
             pltpu.VMEM((heads, CLIP, LANES), bf16),
             pltpu.VMEM((heads, LANES, CLIP), bf16),
-            dma,
-            dma,
+            dma((2,)),
+            dma((2,)),
             dma((tp_count,)),
             dma((tp_count,)),
-            dma((fsdp_count,)),
-            dma((fsdp_count,)),
+            dma((2, fsdp_count)),
+            dma((2, fsdp_count)),
             dma((fsdp_count,)),
             dma((fsdp_count,)),
         ],
@@ -1358,9 +1490,6 @@
     early,
     early_fsdp,
     early_tp,
-    late,
-    late_fsdp,
-    late_tp,
     row_send,
     row_recv,
     side_send,
@@ -1377,8 +1506,6 @@
     three_recv,
     early_send,
     early_recv,
-    late_send,
-    late_recv,
 ):
     f = lax.axis_index("fsdp")
     t = lax.axis_index("tp")
@@ -1392,6 +1519,8 @@
     early[0:4, :] = sums_ref[...]
     early[4:5, :] = jnp.zeros((1, features), f32)
     early[4:5, 0:proj_width] = proj_ref[...]
+    parts = jnp.concatenate([*three_parts(proj_ref[...]), jnp.zeros((5, proj_width), f32)], axis=0)
+    early[7:8, :] = column_sum(contract_cols(parts.astype(bf16), full_ref[0]))
     for level in range(2):
         for c in range(bias_ref.shape[1]):
             early[5 + level : 6 + level, c * units : (c + 1) * units] = bias_ref[level, c]
@@ -1412,9 +1541,6 @@
     start_early, middle_early, finish_early = reduce_copies(
         f, t, fsdp_count, tp_count, early, early_fsdp, early_tp, early_send, early_recv
     )
-    start_late, middle_late, finish_late = reduce_copies(
-        f, t, fsdp_count, tp_count, late, late_fsdp, late_tp, late_send, late_recv
-    )
     start_weights, add_weights, finish_weights = scatter_copies(
         f,
         t,
@@ -1485,13 +1611,12 @@
         return carry
 
     lax.fori_loop(0, tp_count, partial_rows, 0)
-    start_early()
     depth = weight_grad.shape[3]
     add_own()
     tall = 256
 
-    def weight_part(c, carry):
-        columns = pl.ds(pl.multiple_of(c * tall, tall), tall)
+    for c in range(features // tall):
+        columns = slice(c * tall, (c + 1) * tall)
         total = jnp.zeros((tall, proj_width), f32)
         for block in range(tp_count):
             total = total + contract_rows(
@@ -1499,9 +1624,10 @@
                 dproj_ref[block * rows : (block + 1) * rows, :],
             )
         weight_sum[columns, :] = total.astype(bf16)
-        return carry
-
-    lax.fori_loop(0, features // tall, weight_part, 0)
+        along = jnp.sum(total * full_ref[0, columns, :].astype(f32), axis=1, keepdims=True)
+        early[8:9, columns] = jnp.broadcast_to(along, (tall, LANES)).T[0:1, :]
+
+    start_early()
 
     def arrange(i, carry):
         weight_grad[0, i // 2, lax.rem(i, 2)] = weight_sum[
@@ -1514,9 +1640,9 @@
     outputs_ref[...] = partial_ref[...] + mixed_ref[...].astype(f32)
     unit, spread, _ = normalize(x_ref[...], row_of(gain_ref), row_of(shift_ref))
     add_weights()
+
+    lax.fori_loop(0, 2 * last, relay, 0)
     middle_early()
-
-    lax.fori_loop(0, 2 * last, relay, 0)
     finish_own((own_total, heads_sum))
     heads_out[...] = heads_sum[...].astype(bf16)
 
@@ -1551,13 +1677,28 @@
     finish_early()
     for row, total in enumerate((gain2_total, shift2_total, out_bias_total, last_bias_total)):
         total[...] = jnp.sum(early_tp[:, row, :], axis=0)
+    shift_sum = jnp.sum(early_tp[:, 7, :], axis=0, keepdims=True)
+    product = jnp.sum(early_tp[:, 8, :], axis=0, keepdims=True)
+    shift1_total[...] = shift_sum.reshape(-1)
+    gain1_total[...] = ((product - row_of(shift_ref) * shift_sum) / row_of(gain_ref)).reshape(-1)
+    heads = heads_grad.shape[4] // HD
+
+    def piece(head, at, high):
+        owner, index = (head // heads, head % heads)
+        tile, odd = (index, 1) if at == 0 else (heads + index // 2, index % 2)
+        row = early_tp[owner, 4:5, tile * LANES : (tile + 1) * LANES]
+        return row if odd == high else swapped(row)
+
+    for at, total in enumerate((value_bias_total, query_bias_total)):
+        row = jnp.concatenate(
+            [
+                joined(piece(2 * i, at, 0), piece(2 * i + 1, at, 1))
+                for i in range(tp_count * heads // 2)
+            ],
+            axis=1,
+        )
+        total[...] = row.reshape(-1)
     for j in range(tp_count):
-        tiles = [early_tp[j, 4:5, i * LANES : (i + 1) * LANES] for i in range(5)]
-        turned = [pltpu.roll(tile, HD, axis=1) for tile in tiles[:3]]
-        value_bias_total[j : j + 1, 0:LANES] = jnp.where(lane[0:1] < HD, turned[0], tiles[1])
-        value_bias_total[j : j + 1, LANES:] = turned[2][:, :HD]
-        query_bias_total[j : j + 1, 0:LANES] = tiles[3]
-        query_bias_total[j : j + 1, LANES:] = tiles[4][:, :HD]
         bias_total[j : j + 1, :] = (
             early_tp[j, 5:6, :] + early_tp[(j + tp_count // 2) % tp_count, 6:7, :]
         )
@@ -1573,11 +1714,7 @@
                 )
 
     dnorm = part_ref[t]
-    late[0:1, :] = column_sum(dnorm * unit)
-    late[1:2, :] = column_sum(dnorm)
-    start_late()
     inputs_grad[...] = gradient_ref[...] + norm_back(dnorm, unit, spread, row_of(gain_ref))
-    middle_late()
 
     for side, outer in enumerate((t < last, t > 0)):
 
@@ -1603,9 +1740,6 @@
         return carry
 
     lax.fori_loop(1, tp_count, heads_done, 0)
-    finish_late()
-    gain1_total[...] = jnp.sum(late_tp[:, 0, :], axis=0)
-    shift1_total[...] = jnp.sum(late_tp[:, 1, :], axis=0)
 
 
 def finish(
@@ -1648,8 +1782,7 @@
             jax.ShapeDtypeStruct((depth, features), f32),
             jax.ShapeDtypeStruct((depth, width), f32),
             *[jax.ShapeDtypeStruct((features,), f32)] * 6,
-            jax.ShapeDtypeStruct((tp_count, width), f32),
-            jax.ShapeDtypeStruct((tp_count, width), f32),
+            *[jax.ShapeDtypeStruct((tp_count * width,), f32)] * 2,
             jax.ShapeDtypeStruct((tp_count, features), f32),
         ),
         in_specs=whole_specs(15),
@@ -1671,12 +1804,9 @@
             pltpu.VMEM((2, 2 * tp_count, rows // 2, features), bf16),
             pltpu.VMEM((tp_count, depth, width), bf16),
             pltpu.VMEM((tp_count, depth, width), bf16),
-            pltpu.VMEM((7, features), f32),
-            pltpu.VMEM((fsdp_count, 7, features), f32),
-            pltpu.VMEM((tp_count, 7, features), f32),
-            pltpu.VMEM((2, features), f32),
-            pltpu.VMEM((fsdp_count, 2, features), f32),
-            pltpu.VMEM((tp_count, 2, features), f32),
+            pltpu.VMEM((9, features), f32),
+            pltpu.VMEM((fsdp_count, 9, features), f32),
+            pltpu.VMEM((tp_count, 9, features), f32),
             dma((2 * tp_count,)),
             dma((2, 2 * tp_count)),
             dma((tp_count,)),
@@ -1691,8 +1821,6 @@
             dma((count,)),
             dma((count,)),
             dma((count,)),
-            dma((peers,)),
-            dma((peers,)),
             dma((peers,)),
             dma((peers,)),
         ],
@@ -1719,12 +1847,21 @@
     )
 
 
-def pack_columns(key, value, query):
-    lead = key.shape[:-1]
-    heads = key.shape[-1] // HD
-    pairs = jnp.stack([key.reshape(*lead, heads, HD), value.reshape(*lead, heads, HD)], axis=-2)
-    spare = jnp.zeros((*lead, -key.shape[-1] % LANES), key.dtype)
-    return jnp.concatenate([pairs.reshape(*lead, -1), query, spare], axis=-1)
+def write_kernel(*refs):
+    count = len(refs) // 2
+    for source, target in zip(refs[:count], refs[count:]):
+        target[...] = source[...]
+
+
+def write_out(*values):
+    return pl.pallas_call(
+        write_kernel,
+        out_shape=tuple(jax.ShapeDtypeStruct(v.shape, v.dtype) for v in values),
+        in_specs=whole_specs(len(values)),
+        out_specs=tuple(whole_specs(len(values))),
+        compiler_params=pltpu.CompilerParams(vmem_limit_bytes=VMEM_LIMIT // 2),
+        name="write_out",
+    )(*values)
 
 
 def on_device(
@@ -1751,23 +1888,18 @@
     tp_count = lax.axis_size("tp")
     fsdp_count = lax.axis_size("fsdp")
     margin = CLIP - QB
-    local_width = query_weight.shape[1]
-    heads_here = local_width // HD
+    heads_here = query_weight.shape[1] // HD
     unit_count = fc1_weight.shape[0]
-    by_tp = lambda bias: bias.reshape(tp_count, 1, local_width)
-    pair_width = 2 * local_width
-    mlp_own = jnp.stack([fc1_weight, fc2_weight])
-    query, pairs, normed, attention_w, mlp_w, out_parts = project(
+    query, pairs, normed, attention_w, mlp_w, out_parts, mlp_own = project(
         fsdp_count,
         tp_count,
         inputs,
         norm1_gain,
         norm1_shift,
-        pack_columns(key_weight, value_weight, query_weight)[None],
-        pack_columns(jnp.zeros((tp_count, 1, local_width), f32), by_tp(value_bias), by_tp(query_bias)),
-        mlp_own,
+        (key_weight, value_weight, query_weight),
+        (value_bias, query_bias),
+        (fc1_weight, fc2_weight),
         out_weight,
-        pair_width,
         margin,
     )
     spread, context, wide, mlp_other, out_full = attend(
@@ -1846,10 +1978,8 @@
         bias_part,
         proj_sums,
     )
-    grad_qbias = grad_qbias.reshape(-1)
-    grad_vbias = grad_vbias.reshape(-1)
     grad_b1 = jnp.swapaxes(bias_total.reshape(tp_count, fsdp_count, unit_count), 0, 1).reshape(-1)
-    return (
+    return write_out(
         outputs,
         inputs_grad,
         grad_gain1,

time: 222 us -> 201 us (0.905)
  local copies, waits for them, and re-layouts: 21.4 us -> 10.6 us
  Pallas kernels: 197 us -> 189 us
    unnamed x40, local copies, waits for them, and re-layouts: 16.5 us -> 9.58 us
    pallas_call x1, Pallas kernels: 40 us -> 33.9 us  [attend(): pl.pallas_call(functools.partial(attend_kernel, fsdp_count, tp_count), ou...]
    pallas_call x1, Pallas kernels: 50.7 us -> 45.5 us  [finish(): pl.pallas_call(functools.partial(finish_kernel, fsdp_count, tp_count), ou...]
    reshape x5 -> x0, local copies, waits for them, and re-layouts: 2.3 us -> none  [the longest x1 0.76 us: on_device(): by_tp = lambda bias: bias.reshape(tp_count, 1, local_width)]
where the time goes in v7:
time: 201 us
  Pallas kernels  189 us (94%)
  local copies, waits for them, and re-layouts  10.6 us (5%)
    pallas_call x1, Pallas kernels, finish(): pl.pallas_call(functools.partial(finish_kernel, fsdp_count, tp_count), ou...  45.5 us
    pallas_call x1, Pallas kernels, project(): pl.pallas_call(functools.partial(project_kernel, fsdp_count, tp_count), o...  42.8 us
    pallas_call x1, Pallas kernels, attend_back(): pl.pallas_call(functools.partial(attend_back_kernel, fsdp_count, tp_count...  37.7 us
    pallas_call x1, Pallas kernels, attend(): pl.pallas_call(functools.partial(attend_kernel, fsdp_count, tp_count), ou...  33.9 us
    pallas_call x1, Pallas kernels, by_rows(): pl.pallas_call(functools.partial(rows_kernel, fsdp_count, tp_count), out_...  27.8 us
    unnamed x40, local copies, waits for them, and re-layouts  9.58 us

profile of v7, /device:TPU:0, one launch (start us, length us, event | category | flops | bytes accessed | tf_op | source)
XLA Modules:
  0.0 200.9 jit_solution(12170804561189544883)
XLA Ops:
  0.7 0.8 reshape.55
  1.4 0.0 copy-start.15
  1.5 0.0 copy-start.16
  1.5 0.0 copy-start.17
  1.5 0.0 copy-start.18
  1.5 0.1 reshape.56.bias_ref
  1.6 0.0 copy-start
  1.6 1.1 copy-done
  2.7 0.0 copy-start.3
  2.7 0.9 copy-done.3
  3.6 0.0 copy-start.4
  3.6 0.9 copy-done.4
  4.5 0.0 copy-start.5
  4.5 0.8 copy-done.5
  5.3 0.0 copy-start.6
  5.3 0.8 copy-done.6
  6.1 0.0 copy-start.7
  6.1 0.8 copy-done.7
  6.9 0.0 copy-start.8
  6.9 0.8 copy-done.8
  7.7 0.0 copy-start.9
  7.7 0.7 copy-done.9
  8.4 0.0 copy-start.11
  8.4 0.7 copy-done.11
  9.1 0.0 copy-start.13
  9.1 0.7 copy-done.13
  9.8 0.0 copy-start.14
  9.8 0.7 copy-done.14
  10.5 0.0 copy-start.1
  10.5 0.0 copy-start.2
  10.5 42.8 %project.1 = (bf16[1024,256]{1,0:T(8,128)(2,1)S(1)}, bf16[3072,384]{1,0:T(8,128)(2,1)S(1)}, bf16[4,256,768]{2,1,0:T(8,128)(2,1)S(1)}, bf16[1,768,640]{2,1,0:T(8,...) custom-call(f32[256,768]{1,0:T(8,128)S(1)} %copy-done, ...), custom_call_target="tpu_custom_call" | custom-call | tf_op jit(solution)/shard_map/project/pallas_call | solution.py:473
  53.3 0.0 copy-start.19
  53.3 0.6 copy-done.19
  53.9 33.9 %attend.1 = (bf16[4,256,192]{2,1,0:T(8,128)(2,1)S(1)}, bf16[1024,192]{1,0:T(8,128)(2,1)S(1)}, bf16[3,1024,128]{2,1,0:T(8,128)(2,1)S(1)}, bf16[2,768,768]{2,1,0:T(8,128)(2,1)S(1)}, bf16[4,768,192]{2,1,0:T(8,128)(2,1)S(1)}) custom-call(s32[6]{0:T(128)S(1)} %copy-done.19, bf16[1024,256]{1,0:T(8,128)(2,1)S(1)} %get-tuple-element.59.query_ref, ...), custom_call_target="tpu_custom_call" | custom-call | tf_op jit(solution)/shard_map/attend/pallas_call | solution.py:730
  87.8 0.0 copy-done.15
  87.8 0.0 copy-done.16
  87.8 0.0 copy-done.17
  87.9 0.0 copy-done.18
  87.9 0.0 copy-done.1
  87.9 0.0 copy-done.2
  87.9 27.8 %by_rows.1 = (f32[256,768]{1,0:T(8,128)S(1)}, f32[256,768]{1,0:T(8,128)S(1)}, bf16[256,768]{1,0:T(8,128)(2,1)S(1)}, bf16[4,256,192]{2,1,0:T(8,128)(2,1)S(1)}, bf...) custom-call(f32[256,768]{1,0:T(8,128)S(1)} %copy-done.1, ...), custom_call_target="tpu_custom_call" | custom-call | tf_op jit(solution)/shard_map/by_rows/pallas_call | solution.py:927
  115.7 0.0 copy-start.10
  115.7 0.0 copy-start.12
  115.7 37.7 %attend_back.1 = (bf16[1024,640]{1,0:T(8,128)(2,1)S(1)}, bf16[2,96,768]{2,1,0:T(8,128)(2,1)S(1)}, bf16[256,768]{1,0:T(8,128)(2,1)S(1)}, f32[1,640]{1,0:T(1,128)S(1)}) custom-call(s32[6]{0:T(128)S(1)} %copy-done.19, bf16[4,256,192]{2,1,0:T(8,128)(2,1)S(1)} %get-tuple-element.67.dspread_ref, bf16[3,1024,128]{2,1,0:T(8,128)(2,1)S(1)} %get-tuple-element.68.wide_ref, ...), custom_call_target="tpu_custom_call" | custom-call | tf_op jit(solution)/shard_map/attend_back/pallas_call | solution.py:1330
  153.4 0.0 copy-done.10
  153.5 0.0 copy-done.12
  153.5 45.5 %finish.1 = (f32[256,768]{1,0:T(8,128)S(1)}, f32[256,768]{1,0:T(8,128)S(1)}, f32[96,192]{1,0:T(8,128)S(1)}, f32[96,192]{1,0:T(8,128)S(1)}, f32[96,192]{1,0:T(8,1...) custom-call(f32[256,768]{1,0:T(8,128)S(1)} %copy-done.1, ...), custom_call_target="tpu_custom_call" | custom-call | tf_op jit(solution)/shard_map/finish/pallas_call | solution.py:1773
  198.9 0.1 reshape.60
  199.0 0.1 reshape.61.refs_14_
  199.1 1.6 write_out.1
  (2 shorter events, 0.0 us)
Async XLA Ops:
  1.4 86.4 %copy-start.15 = (f32[768]{0:T(1024)S(1)}, f32[768]{0:T(1024)}, u32[]{:S(2)}) copy-start(f32[768]{0:T(1024)} %out_bias_ref.1) | copy-start | bytes 9220
  1.5 86.4 %copy-start.16 = (f32[768]{0:T(1024)S(1)}, f32[768]{0:T(1024)}, u32[]{:S(2)}) copy-start(f32[768]{0:T(1024)} %gain_ref.2) | copy-start | bytes 9220
  1.5 86.4 %copy-start.17 = (f32[768]{0:T(1024)S(1)}, f32[768]{0:T(1024)}, u32[]{:S(2)}) copy-start(f32[768]{0:T(1024)} %shift_ref.2) | copy-start | bytes 9220
  1.5 86.4 %copy-start.18 = (f32[768]{0:T(1024)S(1)}, f32[768]{0:T(1024)}, u32[]{:S(2)}) copy-start(f32[768]{0:T(1024)} %last_bias_ref.1) | copy-start | bytes 9220
  1.6 1.1 copy-start
  2.7 0.9 copy-start.3
  3.6 0.9 copy-start.4
  4.5 0.8 copy-start.5
  5.3 0.8 copy-start.6
  6.1 0.8 copy-start.7
  6.9 0.8 copy-start.8
  7.7 0.7 copy-start.9
  8.4 0.7 copy-start.11
  9.1 0.7 copy-start.13
  9.8 0.7 copy-start.14
  10.5 77.4 %copy-start.1 = (f32[256,768]{1,0:T(8,128)S(1)}, f32[256,768]{1,0:T(8,128)}, u32[]{:S(2)}) copy-start(f32[256,768]{1,0:T(8,128)} %x_ref.3) | copy-start | bytes 2359300
  10.5 77.4 %copy-start.2 = (f32[1024,768]{1,0:T(8,128)S(1)}, f32[1024,768]{1,0:T(8,128)}, u32[]{:S(2)}) copy-start(f32[1024,768]{1,0:T(8,128)} %cotangent_ref.1) | copy-start | bytes 9437188
  53.3 0.7 copy-start.19
  115.7 37.8 %copy-start.10 = (f32[768]{0:T(1024)S(1)}, f32[768]{0:T(1024)}, u32[]{:S(2)}) copy-start(f32[768]{0:T(1024)} %gain_ref.3) | copy-start | bytes 9220
  115.7 37.8 %copy-start.12 = (f32[768]{0:T(1024)S(1)}, f32[768]{0:T(1024)}, u32[]{:S(2)}) copy-start(f32[768]{0:T(1024)} %shift_ref.3) | copy-start | bytes 9220

commit v8 on v7

--- a/solution.py
+++ b/solution.py
@@ -206,24 +206,6 @@
 def project_kernel(
     fsdp_count,
     tp_count,
-    x_hbm,
-    gain_hbm,
-    shift_hbm,
-    key_hbm,
-    value_hbm,
-    query_hbm,
-    value_bias_hbm,
-    query_bias_hbm,
-    up_hbm,
-    down_hbm,
-    out_hbm,
-    query_ref,
-    pair_ref,
-    normed_ref,
-    full_ref,
-    mlp_full,
-    heads_ref,
-    mlp_ref,
     x_ref,
     gain_ref,
     shift_ref,
@@ -232,10 +214,18 @@
     query_weight,
     value_bias,
     query_bias,
+    up_ref,
+    down_ref,
     out_ref,
+    query_ref,
+    pair_ref,
+    normed_ref,
+    full_ref,
+    mlp_full,
+    heads_ref,
+    mlp_ref,
     weight_ref,
     bias_ref,
-    load_sem,
     side_send,
     side_recv,
     weight_send,
@@ -259,26 +249,6 @@
     above = f + 1 < fsdp_count
     below = f > 0
     blank = jnp.zeros((256, pair_width), jnp.bfloat16)
-    loads = [
-        pltpu.make_async_copy(source, target, load_sem.at[i])
-        for i, (source, target) in enumerate(
-            (
-                (key_hbm, key_weight),
-                (value_hbm, value_weight),
-                (query_hbm, query_weight),
-                (x_hbm, x_ref),
-                (gain_hbm, gain_ref),
-                (shift_hbm, shift_ref),
-                (value_bias_hbm, value_bias),
-                (query_bias_hbm, query_bias),
-                (out_hbm, out_ref),
-                (up_hbm, mlp_ref.at[0]),
-                (down_hbm, mlp_ref.at[1]),
-            )
-        )
-    ]
-    for load in loads:
-        load.start()
 
     def clear(i, carry):
         pair_ref[pl.ds(i * 256, 256), :] = blank
@@ -286,9 +256,9 @@
         return carry
 
     lax.fori_loop(0, margin // 256, clear, 0)
-    for load in loads:
-        load.wait()
     pack_weights(key_weight, value_weight, query_weight, weight_ref)
+    mlp_ref[0] = up_ref[...]
+    mlp_ref[1] = down_ref[...]
     greet(fsdp_count, tp_count, f, t)
     bias_ref[...] = pack_bias(t, tp_count, row_of(value_bias), row_of(query_bias))
     start_weights, relay_weights, finish_weights, drain_weights = gather_copies(
@@ -481,16 +451,11 @@
             jax.ShapeDtypeStruct((tp_count, *out_weight.shape), bf16),
             jax.ShapeDtypeStruct((2, depth, features), bf16),
         ),
-        in_specs=[pl.BlockSpec(memory_space=pltpu.MemorySpace.HBM)] * 11,
+        in_specs=whole_specs(11),
         out_specs=tuple(whole_specs(7)),
         scratch_shapes=[
-            *[
-                pltpu.VMEM(v.shape, v.dtype)
-                for v in (x, gain, shift, *weights, *biases, out_weight)
-            ],
             pltpu.VMEM((1, depth, packed_width), bf16),
             pltpu.VMEM((1, packed_width), jnp.float32),
-            dma((11,)),
             dma((tp_count,)),
             dma((tp_count,)),
             dma((fsdp_count,)),
@@ -827,8 +792,14 @@
     unit, spread, normed = normalize(hidden, row_of(gain_ref), row_of(shift_ref))
     unit_ref[...] = unit
     normed_ref[side] = normed.astype(bf16)
-    row_copy = remote(normed_ref.at[side], normed_ref.at[side], row_send, row_recv, f, peer)
-    row_copy.start()
+    sub = rows // 2
+
+    def row_copy(low):
+        piece = normed_ref.at[side, pl.ds(pl.multiple_of(low * sub, sub), sub)]
+        return remote(piece, piece, row_send.at[low], row_recv.at[low], f, peer)
+
+    row_copy(0).start()
+    row_copy(1).start()
     load.wait()
 
     def rounding(i, carry):
@@ -841,15 +812,22 @@
     chunks = own_ref.shape[1] // tile
     mate = lax.rem(t + tp_count // 2, tp_count)
 
+    def norm_copy(low):
+        return remote(
+            norm_out.at[low], norm_in.at[low], norm_send.at[low], norm_recv.at[low], f, peer
+        )
+
     def feed_forward(turn, carry):
-        which = lax.rem(side + turn, 2)
-
-        @pl.when(turn == 1)
+        which = lax.rem(side + turn // 2, 2)
+        low = lax.rem(turn, 2)
+
+        @pl.when(turn >= 2)
         def _():
-            row_copy.wait_recv()
-
-        here = pl.ds(pl.multiple_of(which * rows, rows), rows)
-        normed_rows = normed_ref[which]
+            row_copy(low).wait_recv()
+
+        within = pl.ds(pl.multiple_of(low * sub, sub), sub)
+        here = pl.ds(pl.multiple_of(which * rows + low * sub, sub), sub)
+        normed_rows = normed_ref[which, within, :]
         upstream_rows = rounded[here, :]
 
         for level, (weights, owner) in enumerate(((own_ref, t), (mate_ref, mate))):
@@ -873,17 +851,20 @@
                 dpreact = (dactive * slope).astype(bf16)
                 active_ref[level, c, here, :] = active
                 slope_ref[level, c, here, :] = dpreact
-                norm_sum[which] += jnp.dot(dpreact, up, preferred_element_type=f32)
-                mixed_sum[which] += jnp.dot(active, down, preferred_element_type=f32)
+                norm_sum[which, within, :] += jnp.dot(dpreact, up, preferred_element_type=f32)
+                mixed_sum[which, within, :] += jnp.dot(active, down, preferred_element_type=f32)
                 return inner
 
             lax.fori_loop(0, chunks, chunk, 0)
+
+        @pl.when(turn >= 2)
+        def _():
+            norm_out[low] = norm_sum[1 - side, within, :].astype(bf16)
+            norm_copy(low).start()
+
         return carry
 
-    lax.fori_loop(0, 2, feed_forward, 0)
-    norm_out[...] = norm_sum[1 - side].astype(bf16)
-    norm_copy = remote(norm_out, norm_in, norm_send, norm_recv, f, peer)
-    norm_copy.start()
+    lax.fori_loop(0, 4, feed_forward, 0)
     mixed_ref[...] = mixed_sum[1 - side].astype(bf16)
     outputs_ref[...] = hidden_ref[...] + mixed_sum[side] + row_of(last_bias_ref)
 
@@ -900,8 +881,9 @@
 
         lax.fori_loop(0, chunks, weight_grads, 0)
 
-    norm_copy.wait()
-    dnorm = norm_sum[side] + norm_in[...].astype(f32)
+    norm_copy(0).wait()
+    norm_copy(1).wait()
+    dnorm = norm_sum[side] + jnp.concatenate([norm_in[0], norm_in[1]], axis=0).astype(f32)
     unit = unit_ref[...]
     cotangent = upstream[pl.ds(pl.multiple_of(side * rows, rows), rows), :]
     gradient = cotangent + norm_back(dnorm, unit, spread, row_of(gain_ref))
@@ -914,7 +896,8 @@
     for j in range(tp_count):
         context_ref[j] = jnp.dot(gradient, heads_ref[j], preferred_element_type=f32).astype(bf16)
         heads_grad[j] = contract_rows(gradient, spread_ref[j]).astype(bf16)
-    row_copy.wait_send()
+    row_copy(0).wait_send()
+    row_copy(1).wait_send()
 
 
 def by_rows(fsdp_count, tp_count, x, spread, heads, vectors, bias, own, mate, cotangent):
@@ -949,13 +932,13 @@
             pltpu.VMEM((2, chunks, 2 * rows, 256), bf16),
             pltpu.VMEM((2, rows, features), f32),
             pltpu.VMEM((2, rows, features), f32),
-            pltpu.VMEM((rows, features), bf16),
-            pltpu.VMEM((rows, features), bf16),
+            pltpu.VMEM((2, rows // 2, features), bf16),
+            pltpu.VMEM((2, rows // 2, features), bf16),
             dma,
-            dma,
-            dma,
-            dma,
-            dma,
+            dma((2,)),
+            dma((2,)),
+            dma((2,)),
+            dma((2,)),
         ],
         compiler_params=pltpu.CompilerParams(
             collective_id=4, has_side_effects=True, vmem_limit_bytes=VMEM_LIMIT
@@ -1612,7 +1595,6 @@
 
     lax.fori_loop(0, tp_count, partial_rows, 0)
     depth = weight_grad.shape[3]
-    add_own()
     tall = 256
 
     for c in range(features // tall):
@@ -1628,6 +1610,7 @@
         early[8:9, columns] = jnp.broadcast_to(along, (tall, LANES)).T[0:1, :]
 
     start_early()
+    add_own()
 
     def arrange(i, carry):
         weight_grad[0, i // 2, lax.rem(i, 2)] = weight_sum[

time: 201 us -> 199 us (0.990)
  no operation moved by 1% of the time
where the time goes in v8:
time: 199 us; the launch traced here: 198 us
  Pallas kernels  187 us (94%)
  local copies, waits for them, and re-layouts  10.6 us (5%)
    pallas_call x1, Pallas kernels, finish(): pl.pallas_call(functools.partial(finish_kernel, fsdp_count, tp_count), ou...  45.6 us
    pallas_call x1, Pallas kernels, project(): pl.pallas_call(functools.partial(project_kernel, fsdp_count, tp_count), o...  41.9 us
    pallas_call x1, Pallas kernels, attend_back(): pl.pallas_call(functools.partial(attend_back_kernel, fsdp_count, tp_count...  37.7 us
    pallas_call x1, Pallas kernels, attend(): pl.pallas_call(functools.partial(attend_kernel, fsdp_count, tp_count), ou...  33.9 us
    pallas_call x1, Pallas kernels, by_rows(): pl.pallas_call(functools.partial(rows_kernel, fsdp_count, tp_count), out_...  25.9 us
    unnamed x40, local copies, waits for them, and re-layouts  9.58 us

profile of v8, /device:TPU:0, one launch (start us, length us, event | category | flops | bytes accessed | tf_op | source)
XLA Modules:
  0.0 198.2 jit_solution(1422304264424808896)
XLA Ops:
  0.7 0.8 reshape.55
  1.4 0.0 copy-start.15
  1.5 0.0 copy-start.16
  1.5 0.0 copy-start.17
  1.5 0.0 copy-start.18
  1.5 0.1 reshape.56.bias_ref
  1.6 0.0 copy-start
  1.6 1.1 copy-done
  2.7 0.0 copy-start.3
  2.7 0.9 copy-done.3
  3.6 0.0 copy-start.4
  3.6 0.9 copy-done.4
  4.5 0.0 copy-start.5
  4.5 0.8 copy-done.5
  5.3 0.0 copy-start.6
  5.3 0.8 copy-done.6
  6.1 0.0 copy-start.7
  6.1 0.8 copy-done.7
  6.9 0.0 copy-start.8
  6.9 0.8 copy-done.8
  7.7 0.0 copy-start.9
  7.7 0.7 copy-done.9
  8.4 0.0 copy-start.11
  8.4 0.7 copy-done.11
  9.1 0.0 copy-start.13
  9.1 0.7 copy-done.13
  9.8 0.0 copy-start.14
  9.8 0.7 copy-done.14
  10.5 0.0 copy-start.1
  10.5 0.0 copy-start.2
  10.5 41.9 %project.1 = (bf16[1024,256]{1,0:T(8,128)(2,1)S(1)}, bf16[3072,384]{1,0:T(8,128)(2,1)S(1)}, bf16[4,256,768]{2,1,0:T(8,128)(2,1)S(1)}, bf16[1,768,640]{2,1,0:T(8,...) custom-call(f32[256,768]{1,0:T(8,128)S(1)} %copy-done, ...), custom_call_target="tpu_custom_call" | custom-call | tf_op jit(solution)/shard_map/project/pallas_call | solution.py:443
  52.4 0.0 copy-start.19
  52.5 0.6 copy-done.19
  53.1 33.9 %attend.1 = (bf16[4,256,192]{2,1,0:T(8,128)(2,1)S(1)}, bf16[1024,192]{1,0:T(8,128)(2,1)S(1)}, bf16[3,1024,128]{2,1,0:T(8,128)(2,1)S(1)}, bf16[2,768,768]{2,1,0:T(8,128)(2,1)S(1)}, bf16[4,768,192]{2,1,0:T(8,128)(2,1)S(1)}) custom-call(s32[6]{0:T(128)S(1)} %copy-done.19, bf16[1024,256]{1,0:T(8,128)(2,1)S(1)} %get-tuple-element.59.query_ref, ...), custom_call_target="tpu_custom_call" | custom-call | tf_op jit(solution)/shard_map/attend/pallas_call | solution.py:695
  87.0 0.0 copy-done.15
  87.0 0.0 copy-done.16
  87.0 0.0 copy-done.17
  87.0 0.0 copy-done.18
  87.0 0.0 copy-done.1
  87.1 0.0 copy-done.2
  87.1 25.9 %by_rows.1 = (f32[256,768]{1,0:T(8,128)S(1)}, f32[256,768]{1,0:T(8,128)S(1)}, bf16[256,768]{1,0:T(8,128)(2,1)S(1)}, bf16[4,256,192]{2,1,0:T(8,128)(2,1)S(1)}, bf...) custom-call(f32[256,768]{1,0:T(8,128)S(1)} %copy-done.1, ...), custom_call_target="tpu_custom_call" | custom-call | tf_op jit(solution)/shard_map/by_rows/pallas_call | solution.py:910
  112.9 0.0 copy-start.10
  112.9 0.0 copy-start.12
  113.0 37.7 %attend_back.1 = (bf16[1024,640]{1,0:T(8,128)(2,1)S(1)}, bf16[2,96,768]{2,1,0:T(8,128)(2,1)S(1)}, bf16[256,768]{1,0:T(8,128)(2,1)S(1)}, f32[1,640]{1,0:T(1,128)S(1)}) custom-call(s32[6]{0:T(128)S(1)} %copy-done.19, bf16[4,256,192]{2,1,0:T(8,128)(2,1)S(1)} %get-tuple-element.67.dspread_ref, bf16[3,1024,128]{2,1,0:T(8,128)(2,1)S(1)} %get-tuple-element.68.wide_ref, ...), custom_call_target="tpu_custom_call" | custom-call | tf_op jit(solution)/shard_map/attend_back/pallas_call | solution.py:1313
  150.7 0.0 copy-done.10
  150.7 0.0 copy-done.12
  150.7 45.6 %finish.1 = (f32[256,768]{1,0:T(8,128)S(1)}, f32[256,768]{1,0:T(8,128)S(1)}, f32[96,192]{1,0:T(8,128)S(1)}, f32[96,192]{1,0:T(8,128)S(1)}, f32[96,192]{1,0:T(8,1...) custom-call(f32[256,768]{1,0:T(8,128)S(1)} %copy-done.1, ...), custom_call_target="tpu_custom_call" | custom-call | tf_op jit(solution)/shard_map/finish/pallas_call | solution.py:1756
  196.3 0.1 reshape.60
  196.4 0.1 reshape.61.refs_14_
  196.4 1.6 write_out.1
  (2 shorter events, 0.0 us)
Async XLA Ops:
  1.4 85.6 %copy-start.15 = (f32[768]{0:T(1024)S(1)}, f32[768]{0:T(1024)}, u32[]{:S(2)}) copy-start(f32[768]{0:T(1024)} %out_bias_ref.1) | copy-start | bytes 9220
  1.5 85.6 %copy-start.16 = (f32[768]{0:T(1024)S(1)}, f32[768]{0:T(1024)}, u32[]{:S(2)}) copy-start(f32[768]{0:T(1024)} %gain_ref.4) | copy-start | bytes 9220
  1.5 85.6 %copy-start.17 = (f32[768]{0:T(1024)S(1)}, f32[768]{0:T(1024)}, u32[]{:S(2)}) copy-start(f32[768]{0:T(1024)} %shift_ref.4) | copy-start | bytes 9220
  1.5 85.6 %copy-start.18 = (f32[768]{0:T(1024)S(1)}, f32[768]{0:T(1024)}, u32[]{:S(2)}) copy-start(f32[768]{0:T(1024)} %last_bias_ref.1) | copy-start | bytes 9220
  1.6 1.1 copy-start
  2.7 0.9 copy-start.3
  3.6 0.9 copy-start.4
  4.5 0.8 copy-start.5
  5.3 0.8 copy-start.6
  6.1 0.8 copy-start.7
  6.9 0.8 copy-start.8
  7.7 0.7 copy-start.9
  8.4 0.7 copy-start.11
  9.1 0.7 copy-start.13
  9.8 0.7 copy-start.14
  10.5 76.6 %copy-start.1 = (f32[256,768]{1,0:T(8,128)S(1)}, f32[256,768]{1,0:T(8,128)}, u32[]{:S(2)}) copy-start(f32[256,768]{1,0:T(8,128)} %x_ref.5) | copy-start | bytes 2359300
  10.5 76.6 %copy-start.2 = (f32[1024,768]{1,0:T(8,128)S(1)}, f32[1024,768]{1,0:T(8,128)}, u32[]{:S(2)}) copy-start(f32[1024,768]{1,0:T(8,128)} %cotangent_ref.1) | copy-start | bytes 9437188
  52.4 0.7 copy-start.19
  112.9 37.8 %copy-start.10 = (f32[768]{0:T(1024)S(1)}, f32[768]{0:T(1024)}, u32[]{:S(2)}) copy-start(f32[768]{0:T(1024)} %gain_ref.5) | copy-start | bytes 9220
  112.9 37.8 %copy-start.12 = (f32[768]{0:T(1024)S(1)}, f32[768]{0:T(1024)}, u32[]{:S(2)}) copy-start(f32[768]{0:T(1024)} %shift_ref.5) | copy-start | bytes 9220
